TPU v7x, 256 devices: a whole 4x4x8 slice. The times are simulated.
256 devices in a mesh: seq: 32 (over z, y_lo, core), head: 8 (over y_hi, x).
Axes of the slice: x: 4, y: 4 (y_hi: 2, y_lo: 2; y = y_hi * 2 + y_lo), z: 8, core: 2. Of those that a mesh axis runs over, the one named last changes fastest.
Arguments:
- tokens: bfloat16 [16384, 1024], P('seq'), may hold values from -24 to 24
- norm_attn: float32 [1024], replicated, may hold values from 0.5 to 1.5
- self_qkv: bfloat16 [3, 1024, 1024], P(None, None, 'head'), may hold values from -4 to 4
- self_out: bfloat16 [1024, 1024], P('head'), may hold values from -0.1875 to 0.1875
- norm_ffn: float32 [1024], replicated, may hold values from 0.5 to 1.5
- ffn_in: bfloat16 [2, 1024, 2816], P(None, None, 'head'), may hold values from -0.1875 to 0.1875
- ffn_out: bfloat16 [2816, 1024], P('head'), may hold values from -0.109375 to 0.109375
- norm_final: float32 [1024], replicated, may hold values from 0.5 to 1.5
- pad_lengths: int32 [32], replicated, may hold values from 64 to 512
- targets: bfloat16 [512, 1024], replicated, may hold values from -8 to 8
- target_lengths: int32 [4], replicated, may hold values from 32 to 128
- norm_cross: float32 [1024], replicated, may hold values from 0.1 to 1.9
- cross_query: bfloat16 [1024, 1024], P(None, 'head'), may hold values from -4 to 4
- cross_kv: bfloat16 [2, 1024, 1024], P(None, None, 'head'), may hold values from -4 to 4
- cross_out: bfloat16 [1024, 1024], P('head'), may hold values from -4 to 4
Outputs:
- encoded: bfloat16 [16384, 1024], P('seq')
- decoded: bfloat16 [512, 1024], replicated
All inputs are finite; a program needn't handle non-finite values.
Results may differ from a plain program's by a relative error of at most 0.033.
Values may be sent and summed in bfloat16 or wider, within the bound.
A program may use at most 128 MiB of HBM per device.

v0:
```python
import math

import jax
import jax.numpy as jnp
from jax import lax
from jax.sharding import Mesh
from jax.sharding import PartitionSpec as P

D = 1024
HD = 64
TOK_DEV = 512
TGT_LEN = 128
SEQ = ("seq_0", "seq_1", "seq_2")


epsilon = 1e-06
masked_score = -1e30


def in_one_piece(arrays, axis, dim, along):
    widths = [a.shape[along] for a in arrays]
    both = jnp.concatenate(arrays, axis=along)
    whole = lax.all_gather(both, axis, axis=dim, tiled=True)
    return tuple(jnp.split(whole, [sum(widths[:k]) for k in range(1, len(widths))], axis=along))


def cut_along(x, dim, count):
    before, after = (x.shape[:dim], x.shape[dim + 1 :])
    return jnp.moveaxis(x.reshape(*before, count, -1, *after), dim, 0)


def sent_and_summed(x, axis, dim):
    blocks = cut_along(x, dim, lax.axis_size(axis))
    arrived = lax.all_to_all(blocks, axis, split_axis=0, concat_axis=0, tiled=True)
    return arrived.astype(jnp.float32).sum(axis=0)


def sent_to_all(x, axis):
    copies = jnp.broadcast_to(x, (lax.axis_size(axis), *x.shape))
    return lax.all_to_all(copies, axis, split_axis=0, concat_axis=0, tiled=True)


def over_copies(x, axis):
    everything = sent_to_all(x, axis)
    return jnp.sum(everything, axis=0)


def laid_out(blocks, dim):
    shape = list(blocks.shape[1:])
    shape[dim] *= blocks.shape[0]
    return jnp.moveaxis(blocks, 0, dim).reshape(shape)


def gather_directly(x, axis, dim):
    blocks = sent_to_all(x, axis)
    return laid_out(blocks, dim)


def all_in_one(x, axis):
    leaves = jax.tree.leaves(x)
    order = sorted(range(len(leaves)), key=lambda k: -leaves[k].size)
    width = (1, *leaves[order[0]].shape)[-1]
    lines = [
        jnp.pad(leaves[k].reshape(-1), (0, -leaves[k].size % width)).reshape(-1, width)
        for k in order
    ]
    both, at, found = (lax.all_gather(jnp.concatenate(lines), axis), 0, {})
    for k, line in zip(order, lines):
        share = both[:, at : at + len(line)].reshape(len(both), -1)
        found[k] = share[:, : leaves[k].size].reshape(-1, *leaves[k].shape)
        at += len(line)
    numbers = iter(range(len(leaves)))
    return jax.tree.map(lambda _: found[next(numbers)], x)


def merged_by_axis(x, axes, combine):
    for axis in axes:
        pieces = all_in_one(x, axis)
        x = jax.tree.map(lambda part: part[0], pieces)
        for k in range(1, lax.axis_size(axis)):
            x = combine(x, jax.tree.map(lambda part: part[k], pieces))
    return x


def over_copies_2(x, axis):
    everything = sent_to_all(x, axis)
    return jnp.sum(everything.astype(jnp.float32), axis=0)


def rms_norm(values, gain_vector):
    widened = values.astype(jnp.float32)
    return (
        widened
        * lax.rsqrt(jnp.mean(widened * widened, axis=-1, keepdims=True) + epsilon)
        * gain_vector
    )


def spread_heads(per_head):
    return jnp.repeat(per_head.T, HD, axis=1)


def live_within(positions, lengths, span):
    block_ids = jnp.arange(lengths.shape[0], dtype=jnp.int32)
    owners = positions // span
    lengths_here = jnp.sum(
        jnp.where(owners[:, None] == block_ids[None, :], lengths[None, :], 0), axis=1
    )
    return positions % span < lengths_here


def live_keys(positions, pad_lengths):
    return live_within(positions, pad_lengths, TOK_DEV)


def flash_block(flash_state, query_heads, key_rows, value_rows, live_rows, scaling):
    running_max, running_sum, running_acc = flash_state
    key_count = key_rows.shape[0]
    heads_here = query_heads.shape[1]
    keys_split = key_rows.reshape(key_count, heads_here, HD)
    values_split = value_rows.reshape(key_count, heads_here, HD)
    scores = (
        jnp.einsum("qhd,khd->hqk", query_heads, keys_split, preferred_element_type=jnp.float32)
        * scaling
    )
    scores = jnp.where(live_rows[None, None, :], scores, masked_score)
    new_max = jnp.maximum(running_max, jnp.max(scores, axis=-1))
    shrink = jnp.exp(running_max - new_max)
    weights = jnp.where(live_rows[None, None, :], jnp.exp(scores - new_max[:, :, None]), 0.0)
    new_sum = running_sum * shrink + jnp.sum(weights, axis=-1)
    mixed_values = jnp.einsum(
        "hqk,khd->qhd",
        weights.astype(jnp.bfloat16),
        values_split,
        preferred_element_type=jnp.float32,
    )
    new_acc = running_acc * spread_heads(shrink) + mixed_values.reshape(
        mixed_values.shape[0], heads_here * HD
    )
    return (new_max, new_sum, new_acc)


def feed_forward(normed_in, ffn_in, ffn_out):
    gate_proj = jnp.dot(normed_in, ffn_in[0], preferred_element_type=jnp.float32)
    up_proj = jnp.dot(normed_in, ffn_in[1], preferred_element_type=jnp.float32)
    activated = (jax.nn.gelu(gate_proj, approximate=True) * up_proj).astype(jnp.bfloat16)
    return jnp.dot(activated, ffn_out, preferred_element_type=jnp.float32)


def combine_parts(first_part, second_part):
    first_max, first_sum, first_acc = first_part
    second_max, second_sum, second_acc = second_part
    joint_max = jnp.maximum(first_max, second_max)
    first_scale = jnp.exp(first_max - joint_max)
    second_scale = jnp.exp(second_max - joint_max)
    joint_sum = first_sum * first_scale + second_sum * second_scale
    joint_acc = first_acc * spread_heads(first_scale) + second_acc * spread_heads(second_scale)
    return (joint_max, joint_sum, joint_acc)


def local(
    tokens,
    norm_attn,
    self_qkv,
    self_out,
    norm_ffn,
    ffn_in,
    ffn_out,
    norm_final,
    pad_lengths,
    targets,
    target_lengths,
    norm_cross,
    cross_query,
    cross_kv,
    cross_out,
):
    row_count = tokens.shape[0]
    heads_here = self_qkv.shape[2] // HD
    scaling = HD ** (-0.5)
    normed = rms_norm(tokens, norm_attn).astype(jnp.bfloat16)
    queries = jnp.dot(normed, self_qkv[0], preferred_element_type=jnp.float32).astype(jnp.bfloat16)
    keys_local = jnp.dot(normed, self_qkv[1], preferred_element_type=jnp.float32).astype(
        jnp.bfloat16
    )
    values_local = jnp.dot(normed, self_qkv[2], preferred_element_type=jnp.float32).astype(
        jnp.bfloat16
    )
    query_heads = queries.reshape(row_count, heads_here, HD)
    start_state = (
        jnp.full((heads_here, row_count), masked_score, jnp.float32),
        jnp.zeros((heads_here, row_count), jnp.float32),
        jnp.zeros((row_count, heads_here * HD), jnp.float32),
    )
    key_piece, value_piece = in_one_piece((keys_local, values_local), SEQ, 0, 1)
    piece_rows = key_piece.shape[0]
    block_width = math.gcd(piece_rows, 2048)

    def step_once(inner_state, block_index):
        first_row = block_index * block_width
        key_rows = lax.dynamic_slice_in_dim(key_piece, first_row, block_width, 0)
        value_rows = lax.dynamic_slice_in_dim(value_piece, first_row, block_width, 0)
        positions = first_row + jnp.arange(block_width, dtype=jnp.int32)
        updated = flash_block(
            inner_state,
            query_heads,
            key_rows,
            value_rows,
            live_keys(positions, pad_lengths),
            scaling,
        )
        return (updated, None)

    final_state, unused = lax.scan(
        step_once, start_state, jnp.arange(piece_rows // block_width, dtype=jnp.int32)
    )
    final_max, final_sum, final_acc = final_state
    context = (final_acc / spread_heads(final_sum)).astype(jnp.bfloat16)
    attn_part = jnp.dot(context, self_out, preferred_element_type=jnp.float32)
    share_width = D // lax.axis_size("head")
    first_col = lax.axis_index("head") * share_width
    token_share = lax.dynamic_slice_in_dim(tokens, first_col, share_width, 1).astype(jnp.float32)
    hidden_share = token_share + sent_and_summed(attn_part.astype(jnp.bfloat16), "head", 1)
    square_sum = over_copies(jnp.sum(hidden_share * hidden_share, axis=1), "head")
    ffn_gain = lax.dynamic_slice_in_dim(norm_ffn, first_col, share_width, 0)
    ffn_share_in = (
        hidden_share * lax.rsqrt(square_sum[:, None] / D + epsilon) * ffn_gain[None, :]
    ).astype(jnp.bfloat16)
    ffn_normed = gather_directly(ffn_share_in, "head", 1)
    ffn_part = feed_forward(ffn_normed, ffn_in, ffn_out)
    final_share = hidden_share + sent_and_summed(ffn_part.astype(jnp.bfloat16), "head", 1)
    final_square = over_copies(jnp.sum(final_share * final_share, axis=1), "head")
    final_gain = lax.dynamic_slice_in_dim(norm_final, first_col, share_width, 0)
    encoded_share = (
        final_share * lax.rsqrt(final_square[:, None] / D + epsilon) * final_gain[None, :]
    ).astype(jnp.bfloat16)
    encoded = gather_directly(encoded_share, "head", 1)
    target_rows = targets.shape[0]
    cross_normed = rms_norm(targets, norm_cross).astype(jnp.bfloat16)
    cross_queries = jnp.dot(cross_normed, cross_query, preferred_element_type=jnp.float32).astype(
        jnp.bfloat16
    )
    cross_keys = jnp.dot(encoded, cross_kv[0], preferred_element_type=jnp.float32).astype(
        jnp.bfloat16
    )
    cross_values = jnp.dot(encoded, cross_kv[1], preferred_element_type=jnp.float32).astype(
        jnp.bfloat16
    )
    cross_heads = cross_queries.reshape(target_rows, heads_here, HD)
    keys_split = cross_keys.reshape(row_count, heads_here, HD)
    values_split = cross_values.reshape(row_count, heads_here, HD)
    positions = lax.axis_index(SEQ) * row_count + jnp.arange(row_count, dtype=jnp.int32)
    live_here = live_keys(positions, pad_lengths)
    cross_scores = (
        jnp.einsum("qhd,khd->hqk", cross_heads, keys_split, preferred_element_type=jnp.float32)
        * scaling
    )
    cross_scores = jnp.where(live_here[None, None, :], cross_scores, masked_score)
    local_max = jnp.max(cross_scores, axis=-1)
    weights = jnp.where(
        live_here[None, None, :], jnp.exp(cross_scores - local_max[:, :, None]), 0.0
    )
    local_sum = jnp.sum(weights, axis=-1)
    local_mixed = jnp.einsum(
        "hqk,khd->qhd",
        weights.astype(jnp.bfloat16),
        values_split,
        preferred_element_type=jnp.float32,
    )
    joint_max, weight_sum, mixed_values = merged_by_axis(
        (local_max, local_sum, local_mixed.reshape(target_rows, heads_here * HD)),
        SEQ,
        combine_parts,
    )
    share_rows = target_rows // lax.axis_size(SEQ)
    first_row = lax.axis_index(SEQ) * share_rows
    mixed_rows = lax.dynamic_slice_in_dim(mixed_values, first_row, share_rows, 0)
    sum_rows = lax.dynamic_slice_in_dim(weight_sum, first_row, share_rows, 1)
    cross_context = (mixed_rows / spread_heads(sum_rows)).astype(jnp.bfloat16)
    cross_part = jnp.dot(cross_context, cross_out, preferred_element_type=jnp.float32)
    cross_total = over_copies_2(cross_part.astype(jnp.bfloat16), "head").astype(jnp.float32)
    slots = first_row + jnp.arange(share_rows, dtype=jnp.int32)
    target_live = live_within(slots, target_lengths, TGT_LEN)
    target_share = lax.dynamic_slice_in_dim(targets, first_row, share_rows, 0).astype(jnp.float32)
    decoded_share = (target_share + jnp.where(target_live[:, None], cross_total, 0.0)).astype(
        jnp.bfloat16
    )
    decoded = gather_directly(decoded_share, SEQ, 0)
    return (encoded, decoded)


def solution(mesh):
    torus = Mesh(
        mesh.devices.reshape(8, 2, 2, mesh.shape["head"]), ("seq_0", "seq_1", "seq_2", "head")
    )
    in_specs = (
        P(SEQ, None),
        P(),
        P(None, None, "head"),
        P("head", None),
        P(),
        P(None, None, "head"),
        P("head", None),
        P(),
        P(),
        P(),
        P(),
        P(),
        P(None, "head"),
        P(None, None, "head"),
        P("head", None),
    )
    out_specs = (P(SEQ, None), P())
    return jax.shard_map(local, mesh=torus, in_specs=in_specs, out_specs=out_specs, check_vma=False)
```

profile of v0, /device:TPU:1, one launch (start us, length us, event | category | flops | bytes accessed | tf_op | source)
XLA Modules:
  0.0 477.5 jit_solution(13851711400784383767)
XLA Ops:
  14.6 74.5 %all-gather.6.cloned.1.call-done = bf16[16384,256]{0,1:T(8,128)(2,1)} async-done(((bf16[512,256]{0,1:T(8,128)(2,1)}), bf16[16384,256]{0,1:T(8,128)(2,1)}) %all-gather.6.cloned.1.call-update) | async-done | bytes 8388624 | tf_op jit(solution)/shard_map/all_gather | solution.py:23
  89.1 5.8 %fusion.172 = (bf16[16384,128]{0,1:T(8,128)(2,1)}, bf16[16384,128]{0,1:T(8,128)(2,1)}) fusion(bf16[16384,256]{0,1:T(8,128)(2,1)} %all-gather.6.cloned.1.call-done), kind=kLoop, calls=%fused_computation.302 | loop fusion | bytes 16777216 | tf_op jit(solution)/shard_map/split | solution.py:24
  94.9 129.6 %while.17 = (s32[]{:T(128)}, f32[2,512]{1,0:T(2,128)S(1)}, f32[2,512]{1,0:T(2,128)S(1)}, f32[512,128]{0,1:T(8,128)S(1)}, s32[8]{0:T(128)S(1)}, /*index=5*/s32[32...) while((s32[]{:T(128)}, f32[2,512]{1,0:T(2,128)S(1)}, ...), condition=%wide.region_5.6_spmd.clone, body=%wide.region_1.5_spmd.clone.sunk | while | flops 564590592 | bytes 54763900 | solution.py:214
  101.9 6.4 %fusion.208 = f32[2,64,512]{2,1,0:T(8,128)S(1)} fusion(bf16[2048,2,64]{0,2,1:T(8,128)(2,1)S(1)} %bitcast.501, f32[2,2048,512]{2,1,0:T(8,128)} %get-tuple-element.294, f32[2,512]{1,0:T(2,128)S(1)} %get-tuple-element.324, pred[2048]{0:T(1024)(128)(4,1)S(1)} %fusion.204), kind=kOutput, calls=%fused_computation.7.clone.1 | convolution fusion | flops 278921216 | bytes 9181184 | tf_op jit(solution)/shard_map/while/body/eval_jaxpr/hqk,khd->qhd/dot_general | solution.py:131
  118.1 6.4 %fusion.208 = f32[2,64,512]{2,1,0:T(8,128)S(1)} fusion(bf16[2048,2,64]{0,2,1:T(8,128)(2,1)S(1)} %bitcast.501, f32[2,2048,512]{2,1,0:T(8,128)} %get-tuple-element.294, f32[2,512]{1,0:T(2,128)S(1)} %get-tuple-element.324, pred[2048]{0:T(1024)(128)(4,1)S(1)} %fusion.204), kind=kOutput, calls=%fused_computation.7.clone.1 | convolution fusion | flops 278921216 | bytes 9181184 | tf_op jit(solution)/shard_map/while/body/eval_jaxpr/hqk,khd->qhd/dot_general | solution.py:131
  134.3 6.4 %fusion.208 = f32[2,64,512]{2,1,0:T(8,128)S(1)} fusion(bf16[2048,2,64]{0,2,1:T(8,128)(2,1)S(1)} %bitcast.501, f32[2,2048,512]{2,1,0:T(8,128)} %get-tuple-element.294, f32[2,512]{1,0:T(2,128)S(1)} %get-tuple-element.324, pred[2048]{0:T(1024)(128)(4,1)S(1)} %fusion.204), kind=kOutput, calls=%fused_computation.7.clone.1 | convolution fusion | flops 278921216 | bytes 9181184 | tf_op jit(solution)/shard_map/while/body/eval_jaxpr/hqk,khd->qhd/dot_general | solution.py:131
  150.5 6.4 %fusion.208 = f32[2,64,512]{2,1,0:T(8,128)S(1)} fusion(bf16[2048,2,64]{0,2,1:T(8,128)(2,1)S(1)} %bitcast.501, f32[2,2048,512]{2,1,0:T(8,128)} %get-tuple-element.294, f32[2,512]{1,0:T(2,128)S(1)} %get-tuple-element.324, pred[2048]{0:T(1024)(128)(4,1)S(1)} %fusion.204), kind=kOutput, calls=%fused_computation.7.clone.1 | convolution fusion | flops 278921216 | bytes 9181184 | tf_op jit(solution)/shard_map/while/body/eval_jaxpr/hqk,khd->qhd/dot_general | solution.py:131
  166.7 6.4 %fusion.208 = f32[2,64,512]{2,1,0:T(8,128)S(1)} fusion(bf16[2048,2,64]{0,2,1:T(8,128)(2,1)S(1)} %bitcast.501, f32[2,2048,512]{2,1,0:T(8,128)} %get-tuple-element.294, f32[2,512]{1,0:T(2,128)S(1)} %get-tuple-element.324, pred[2048]{0:T(1024)(128)(4,1)S(1)} %fusion.204), kind=kOutput, calls=%fused_computation.7.clone.1 | convolution fusion | flops 278921216 | bytes 9181184 | tf_op jit(solution)/shard_map/while/body/eval_jaxpr/hqk,khd->qhd/dot_general | solution.py:131
  182.9 6.4 %fusion.208 = f32[2,64,512]{2,1,0:T(8,128)S(1)} fusion(bf16[2048,2,64]{0,2,1:T(8,128)(2,1)S(1)} %bitcast.501, f32[2,2048,512]{2,1,0:T(8,128)} %get-tuple-element.294, f32[2,512]{1,0:T(2,128)S(1)} %get-tuple-element.324, pred[2048]{0:T(1024)(128)(4,1)S(1)} %fusion.204), kind=kOutput, calls=%fused_computation.7.clone.1 | convolution fusion | flops 278921216 | bytes 9181184 | tf_op jit(solution)/shard_map/while/body/eval_jaxpr/hqk,khd->qhd/dot_general | solution.py:131
  199.1 6.4 %fusion.208 = f32[2,64,512]{2,1,0:T(8,128)S(1)} fusion(bf16[2048,2,64]{0,2,1:T(8,128)(2,1)S(1)} %bitcast.501, f32[2,2048,512]{2,1,0:T(8,128)} %get-tuple-element.294, f32[2,512]{1,0:T(2,128)S(1)} %get-tuple-element.324, pred[2048]{0:T(1024)(128)(4,1)S(1)} %fusion.204), kind=kOutput, calls=%fused_computation.7.clone.1 | convolution fusion | flops 278921216 | bytes 9181184 | tf_op jit(solution)/shard_map/while/body/eval_jaxpr/hqk,khd->qhd/dot_general | solution.py:131
  215.3 6.4 %fusion.208 = f32[2,64,512]{2,1,0:T(8,128)S(1)} fusion(bf16[2048,2,64]{0,2,1:T(8,128)(2,1)S(1)} %bitcast.501, f32[2,2048,512]{2,1,0:T(8,128)} %get-tuple-element.294, f32[2,512]{1,0:T(2,128)S(1)} %get-tuple-element.324, pred[2048]{0:T(1024)(128)(4,1)S(1)} %fusion.204), kind=kOutput, calls=%fused_computation.7.clone.1 | convolution fusion | flops 278921216 | bytes 9181184 | tf_op jit(solution)/shard_map/while/body/eval_jaxpr/hqk,khd->qhd/dot_general | solution.py:131
  226.2 6.3 %all-to-all-start = ((bf16[8,512,128]{2,1,0:T(8,128)(2,1)}), bf16[8,512,128]{2,1,0:T(8,128)(2,1)S(1)}, u32[]{:S(2)}, u32[]{:S(2)}) async-start(bf16[8,512,128]{2,1,0:T(8,128)(2,1)} %bitcast.473), calls=%async_computation | async-start | bytes 2097152 | tf_op jit(solution)/shard_map/all_to_all | solution.py:34
  232.5 17.4 %all-to-all-done = bf16[8,512,128]{2,1,0:T(8,128)(2,1)S(1)} async-done(((bf16[8,512,128]{2,1,0:T(8,128)(2,1)}), bf16[8,512,128]{2,1,0:T(8,128)(2,1)S(1)}, u32[]{:S(2)}, u32[]{:S(2)}) %all-to-all-start) | async-done | bytes 1048608 | tf_op jit(solution)/shard_map/all_to_all | solution.py:34
  254.9 5.7 %all-to-all-done.1 = f32[8,1,512]{2,1,0:T(1,128)S(1)} async-done(((f32[8,1,512]{2,1,0:T(1,128)}), f32[8,1,512]{2,1,0:T(1,128)S(1)}, u32[]{:S(2)}, u32[]{:S(2)}) %all-to-all-start.1) | async-done | bytes 16416 | tf_op jit(solution)/shard_map/all_to_all | solution.py:40
  261.0 18.6 %all_to_all.42 = bf16[8,512,128]{1,2,0:T(8,128)(2,1)S(1)} all-to-all(bf16[8,512,128]{1,2,0:T(8,128)(2,1)S(1)} %broadcast_in_dim.224), channel_id=1, replica_groups=mesh['seq_0'=8,'seq_1'=2,'seq_2'=2,'head'=8] {'head'}, dimensions={0} | all-to-all | bytes 2097152 | tf_op jit(solution)/shard_map/all_to_all | solution.py:40
  290.6 17.3 %all-to-all-done.3 = bf16[8,512,128]{2,1,0:T(8,128)(2,1)S(1)} async-done(((bf16[8,512,128]{2,1,0:T(8,128)(2,1)}), bf16[8,512,128]{2,1,0:T(8,128)(2,1)S(1)}, u32[]{:S(2)}, u32[]{:S(2)}) %all-to-all-start.3) | async-done | bytes 1048608 | tf_op jit(solution)/shard_map/all_to_all | solution.py:34
  327.0 13.9 %all-to-all-done.5 = bf16[8,512,128]{2,1,0:T(8,128)(2,1)S(1)} async-done(((bf16[8,512,128]{2,1,0:T(8,128)(2,1)}), bf16[8,512,128]{2,1,0:T(8,128)(2,1)S(1)}, u32[]{:S(2)}, u32[]{:S(2)}) %all-to-all-start.5) | async-done | bytes 1048608 | tf_op jit(solution)/shard_map/all_to_all | solution.py:40
  346.9 32.5 %all-gather.8.cloned.1.call-done = f32[4224,128]{1,0:T(8,128)} async-done(((f32[528,128]{1,0:T(8,128)}), f32[4224,128]{1,0:T(8,128)}) %all-gather.8.cloned.1.call-update) | async-done | bytes 2162704 | tf_op jit(solution)/shard_map/all_gather | solution.py:67
  402.9 6.0 %all-gather.1 = f32[1056,128]{1,0:T(8,128)S(1)} all-gather(f32[528,128]{1,0:T(8,128)S(1)} %pad_maximum_fusion.1), channel_id=3, replica_groups=mesh['seq_0'=8,'seq_1'=2,'seq_2'=2,'head'=8] {'seq_1'}, dimensions={0}, use_global_device_ids=true | all-gather | bytes 811008 | tf_op jit(solution)/shard_map/all_gather | solution.py:67
  409.4 7.7 %all-gather.2 = f32[1056,128]{1,0:T(8,128)S(1)} all-gather(f32[528,128]{1,0:T(8,128)S(1)} %pad_maximum_fusion.2), channel_id=4, replica_groups=mesh['seq_0'=8,'seq_1'=2,'seq_2'=2,'head'=8] {'seq_2'}, dimensions={0}, use_global_device_ids=true | all-gather | bytes 811008 | tf_op jit(solution)/shard_map/all_gather | solution.py:67
  418.7 6.6 %all-to-all-start.6 = ((bf16[8,16,1024]{2,1,0:T(8,128)(2,1)}), bf16[8,16,1024]{2,1,0:T(8,128)(2,1)S(1)}, u32[]{:S(2)}, u32[]{:S(2)}) async-start(bf16[8,16,1024]{2,1,0:T(8,128)(2,1)} %broadcast_in_dim.254), calls=%async_computation.6 | async-start | bytes 524288 | tf_op jit(solution)/shard_map/all_to_all | solution.py:40
  425.4 8.4 %all-to-all-done.6 = bf16[8,16,1024]{2,1,0:T(8,128)(2,1)S(1)} async-done(((bf16[8,16,1024]{2,1,0:T(8,128)(2,1)}), bf16[8,16,1024]{2,1,0:T(8,128)(2,1)S(1)}, u32[]{:S(2)}, u32[]{:S(2)}) %all-to-all-start.6) | async-done | bytes 262176 | tf_op jit(solution)/shard_map/all_to_all | solution.py:40
  435.8 5.9 %all-to-all-start.7 = ((bf16[32,16,1024]{2,1,0:T(8,128)(2,1)}), bf16[32,16,1024]{2,1,0:T(8,128)(2,1)S(1)}, u32[]{:S(2)}, u32[]{:S(2)}) async-start(bf16[32,16,1024]{2,1,0:T(8,128)(2,1)} %broadcast_in_dim.256), calls=%async_computation.7 | async-start | bytes 2097152 | tf_op jit(solution)/shard_map/all_to_all | solution.py:40
  442.9 26.8 %all-to-all-done.7 = bf16[32,16,1024]{2,1,0:T(8,128)(2,1)S(1)} async-done(((bf16[32,16,1024]{2,1,0:T(8,128)(2,1)}), bf16[32,16,1024]{2,1,0:T(8,128)(2,1)S(1)}, u32[]{:S(2)}, u32[]{:S(2)}) %all-to-all-start.7) | async-done | bytes 1048608 | tf_op jit(solution)/shard_map/all_to_all | solution.py:40
  (294 shorter events, 152.3 us)
Async XLA Ops:
  7.2 273.9 %copy-start = (bf16[352,1024]{1,0:T(8,128)(2,1)S(1)}, bf16[352,1024]{1,0:T(8,128)(2,1)}, u32[]{:S(2)}) copy-start(bf16[352,1024]{1,0:T(8,128)(2,1)} %param.23) | copy-start | bytes 2162692
  7.2 81.9 %all-gather.6.cloned.1.call-start = ((), (), s32[]{:S(2)}) async-start(), calls=%async_computation.8 | async-start | bytes 8650752 | tf_op jit(solution)/shard_map/all_gather | solution.py:23
  14.6 80.3 %copy-start.8 = (s32[32]{0:T(128)S(1)}, s32[32]{0:T(128)}, u32[]{:S(2)}) copy-start(s32[32]{0:T(128)} %param.25) | copy-start | bytes 388
  94.9 129.6 %copy-start.7 = (bf16[128,1024]{1,0:T(8,128)(2,1)S(1)}, bf16[128,1024]{1,0:T(8,128)(2,1)}, u32[]{:S(2)}) copy-start(bf16[128,1024]{1,0:T(8,128)(2,1)} %param.20) | copy-start | bytes 786436
  101.9 6.5 %slice-start = ((s8[8388608]{0:T(1024)(128)(4,1)}), s8[4194304]{0:T(1024)(128)(4,1)S(1)}, s32[]{:S(2)}) async-start(s8[8388608]{0:T(1024)(128)(4,1)} %bitcast.498), calls=%async_computation.10 | async-start | bytes 8388608 | tf_op jit(solution)/shard_map/while
  101.9 6.5 %slice-start.1 = ((s8[8388608]{0:T(1024)(128)(4,1)}), s8[4194304]{0:T(1024)(128)(4,1)S(1)}, s32[]{:S(2)}) async-start(s8[8388608]{0:T(1024)(128)(4,1)} %bitcast.498), calls=%async_computation.11 | async-start | bytes 8388608 | tf_op jit(solution)/shard_map/while
  118.1 6.5 %slice-start = ((s8[8388608]{0:T(1024)(128)(4,1)}), s8[4194304]{0:T(1024)(128)(4,1)S(1)}, s32[]{:S(2)}) async-start(s8[8388608]{0:T(1024)(128)(4,1)} %bitcast.498), calls=%async_computation.10 | async-start | bytes 8388608 | tf_op jit(solution)/shard_map/while
  150.5 6.5 %slice-start = ((s8[8388608]{0:T(1024)(128)(4,1)}), s8[4194304]{0:T(1024)(128)(4,1)S(1)}, s32[]{:S(2)}) async-start(s8[8388608]{0:T(1024)(128)(4,1)} %bitcast.498), calls=%async_computation.10 | async-start | bytes 8388608 | tf_op jit(solution)/shard_map/while
  166.7 6.5 %slice-start = ((s8[8388608]{0:T(1024)(128)(4,1)}), s8[4194304]{0:T(1024)(128)(4,1)S(1)}, s32[]{:S(2)}) async-start(s8[8388608]{0:T(1024)(128)(4,1)} %bitcast.498), calls=%async_computation.10 | async-start | bytes 8388608 | tf_op jit(solution)/shard_map/while
  226.2 23.7 %all-to-all-start = ((bf16[8,512,128]{2,1,0:T(8,128)(2,1)}), bf16[8,512,128]{2,1,0:T(8,128)(2,1)S(1)}, u32[]{:S(2)}, u32[]{:S(2)}) async-start(bf16[8,512,128]{2,1,0:T(8,128)(2,1)} %bitcast.473), calls=%async_computation | async-start | bytes 2097152 | tf_op jit(solution)/shard_map/all_to_all | solution.py:34
  250.8 9.8 %all-to-all-start.1 = ((f32[8,1,512]{2,1,0:T(1,128)}), f32[8,1,512]{2,1,0:T(1,128)S(1)}, u32[]{:S(2)}, u32[]{:S(2)}) async-start(f32[8,1,512]{2,1,0:T(1,128)} %broadcast_in_dim.223), calls=%async_computation.1 | async-start | bytes 32768 | tf_op jit(solution)/shard_map/all_to_all | solution.py:40
  260.9 18.7 %copy-start.9 = (bf16[2,1024,352]{1,2,0:T(8,128)(2,1)S(1)}, bf16[2,1024,352]{1,2,0:T(8,128)(2,1)}, u32[]{:S(2)}) copy-start(bf16[2,1024,352]{1,2,0:T(8,128)(2,1)} %param.22) | copy-start | bytes 4325380
  287.0 20.9 %all-to-all-start.3 = ((bf16[8,512,128]{2,1,0:T(8,128)(2,1)}), bf16[8,512,128]{2,1,0:T(8,128)(2,1)S(1)}, u32[]{:S(2)}, u32[]{:S(2)}) async-start(bf16[8,512,128]{2,1,0:T(8,128)(2,1)} %bitcast.471), calls=%async_computation.3 | async-start | bytes 2097152 | tf_op jit(solution)/shard_map/all_to_all | solution.py:34
  308.8 9.8 %all-to-all-start.4 = ((f32[8,1,512]{2,1,0:T(1,128)}), f32[8,1,512]{2,1,0:T(1,128)S(1)}, u32[]{:S(2)}, u32[]{:S(2)}) async-start(f32[8,1,512]{2,1,0:T(1,128)} %broadcast_in_dim.225), calls=%async_computation.4 | async-start | bytes 32768 | tf_op jit(solution)/shard_map/all_to_all | solution.py:40
  318.9 6.6 %copy-start.5 = (bf16[512,1024]{1,0:T(8,128)(2,1)S(1)}, bf16[512,1024]{1,0:T(8,128)(2,1)}, u32[]{:S(2)}) copy-start(bf16[512,1024]{1,0:T(8,128)(2,1)} %param.26) | copy-start | bytes 3145732
  318.9 6.6 %copy-start.11 = (f32[1024]{0:T(1024)S(1)}, f32[1024]{0:T(1024)}, u32[]{:S(2)}) copy-start(f32[1024]{0:T(1024)} %param.28) | copy-start | bytes 12292
  320.0 20.9 %all-to-all-start.5 = ((bf16[8,512,128]{2,1,0:T(8,128)(2,1)}), bf16[8,512,128]{2,1,0:T(8,128)(2,1)S(1)}, u32[]{:S(2)}, u32[]{:S(2)}) async-start(bf16[8,512,128]{2,1,0:T(8,128)(2,1)} %broadcast_in_dim.226), calls=%async_computation.5 | async-start | bytes 2097152 | tf_op jit(solution)/shard_map/all_to_all | solution.py:40
  323.6 55.8 %all-gather.8.cloned.1.call-start = ((), (), s32[]{:S(2)}) async-start(), calls=%async_computation.9 | async-start | bytes 2433024 | tf_op jit(solution)/shard_map/all_gather | solution.py:67
  388.2 12.6 %copy-start.4 = (f32[4224,128]{1,0:T(8,128)S(1)}, f32[4224,128]{1,0:T(8,128)}, u32[]{:S(2)}) copy-start(f32[4224,128]{1,0:T(8,128)} %all-gather.8.cloned.1.call-done) | copy-start | bytes 6488068
  409.3 8.5 %copy-start.6 = (bf16[128,1024]{1,0:T(8,128)(2,1)S(1)}, bf16[128,1024]{1,0:T(8,128)(2,1)}, u32[]{:S(2)}) copy-start(bf16[128,1024]{1,0:T(8,128)(2,1)} %param.31) | copy-start | bytes 786436
  409.4 15.9 %copy-start.12 = (s32[4]{0:T(128)S(1)}, s32[4]{0:T(128)}, u32[]{:S(2)}) copy-start(s32[4]{0:T(128)} %param.27) | copy-start | bytes 52
  418.7 22.9 %copy-start.2 = (bf16[8,512,128]{1,2,0:T(8,128)(2,1)S(1)}, bf16[8,512,128]{1,2,0:T(8,128)(2,1)}, u32[]{:S(2)}) copy-start(bf16[8,512,128]{1,2,0:T(8,128)(2,1)} %copy-done.1) | copy-start | bytes 3145732
  418.7 15.1 %all-to-all-start.6 = ((bf16[8,16,1024]{2,1,0:T(8,128)(2,1)}), bf16[8,16,1024]{2,1,0:T(8,128)(2,1)S(1)}, u32[]{:S(2)}, u32[]{:S(2)}) async-start(bf16[8,16,1024]{2,1,0:T(8,128)(2,1)} %broadcast_in_dim.254), calls=%async_computation.6 | async-start | bytes 524288 | tf_op jit(solution)/shard_map/all_to_all | solution.py:40
  435.8 33.9 %all-to-all-start.7 = ((bf16[32,16,1024]{2,1,0:T(8,128)(2,1)}), bf16[32,16,1024]{2,1,0:T(8,128)(2,1)S(1)}, u32[]{:S(2)}, u32[]{:S(2)}) async-start(bf16[32,16,1024]{2,1,0:T(8,128)(2,1)} %broadcast_in_dim.256), calls=%async_computation.7 | async-start | bytes 2097152 | tf_op jit(solution)/shard_map/all_to_all | solution.py:40
  (14 other events, 81.6 us)
Sparse Core Ops, SparseCore 0:
  13.2 75.8 all-gather.5
  347.0 32.3 all-gather.7
where the time goes:
time: 479 us; the launch traced here: 478 us
  waiting for transfers between devices  202 us (42%)
  matrix products  101 us (21%)
  local copies, waits for them, and re-layouts  53.9 us (11%)
  other arithmetic  34.1 us (7%)
  starting transfers between devices  32.8 us (7%)
  blocking collectives  32.3 us (7%)
  between operations  14.7 us (3%)
  loops' own time  6.13 us (1%)
    all_gather x1, waiting for transfers between devices, in_one_piece(): whole = lax.all_gather(both, axis, axis=dim, tiled=True)  74.5 us
    all_to_all x5, waiting for transfers between devices, sent_to_all(): return lax.all_to_all(copies, axis, split_axis=0, concat_axis=0, tiled=True)  60.5 us
    dot_general x8, matrix products, flash_block(): jnp.einsum('hqk,khd->qhd', weights.astype(jnp.bfloat16), values_split, pr...  51.1 us
    all_to_all x2, waiting for transfers between devices, sent_and_summed(): lax.all_to_all(blocks, axis, split_axis=0, concat_axis=0, tiled=True)  34.7 us
    dot_general x8, matrix products, flash_block(): jnp.einsum('qhd,khd->hqk', query_heads, keys_split, preferred_element_typ...  34.3 us
    all_gather x1, waiting for transfers between devices, all_in_one(): both, at, found = (lax.all_gather(jnp.concatenate(lines), axis), 0, {})  32.5 us
    all_to_all x5, starting transfers between devices, sent_to_all(): return lax.all_to_all(copies, axis, split_axis=0, concat_axis=0, tiled=True)  22.6 us
    reduce_sum x8, other arithmetic, flash_block(): new_sum = running_sum * shrink + jnp.sum(weights, axis=-1)  20.9 us
  transfers between devices with their start and end apart: 9, of which 9 were waited for; matrix products, arithmetic and copies ran while one was open for 2% of the time, Pallas kernels for 0%

commit v1 on v0

v1 whole, which is shorter than its diff:
```python
import functools
import math

import jax
import jax.numpy as jnp
from jax import lax
from jax.experimental import pallas as pl
from jax.experimental.pallas import tpu as pltpu
from jax.sharding import Mesh
from jax.sharding import PartitionSpec as P

D = 1024
HD = 64
TOK_DEV = 512
TGT_LEN = 128


epsilon = 1e-06
masked_score = -1e30


NZ = 8
SLOTS = 32
UP = (("O", 0, 0), ("O", 0, 1), ("O", 1, 0), ("O", 1, 1), ("O", 2, 0), ("O", 2, 1), ("P", 2, 0), ("O", 3, 0), ("P", 2, 1), ("P", 3, 0))
DOWN = (("O", 0, 1), ("O", 0, 0), ("O", -1, 1), ("O", -1, 0), ("O", -2, 1), ("O", -2, 0), ("P", -2, 1), ("O", -3, 1), ("P", -3, 1), ("P", -2, 0))
SIDE = (("O", 0, 0), ("O", 0, 1), ("O", 1, 0), ("O", -1, 1), ("O", 2, 0), ("O", -2, 1), ("O", 2, 1), ("O", -2, 0), ("O", 1, 1), ("O", -1, 0))
CHIPS = (("O", 0), ("O", 1), ("O", -1), ("P", 0), ("O", 2), ("O", -2), ("O", 3), ("O", -3), ("P", 2), ("P", -2), ("O", 4), ("P", 1), ("P", 3), ("P", -1), ("P", -3), ("P", 4))
STEPS_BEFORE = {1: (0, 1), 3: (2,), 4: (3,), 6: (4, 5), 8: (6,), 9: (7,), 11: (8,), 13: (9,)}
STEPS = 10


def link_plan():
    arrive = {("O", 0, 0): -1, ("O", 0, 1): -1}
    arrivals = []
    for s in range(STEPS):
        new = [(UP[s][0], UP[s][1] + 1, UP[s][2]), (DOWN[s][0], DOWN[s][1] - 1, DOWN[s][2])]
        new.append(("P", SIDE[s][1], SIDE[s][2]))
        arrive.update({item: s for item in new})
        arrivals.append(new)
    waiting = {"up": list(UP), "down": list(DOWN), "side": list(SIDE)}
    sent = {name: 0 for name in waiting}
    sends = []
    for s in range(-1, STEPS):
        now = []
        for name, queue in waiting.items():
            while queue and sent[name] <= s + 2 and arrive[queue[0]] <= s:
                now.append((name, queue.pop(0)))
                sent[name] += 1
        sends.append(now)
    return arrivals, sends


def key_bias(length, rows):
    row = lax.broadcasted_iota(jnp.int32, (rows, 128), 0)
    lane = lax.broadcasted_iota(jnp.int32, (rows, 128), 1)
    return jnp.where((lane == 0) & (row >= length), masked_score, 0.0).astype(jnp.bfloat16)


def spread_queries(q_t):
    rows = lax.broadcasted_iota(jnp.int32, (256, 2 * q_t.shape[1]), 0)
    cols = lax.broadcasted_iota(jnp.int32, (256, 2 * q_t.shape[1]), 1)
    half = q_t.shape[1]
    two = jnp.concatenate([q_t, q_t], axis=1)
    full = jnp.concatenate([two, jnp.zeros_like(two)], axis=0)
    keep = ((rows < HD) & (cols < half)) | ((rows >= HD) & (rows < 2 * HD) & (cols >= half))
    return jnp.where(keep, full, jnp.where(rows == 2 * HD, 1.0, 0.0)).astype(jnp.bfloat16)


def self_attention_kernel(
    lens, tokens, gain, wqkv, context, keys, values, spread, acc, scores_0, scores_1, send, recv
):
    me = lax.axis_index("seq")
    core = lax.rem(me, 2)
    y = lax.rem(me // 2, 2)
    z = me // 4

    def index(dz, dy, dc):
        z_at = lax.rem(z + dz + NZ, NZ)
        y_at = y if dy == 0 else 1 - y
        c_at = core if dc == 0 else 1 - core
        return z_at * 4 + y_at * 2 + c_at

    places = {"up": index(1, 0, 0), "down": index(-1, 0, 0), "side": index(0, 1, 0), "mate": index(0, 0, 1)}
    barrier = pltpu.get_barrier_semaphore()
    for place in places.values():
        pl.semaphore_signal(barrier, inc=1, device_id={"seq": place}, device_id_type=pl.DeviceIdType.MESH)

    x = tokens[...].astype(jnp.float32)
    normed = (
        x * lax.rsqrt(jnp.mean(x * x, axis=1, keepdims=True) + epsilon) * gain[...]
    ).astype(jnp.bfloat16)
    keys[me] = jnp.dot(normed, wqkv[1], preferred_element_type=jnp.float32).astype(jnp.bfloat16)
    values[me] = jnp.dot(normed, wqkv[2], preferred_element_type=jnp.float32).T.astype(jnp.bfloat16)
    q_t = jnp.dot(normed, wqkv[0], preferred_element_type=jnp.float32).T
    pl.semaphore_wait(barrier, 4)

    numbers = iter(range(128))
    started = []

    def copy(kv, slot, place, number):
        buffer = (keys, values)[kv]
        return pltpu.make_async_remote_copy(
            src_ref=buffer.at[slot],
            dst_ref=buffer.at[slot],
            send_sem=send.at[number],
            recv_sem=recv.at[kv, slot],
            device_id={"seq": places[place]},
            device_id_type=pl.DeviceIdType.MESH,
        )

    def slot_of(line, d):
        return index(-d, 0 if line == "O" else 1, 0)

    def push(kv, slot, place):
        number = next(numbers)
        copy(kv, slot, place, number).start()
        started.append((kv, place, number))

    arrivals, sends = link_plan()
    for name, (line, d, kv) in sends[0]:
        push(kv, me, name)
    for kv in range(2):
        push(kv, me, "mate")

    spread[...] = spread_queries(q_t * (HD ** (-0.5) * math.log2(math.e)))
    acc[...] = jnp.zeros_like(acc)

    def step(s):
        for line, d, kv in arrivals[s]:
            slot = slot_of(line, d)
            copy(kv, slot, "mate", 0).wait_recv()
            push(kv, slot, "mate")
        for name, (line, d, kv) in sends[s + 1]:
            push(kv, slot_of(line, d), name)

    def chip_slot(j, dc):
        dz, dy = jnp.int32(0), jnp.int32(0)
        for k, (line, d) in enumerate(CHIPS):
            dz = jnp.where(j == k, -d, dz)
            dy = jnp.where(j == k, 0 if line == "O" else 1, dy)
        z_at = lax.rem(z + dz + NZ, NZ)
        y_at = lax.rem(y + dy, 2)
        c_at = core if dc == 0 else 1 - core
        return z_at * 4 + y_at * 2 + c_at

    def score(slot, into):
        rows = jnp.concatenate([keys[slot], key_bias(lens[slot], TOK_DEV)], axis=1)
        s = jnp.dot(rows, spread[...], preferred_element_type=jnp.float32)
        into[...] = s
        return jnp.max(s, axis=0, keepdims=True)

    def rest(slot, held, old, top):
        p = jnp.exp2(held[...] - top).astype(jnp.bfloat16)
        shrink = jnp.exp2(old - top)
        ones = jnp.ones((16, TOK_DEV), jnp.bfloat16)
        for h in range(2):
            cols = slice(h * TOK_DEV, (h + 1) * TOK_DEV)
            lhs = jnp.concatenate([values[slot, pl.ds(h * HD, HD), :], ones], axis=0)
            acc[h] = acc[h] * shrink[:, cols] + jnp.dot(lhs, p[:, cols], preferred_element_type=jnp.float32)

    def arrived(slot):
        for kv in range(2):
            copy(kv, slot, "mate", 0).wait_recv()

    start = jnp.full((1, 2 * TOK_DEV), masked_score, jnp.float32)
    mate = index(0, 0, 1)
    top = score(me, scores_0)
    arrived(mate)
    following = jnp.maximum(top, score(mate, scores_1))
    rest(me, scores_0, start, top)

    def body(j, carry):
        old, top = carry
        for at, steps in STEPS_BEFORE.items():

            @pl.when(j == at)
            def _():
                for s in steps:
                    step(s)

        here, there = chip_slot(j, 0), chip_slot(j, 1)
        later = jnp.maximum(top, score(here, scores_0))
        rest(chip_slot(j - 1, 1), scores_1, old, top)
        old, top = top, later
        arrived(there)
        later = jnp.maximum(top, score(there, scores_1))
        rest(here, scores_0, old, top)
        return top, later

    old, top = lax.fori_loop(1, len(CHIPS), body, (top, following))
    rest(chip_slot(jnp.int32(len(CHIPS) - 1), 1), scores_1, old, top)
    both = jnp.concatenate([acc[h, 0:HD, :] / acc[h, HD : HD + 1, :] for h in range(2)], axis=0)
    context[...] = both.T.astype(jnp.bfloat16)
    for kv, place, number in started:
        copy(kv, me, place, number).wait_send()


def self_attention(lens, tokens, gain, wqkv):
    vmem = pl.BlockSpec(memory_space=pltpu.VMEM)
    return pl.pallas_call(
        self_attention_kernel,
        out_shape=jax.ShapeDtypeStruct((TOK_DEV, 2 * HD), jnp.bfloat16),
        in_specs=[pl.BlockSpec(memory_space=pltpu.SMEM), vmem, vmem, vmem],
        out_specs=vmem,
        scratch_shapes=[
            pltpu.VMEM((SLOTS, TOK_DEV, 2 * HD), jnp.bfloat16),
            pltpu.VMEM((SLOTS, 2 * HD, TOK_DEV), jnp.bfloat16),
            pltpu.VMEM((256, 2 * TOK_DEV), jnp.bfloat16),
            pltpu.VMEM((2, HD + 16, TOK_DEV), jnp.float32),
            pltpu.VMEM((TOK_DEV, 2 * TOK_DEV), jnp.float32),
            pltpu.VMEM((TOK_DEV, 2 * TOK_DEV), jnp.float32),
            pltpu.SemaphoreType.DMA((72,)),
            pltpu.SemaphoreType.DMA((2, SLOTS)),
        ],
        compiler_params=pltpu.CompilerParams(
            collective_id=0, has_side_effects=True, vmem_limit_bytes=56 << 20
        ),
        name="self_attention",
    )(lens, tokens, gain, wqkv)


def cut_along(x, dim, count):
    before, after = (x.shape[:dim], x.shape[dim + 1 :])
    return jnp.moveaxis(x.reshape(*before, count, -1, *after), dim, 0)


def sent_and_summed(x, axis, dim):
    blocks = cut_along(x, dim, lax.axis_size(axis))
    arrived = lax.all_to_all(blocks, axis, split_axis=0, concat_axis=0, tiled=True)
    return arrived.astype(jnp.float32).sum(axis=0)


def sent_to_all(x, axis):
    copies = jnp.broadcast_to(x, (lax.axis_size(axis), *x.shape))
    return lax.all_to_all(copies, axis, split_axis=0, concat_axis=0, tiled=True)


def laid_out(blocks, dim):
    shape = list(blocks.shape[1:])
    shape[dim] *= blocks.shape[0]
    return jnp.moveaxis(blocks, 0, dim).reshape(shape)


def gather_directly(x, axis, dim):
    blocks = sent_to_all(x, axis)
    return laid_out(blocks, dim)


def over_copies_2(x, axis):
    everything = sent_to_all(x, axis)
    return jnp.sum(everything.astype(jnp.float32), axis=0)


def rms_norm(values, gain_vector):
    widened = values.astype(jnp.float32)
    return (
        widened
        * lax.rsqrt(jnp.mean(widened * widened, axis=-1, keepdims=True) + epsilon)
        * gain_vector
    )


def spread_heads(per_head):
    return jnp.repeat(per_head.T, HD, axis=1)


def live_within(positions, lengths, span):
    block_ids = jnp.arange(lengths.shape[0], dtype=jnp.int32)
    owners = positions // span
    lengths_here = jnp.sum(
        jnp.where(owners[:, None] == block_ids[None, :], lengths[None, :], 0), axis=1
    )
    return positions % span < lengths_here


def live_keys(positions, pad_lengths):
    return live_within(positions, pad_lengths, TOK_DEV)


def feed_forward(normed_in, ffn_in, ffn_out):
    gate_proj = jnp.dot(normed_in, ffn_in[0], preferred_element_type=jnp.float32)
    up_proj = jnp.dot(normed_in, ffn_in[1], preferred_element_type=jnp.float32)
    activated = (jax.nn.gelu(gate_proj, approximate=True) * up_proj).astype(jnp.bfloat16)
    return jnp.dot(activated, ffn_out, preferred_element_type=jnp.float32)


def local(
    tokens,
    norm_attn,
    self_qkv,
    self_out,
    norm_ffn,
    ffn_in,
    ffn_out,
    norm_final,
    pad_lengths,
    targets,
    target_lengths,
    norm_cross,
    cross_query,
    cross_kv,
    cross_out,
):
    row_count = tokens.shape[0]
    heads_here = self_qkv.shape[2] // HD
    scaling = HD ** (-0.5)
    context = self_attention(pad_lengths, tokens, norm_attn.reshape(1, D), self_qkv)
    attn_part = jnp.dot(context, self_out, preferred_element_type=jnp.float32)
    share = row_count // lax.axis_size("head")
    first = lax.axis_index("head") * share
    token_share = lax.dynamic_slice_in_dim(tokens, first, share, 0).astype(jnp.float32)
    hidden_share = token_share + sent_and_summed(attn_part.astype(jnp.bfloat16), "head", 0)
    ffn_normed = gather_directly(rms_norm(hidden_share, norm_ffn).astype(jnp.bfloat16), "head", 0)
    ffn_part = feed_forward(ffn_normed, ffn_in, ffn_out)
    final_share = hidden_share + sent_and_summed(ffn_part.astype(jnp.bfloat16), "head", 0)
    encoded = gather_directly(rms_norm(final_share, norm_final).astype(jnp.bfloat16), "head", 0)
    target_rows = targets.shape[0]
    cross_normed = rms_norm(targets, norm_cross).astype(jnp.bfloat16)
    cross_queries = jnp.dot(cross_normed, cross_query, preferred_element_type=jnp.float32).astype(
        jnp.bfloat16
    )
    cross_keys = jnp.dot(encoded, cross_kv[0], preferred_element_type=jnp.float32).astype(
        jnp.bfloat16
    )
    cross_values = jnp.dot(encoded, cross_kv[1], preferred_element_type=jnp.float32).astype(
        jnp.bfloat16
    )
    cross_heads = cross_queries.reshape(target_rows, heads_here, HD)
    keys_split = cross_keys.reshape(row_count, heads_here, HD)
    values_split = cross_values.reshape(row_count, heads_here, HD)
    positions = lax.axis_index("seq") * row_count + jnp.arange(row_count, dtype=jnp.int32)
    live_here = live_keys(positions, pad_lengths)
    cross_scores = (
        jnp.einsum("qhd,khd->hqk", cross_heads, keys_split, preferred_element_type=jnp.float32)
        * scaling
    )
    cross_scores = jnp.where(live_here[None, None, :], cross_scores, masked_score)
    local_max = jnp.max(cross_scores, axis=-1)
    weights = jnp.where(
        live_here[None, None, :], jnp.exp(cross_scores - local_max[:, :, None]), 0.0
    )
    local_sum = jnp.sum(weights, axis=-1)
    local_mixed = jnp.einsum(
        "hqk,khd->qhd",
        weights.astype(jnp.bfloat16),
        values_split,
        preferred_element_type=jnp.float32,
    )
    shares = lax.axis_size("seq")
    share_rows = target_rows // shares
    tops_sums = jnp.concatenate([local_max, local_sum], axis=0)
    tops_sums = tops_sums.reshape(2 * heads_here, shares, share_rows).transpose(1, 0, 2)
    tops_sums = jnp.pad(tops_sums.reshape(shares, 1, -1), ((0, 0), (0, 0), (0, 128 - 2 * heads_here * share_rows)))
    parts = jnp.concatenate([local_mixed.reshape(shares, share_rows, heads_here * HD), tops_sums], axis=1)
    parts = lax.all_to_all(parts, "seq", split_axis=0, concat_axis=0, tiled=True)
    stats = parts[:, share_rows, : 2 * heads_here * share_rows].reshape(shares, 2, heads_here, share_rows)
    tops, sums = stats[:, 0], stats[:, 1]
    factors = jnp.exp(tops - jnp.max(tops, axis=0, keepdims=True))
    total = jnp.sum(sums * factors, axis=0)
    spread = jnp.repeat(factors.transpose(0, 2, 1), HD, axis=2)
    mixed_rows = jnp.sum(parts[:, :share_rows] * spread, axis=0)
    first_row = lax.axis_index("seq") * share_rows
    cross_context = (mixed_rows / spread_heads(total)).astype(jnp.bfloat16)
    cross_part = jnp.dot(cross_context, cross_out, preferred_element_type=jnp.float32)
    cross_total = over_copies_2(cross_part.astype(jnp.bfloat16), "head").astype(jnp.float32)
    slots = first_row + jnp.arange(share_rows, dtype=jnp.int32)
    target_live = live_within(slots, target_lengths, TGT_LEN)
    target_share = lax.dynamic_slice_in_dim(targets, first_row, share_rows, 0).astype(jnp.float32)
    decoded_share = (target_share + jnp.where(target_live[:, None], cross_total, 0.0)).astype(
        jnp.bfloat16
    )
    decoded = gather_directly(decoded_share, "seq", 0)
    return (encoded, decoded)


def solution(mesh):
    in_specs = (
        P("seq", None),
        P(),
        P(None, None, "head"),
        P("head", None),
        P(),
        P(None, None, "head"),
        P("head", None),
        P(),
        P(),
        P(),
        P(),
        P(),
        P(None, "head"),
        P(None, None, "head"),
        P("head", None),
    )
    out_specs = (P("seq", None), P())
    return jax.shard_map(local, mesh=mesh, in_specs=in_specs, out_specs=out_specs, check_vma=False)
```

time: 479 us -> 223 us (0.47)
  waiting for transfers between devices: 202 us -> 72.2 us
  matrix products: 101 us -> 12.2 us
  Pallas kernels: 0 us -> 51.8 us
  local copies, waits for them, and re-layouts: 53.9 us -> 6.3 us
  other arithmetic: 34.1 us -> 3.89 us
  blocking collectives: 32.3 us -> 52.6 us
  between operations: 14.7 us -> 0.99 us
  starting transfers between devices: 32.8 us -> 22.5 us
  loops' own time: 6.13 us -> 0 us
    all_gather x2 -> x0, waiting for transfers between devices: 107 us -> none  [the longest x1 74.5 us: in_one_piece(): whole = lax.all_gather(both, axis, axis=dim, tiled=True)]
    dot_general x19 -> x0, matrix products: 90.4 us -> none  [the longest x8 51.1 us: flash_block(): jnp.einsum('hqk,khd->qhd', weights.astype(jnp.bfloat16), values_split, pr...]
    pallas_call x0 -> x1, Pallas kernels: none -> 51.8 us  [self_attention(): pl.pallas_call(self_attention_kernel, out_shape=jax.ShapeDtypeStruct((TOK...]
    all_to_all x5 -> x2, waiting for transfers between devices: 60.5 us -> 23.9 us  [sent_to_all(): return lax.all_to_all(copies, axis, split_axis=0, concat_axis=0, tiled=True)]
    all_to_all x1 -> x2, blocking collectives: 18.6 us -> 52.6 us  [sent_to_all(): return lax.all_to_all(copies, axis, split_axis=0, concat_axis=0, tiled=True)]
    reduce_sum x12 -> x2, other arithmetic: 21.3 us -> 0.22 us  [the longest x1 0.17 us: local(): total = jnp.sum(sums * factors, axis=0)]
    dynamic_slice x19 -> x0, local copies, waits for them, and re-layouts: 16.5 us -> none  [the longest x8 10.2 us: step_once(): lax.dynamic_slice_in_dim(value_piece, first_row, block_width, 0)]
    all_to_all x5 -> x2, starting transfers between devices: 22.6 us -> 6.97 us  [sent_to_all(): return lax.all_to_all(copies, axis, split_axis=0, concat_axis=0, tiled=True)]
  transfers between devices with their start and end apart: 9 -> 5, of which waited for: 9 -> 5; matrix products, arithmetic and copies ran while one was open for 2% -> 0% of each run, Pallas kernels for 0% -> 0%
where the time goes in v1:
time: 223 us
  waiting for transfers between devices  72.2 us (32%)
  blocking collectives  52.6 us (24%)
  Pallas kernels  51.8 us (23%)
  starting transfers between devices  22.5 us (10%)
  matrix products  12.2 us (5%)
  local copies, waits for them, and re-layouts  6.3 us (3%)
  other arithmetic  3.89 us (2%)
    all_to_all x2, blocking collectives, sent_to_all(): return lax.all_to_all(copies, axis, split_axis=0, concat_axis=0, tiled=True)  52.6 us
    pallas_call x1, Pallas kernels, self_attention(): pl.pallas_call(self_attention_kernel, out_shape=jax.ShapeDtypeStruct((TOK...  51.8 us
    all_to_all x2, waiting for transfers between devices, sent_and_summed(): lax.all_to_all(blocks, axis, split_axis=0, concat_axis=0, tiled=True)  34.7 us
    all_to_all x2, waiting for transfers between devices, sent_to_all(): return lax.all_to_all(copies, axis, split_axis=0, concat_axis=0, tiled=True)  23.9 us
    all_to_all x1, waiting for transfers between devices, local(): lax.all_to_all(parts, 'seq', split_axis=0, concat_axis=0, tiled=True)  13.7 us
    all_to_all x2, starting transfers between devices, sent_and_summed(): lax.all_to_all(blocks, axis, split_axis=0, concat_axis=0, tiled=True)  10.5 us
    all_to_all x2, starting transfers between devices, sent_to_all(): return lax.all_to_all(copies, axis, split_axis=0, concat_axis=0, tiled=True)  6.97 us
    all_to_all x1, starting transfers between devices, local(): lax.all_to_all(parts, 'seq', split_axis=0, concat_axis=0, tiled=True)  4.99 us
  transfers between devices with their start and end apart: 5, of which 5 were waited for; matrix products, arithmetic and copies ran while one was open for 0% of the time, Pallas kernels for 0%

profile of v1, /device:TPU:1, one launch (start us, length us, event | category | flops | bytes accessed | tf_op | source)
XLA Modules:
  0.0 222.5 jit_solution(3823630303871226972)
XLA Ops:
  0.7 51.8 %self_attention.1 = bf16[512,128]{1,0:T(8,128)(2,1)} custom-call(s32[32]{0:T(128)} %lens.1, bf16[512,1024]{1,0:T(8,128)(2,1)} %tokens.1, f32[1,1024]{1,0:T(1,128)} %bitcast.70, bf16[3,1024,128]{2,1,0:T(8,128)(2,1)} %wqkv.1), custom_call_target="tpu_custom_call" | custom-call | tf_op jit(solution)/shard_map/self_attention/pallas_call | solution.py:200
  52.4 2.4 %convolution_convert_fusion = bf16[512,1024]{1,0:T(8,128)(2,1)} fusion(bf16[512,128]{1,0:T(8,128)(2,1)} %self_attention.1, bf16[128,1024]{1,0:T(8,128)(2,1)S(1)} %copy-done.4), kind=kOutput, calls=%fused_computation.10 | convolution fusion | flops 134742016 | bytes 1441792 | tf_op jit(solution)/shard_map/dot_general | solution.py:308
  54.8 6.8 %all-to-all-start = ((bf16[8,64,1024]{2,1,0:T(8,128)(2,1)}), bf16[8,64,1024]{2,1,0:T(8,128)(2,1)S(1)}, u32[]{:S(2)}, u32[]{:S(2)}) async-start(bf16[8,64,1024]{2,1,0:T(8,128)(2,1)} %bitcast.1), calls=%async_computation | async-start | bytes 2097152 | tf_op jit(solution)/shard_map/all_to_all | solution.py:229
  61.6 17.4 %all-to-all-done = bf16[8,64,1024]{2,1,0:T(8,128)(2,1)S(1)} async-done(((bf16[8,64,1024]{2,1,0:T(8,128)(2,1)}), bf16[8,64,1024]{2,1,0:T(8,128)(2,1)S(1)}, u32[]{:S(2)}, u32[]{:S(2)}) %all-to-all-start) | async-done | bytes 1048608 | tf_op jit(solution)/shard_map/all_to_all | solution.py:229
  79.6 18.9 %all_to_all.35 = bf16[8,64,1024]{2,1,0:T(8,128)(2,1)S(1)} all-to-all(bf16[8,64,1024]{2,1,0:T(8,128)(2,1)S(1)} %broadcast_in_dim.89), channel_id=1, replica_groups=mesh['seq'=32,'head'=8] {'head'}, dimensions={0} | all-to-all | bytes 2097152 | tf_op jit(solution)/shard_map/all_to_all | solution.py:235
  98.5 1.4 fusion.25
  99.9 3.6 %convolution_convert_fusion.1 = bf16[512,1024]{1,0:T(8,128)(2,1)} fusion(bf16[352,1024]{1,0:T(8,128)(2,1)S(1)} %copy-done, bf16[512,1024]{1,0:T(8,128)(2,1)S(1)} %bitcast.62, f32[512,352]{0,1:T(8,128)} %fusion.25, bf16[2,1024,352]{1,2,0:T(8,128)(2,1)} %param.20), kind=kOutput, calls=%fused_computation.11 | convolution fusion | flops 740524032 | bytes 4259840 | tf_op jit(solution)/shard_map/dot_general | solution.py:284
  103.5 3.7 %all-to-all-start.2 = ((bf16[8,64,1024]{2,1,0:T(8,128)(2,1)}), bf16[8,64,1024]{2,1,0:T(8,128)(2,1)S(1)}, u32[]{:S(2)}, u32[]{:S(2)}) async-start(bf16[8,64,1024]{2,1,0:T(8,128)(2,1)} %bitcast.60), calls=%async_computation.2 | async-start | bytes 2097152 | tf_op jit(solution)/shard_map/all_to_all | solution.py:229
  107.3 17.3 %all-to-all-done.2 = bf16[8,64,1024]{2,1,0:T(8,128)(2,1)S(1)} async-done(((bf16[8,64,1024]{2,1,0:T(8,128)(2,1)}), bf16[8,64,1024]{2,1,0:T(8,128)(2,1)S(1)}, u32[]{:S(2)}, u32[]{:S(2)}) %all-to-all-start.2) | async-done | bytes 1048608 | tf_op jit(solution)/shard_map/all_to_all | solution.py:229
  125.0 1.1 broadcast_in_dim.90
  126.1 3.6 %all-to-all-start.3 = ((bf16[8,64,1024]{2,1,0:T(8,128)(2,1)}), bf16[8,64,1024]{2,1,0:T(8,128)(2,1)S(1)}, u32[]{:S(2)}, u32[]{:S(2)}) async-start(bf16[8,64,1024]{2,1,0:T(8,128)(2,1)} %broadcast_in_dim.90), calls=%async_computation.3 | async-start | bytes 2097152 | tf_op jit(solution)/shard_map/all_to_all | solution.py:235
  130.7 16.3 %all-to-all-done.3 = bf16[8,64,1024]{2,1,0:T(8,128)(2,1)S(1)} async-done(((bf16[8,64,1024]{2,1,0:T(8,128)(2,1)}), bf16[8,64,1024]{2,1,0:T(8,128)(2,1)S(1)}, u32[]{:S(2)}, u32[]{:S(2)}) %all-to-all-start.3) | async-done | bytes 1048608 | tf_op jit(solution)/shard_map/all_to_all | solution.py:235
  147.0 1.4 convolution_convert_fusion.2
  148.5 1.4 convolution_convert_fusion.4
  152.5 0.8 select_maximum_fusion
  153.3 5.0 %all-to-all-start.4 = ((f32[32,17,128]{2,1,0:T(8,128)}), f32[32,17,128]{2,1,0:T(8,128)S(1)}, u32[]{:S(2)}, u32[]{:S(2)}) async-start(f32[32,17,128]{2,1,0:T(8,128)} %select_maximum_fusion), calls=%async_computation.4 | async-start | bytes 786432 | tf_op jit(solution)/shard_map/all_to_all | solution.py:355
  158.3 13.7 %all-to-all-done.4 = f32[32,17,128]{2,1,0:T(8,128)S(1)} async-done(((f32[32,17,128]{2,1,0:T(8,128)}), f32[32,17,128]{2,1,0:T(8,128)S(1)}, u32[]{:S(2)}, u32[]{:S(2)}) %all-to-all-start.4) | async-done | bytes 278560 | tf_op jit(solution)/shard_map/all_to_all | solution.py:355
  174.0 0.7 broadcast_in_dim.101
  174.7 3.4 %all-to-all-start.5 = ((bf16[8,16,1024]{2,1,0:T(8,128)(2,1)}), bf16[8,16,1024]{2,1,0:T(8,128)(2,1)S(1)}, u32[]{:S(2)}, u32[]{:S(2)}) async-start(bf16[8,16,1024]{2,1,0:T(8,128)(2,1)} %broadcast_in_dim.101), calls=%async_computation.5 | async-start | bytes 524288 | tf_op jit(solution)/shard_map/all_to_all | solution.py:235
  178.2 7.6 %all-to-all-done.5 = bf16[8,16,1024]{2,1,0:T(8,128)(2,1)S(1)} async-done(((bf16[8,16,1024]{2,1,0:T(8,128)(2,1)}), bf16[8,16,1024]{2,1,0:T(8,128)(2,1)S(1)}, u32[]{:S(2)}, u32[]{:S(2)}) %all-to-all-start.5) | async-done | bytes 262176 | tf_op jit(solution)/shard_map/all_to_all | solution.py:235
  185.9 0.8 add_convert_fusion
  186.8 33.7 %all_to_all.36 = bf16[32,16,1024]{2,1,0:T(8,128)(2,1)S(1)} all-to-all(bf16[32,16,1024]{2,1,0:T(8,128)(2,1)S(1)} %broadcast_in_dim.103), channel_id=1, replica_groups=mesh['seq'=32,'head'=8] {'seq'}, dimensions={0} | all-to-all | bytes 2097152 | tf_op jit(solution)/shard_map/all_to_all | solution.py:235
  220.6 1.0 copy.43
  221.5 1.0 copy.44
  (65 shorter events, 6.7 us)
Async XLA Ops:
  0.6 99.3 %copy-start = (bf16[352,1024]{1,0:T(8,128)(2,1)S(1)}, bf16[352,1024]{1,0:T(8,128)(2,1)}, u32[]{:S(2)}) copy-start(bf16[352,1024]{1,0:T(8,128)(2,1)} %param.21) | copy-start | bytes 2162692
  0.6 51.8 %copy-start.4 = (bf16[128,1024]{1,0:T(8,128)(2,1)S(1)}, bf16[128,1024]{1,0:T(8,128)(2,1)}, u32[]{:S(2)}) copy-start(bf16[128,1024]{1,0:T(8,128)(2,1)} %param.18) | copy-start | bytes 786436
  52.4 26.8 %copy-start.1 = (bf16[512,1024]{1,0:T(8,128)(2,1)S(1)}, bf16[512,1024]{1,0:T(8,128)(2,1)}, u32[]{:S(2)}) copy-start(bf16[512,1024]{1,0:T(8,128)(2,1)} %tokens.1) | copy-start | bytes 3145732
  54.8 24.5 %copy-start.5 = (f32[1024]{0:T(1024)S(1)}, f32[1024]{0:T(1024)}, u32[]{:S(2)}) copy-start(f32[1024]{0:T(1024)} %param.19) | copy-start | bytes 12292
  54.8 24.2 %all-to-all-start = ((bf16[8,64,1024]{2,1,0:T(8,128)(2,1)}), bf16[8,64,1024]{2,1,0:T(8,128)(2,1)S(1)}, u32[]{:S(2)}, u32[]{:S(2)}) async-start(bf16[8,64,1024]{2,1,0:T(8,128)(2,1)} %bitcast.1), calls=%async_computation | async-start | bytes 2097152 | tf_op jit(solution)/shard_map/all_to_all | solution.py:229
  79.2 19.3 %copy-start.8 = (bf16[2,1024,352]{1,2,0:T(8,128)(2,1)S(1)}, bf16[2,1024,352]{1,2,0:T(8,128)(2,1)}, u32[]{:S(2)}) copy-start(bf16[2,1024,352]{1,2,0:T(8,128)(2,1)} %param.20) | copy-start | bytes 4325380
  103.5 21.4 %copy-start.6 = (f32[1024]{0:T(1024)S(1)}, f32[1024]{0:T(1024)}, u32[]{:S(2)}) copy-start(f32[1024]{0:T(1024)} %param.22) | copy-start | bytes 12292
  103.5 21.0 %all-to-all-start.2 = ((bf16[8,64,1024]{2,1,0:T(8,128)(2,1)}), bf16[8,64,1024]{2,1,0:T(8,128)(2,1)S(1)}, u32[]{:S(2)}, u32[]{:S(2)}) async-start(bf16[8,64,1024]{2,1,0:T(8,128)(2,1)} %bitcast.60), calls=%async_computation.2 | async-start | bytes 2097152 | tf_op jit(solution)/shard_map/all_to_all | solution.py:229
  124.9 4.8 %copy-start.7 = (s32[32]{0:T(128)S(1)}, s32[32]{0:T(128)}, u32[]{:S(2)}) copy-start(s32[32]{0:T(128)} %lens.1) | copy-start | bytes 388
  124.9 4.9 %copy-start.2 = (bf16[512,1024]{1,0:T(8,128)(2,1)S(1)}, bf16[512,1024]{1,0:T(8,128)(2,1)}, u32[]{:S(2)}) copy-start(bf16[512,1024]{1,0:T(8,128)(2,1)} %param.24) | copy-start | bytes 3145732
  125.0 5.1 %copy-start.9 = (bf16[1024,128]{1,0:T(8,128)(2,1)S(1)}, bf16[1024,128]{1,0:T(8,128)(2,1)}, u32[]{:S(2)}) copy-start(bf16[1024,128]{1,0:T(8,128)(2,1)} %param.27) | copy-start | bytes 786436
  125.0 5.1 %copy-start.10 = (f32[1024]{0:T(1024)S(1)}, f32[1024]{0:T(1024)}, u32[]{:S(2)}) copy-start(f32[1024]{0:T(1024)} %param.26) | copy-start | bytes 12292
  126.1 20.9 %all-to-all-start.3 = ((bf16[8,64,1024]{2,1,0:T(8,128)(2,1)}), bf16[8,64,1024]{2,1,0:T(8,128)(2,1)S(1)}, u32[]{:S(2)}, u32[]{:S(2)}) async-start(bf16[8,64,1024]{2,1,0:T(8,128)(2,1)} %broadcast_in_dim.90), calls=%async_computation.3 | async-start | bytes 2097152 | tf_op jit(solution)/shard_map/all_to_all | solution.py:235
  152.5 21.3 %copy-start.3 = (bf16[128,1024]{1,0:T(8,128)(2,1)S(1)}, bf16[128,1024]{1,0:T(8,128)(2,1)}, u32[]{:S(2)}) copy-start(bf16[128,1024]{1,0:T(8,128)(2,1)} %param.29) | copy-start | bytes 786436
  153.3 24.8 %copy-start.11 = (s32[4]{0:T(128)S(1)}, s32[4]{0:T(128)}, u32[]{:S(2)}) copy-start(s32[4]{0:T(128)} %param.25) | copy-start | bytes 52
  153.3 18.7 %all-to-all-start.4 = ((f32[32,17,128]{2,1,0:T(8,128)}), f32[32,17,128]{2,1,0:T(8,128)S(1)}, u32[]{:S(2)}, u32[]{:S(2)}) async-start(f32[32,17,128]{2,1,0:T(8,128)} %select_maximum_fusion), calls=%async_computation.4 | async-start | bytes 786432 | tf_op jit(solution)/shard_map/all_to_all | solution.py:355
  174.7 11.1 %all-to-all-start.5 = ((bf16[8,16,1024]{2,1,0:T(8,128)(2,1)}), bf16[8,16,1024]{2,1,0:T(8,128)(2,1)S(1)}, u32[]{:S(2)}, u32[]{:S(2)}) async-start(bf16[8,16,1024]{2,1,0:T(8,128)(2,1)} %broadcast_in_dim.101), calls=%async_computation.5 | async-start | bytes 524288 | tf_op jit(solution)/shard_map/all_to_all | solution.py:235

commit v2 on v1

v2 whole, which is shorter than its diff:
```python
import functools
import math

import jax
import jax.numpy as jnp
from jax import lax
from jax.experimental import pallas as pl
from jax.experimental.pallas import tpu as pltpu
from jax.sharding import Mesh
from jax.sharding import PartitionSpec as P

D = 1024
HD = 64
TOK_DEV = 512
TGT_LEN = 128


epsilon = 1e-06
masked_score = -1e30


NZ = 8
SLOTS = 32
UP = (("O", 0, 0), ("O", 0, 1), ("O", 1, 0), ("O", 1, 1), ("O", 2, 0), ("O", 2, 1), ("P", 2, 0), ("O", 3, 0), ("P", 2, 1), ("P", 3, 0))
DOWN = (("O", 0, 1), ("O", 0, 0), ("O", -1, 1), ("O", -1, 0), ("O", -2, 1), ("O", -2, 0), ("P", -2, 1), ("O", -3, 1), ("P", -3, 1), ("P", -2, 0))
SIDE = (("O", 0, 0), ("O", 0, 1), ("O", 1, 0), ("O", -1, 1), ("O", 2, 0), ("O", -2, 1), ("O", 2, 1), ("O", -2, 0), ("O", 1, 1), ("O", -1, 0))
CHIPS = (("O", 0), ("O", 1), ("O", -1), ("P", 0), ("O", 2), ("O", -2), ("O", 3), ("O", -3), ("P", 2), ("P", -2), ("O", 4), ("P", 1), ("P", 3), ("P", -1), ("P", -3), ("P", 4))
STEPS_BEFORE = {1: (0, 1), 3: (2,), 4: (3,), 6: (4, 5), 8: (6,), 9: (7,), 11: (8,), 13: (9,)}
STEPS = 10
WEIGHT_STEPS_BEFORE = {3: (("pass", 0),), 9: (("pass", 1), ("end", 0)), 13: (("pass", 2),)}
FF_DEV = 352
ROWS = 128


def link_plan():
    arrive = {("O", 0, 0): -1, ("O", 0, 1): -1}
    arrivals = []
    for s in range(STEPS):
        new = [(UP[s][0], UP[s][1] + 1, UP[s][2]), (DOWN[s][0], DOWN[s][1] - 1, DOWN[s][2])]
        new.append(("P", SIDE[s][1], SIDE[s][2]))
        arrive.update({item: s for item in new})
        arrivals.append(new)
    waiting = {"up": list(UP), "down": list(DOWN), "side": list(SIDE)}
    sent = {name: 0 for name in waiting}
    sends = []
    for s in range(-1, STEPS):
        now = []
        for name, queue in waiting.items():
            while queue and sent[name] <= s + 2 and arrive[queue[0]] <= s:
                now.append((name, queue.pop(0)))
                sent[name] += 1
        sends.append(now)
    return arrivals, sends


def key_bias(length, rows):
    row = lax.broadcasted_iota(jnp.int32, (rows, 128), 0)
    lane = lax.broadcasted_iota(jnp.int32, (rows, 128), 1)
    return jnp.where((lane == 0) & (row >= length), masked_score, 0.0).astype(jnp.bfloat16)


def spread_queries(q_t):
    rows = lax.broadcasted_iota(jnp.int32, (256, 2 * q_t.shape[1]), 0)
    cols = lax.broadcasted_iota(jnp.int32, (256, 2 * q_t.shape[1]), 1)
    half = q_t.shape[1]
    two = jnp.concatenate([q_t, q_t], axis=1)
    full = jnp.concatenate([two, jnp.zeros_like(two)], axis=0)
    keep = ((rows < HD) & (cols < half)) | ((rows >= HD) & (rows < 2 * HD) & (cols >= half))
    return jnp.where(keep, full, jnp.where(rows == 2 * HD, 1.0, 0.0)).astype(jnp.bfloat16)


def normalised(x, gain):
    return x * lax.rsqrt(jnp.mean(x * x, axis=1, keepdims=True) + epsilon) * gain


def dot32(a, b):
    return jnp.dot(a, b, preferred_element_type=jnp.float32)


def layer_kernel(
    lens,
    tokens,
    gain_attn,
    wqkv,
    gain_ffn,
    gain_final,
    gain_cross,
    wo_hbm,
    wi_hbm,
    wf_hbm,
    targets_hbm,
    wcq_hbm,
    wckv_hbm,
    encoded,
    mixed,
    stats,
    keys,
    values,
    spread,
    acc,
    scores_0,
    scores_1,
    wo,
    wi,
    wf,
    targets,
    wcq,
    wckv,
    wo_all,
    wi_all,
    wf_all,
    ctx,
    ctx_in,
    hidden,
    part,
    out_1,
    in_1,
    out_2,
    in_2,
    enc,
    cross_spread,
    cross_values,
    local_sem,
    send,
    recv,
    recv_w,
    recv_c,
    recv_y,
    recv_e,
):
    me = lax.axis_index("seq")
    core = lax.rem(me, 2)
    y = lax.rem(me // 2, 2)
    z = me // 4
    head = lax.axis_index("head")
    x = lax.rem(head, 4)
    yh = head // 4

    def index(dz, dy, dc):
        z_at = lax.rem(z + dz + NZ, NZ)
        y_at = y if dy == 0 else 1 - y
        c_at = core if dc == 0 else 1 - core
        return z_at * 4 + y_at * 2 + c_at

    places = {
        "up": {"seq": index(1, 0, 0)},
        "down": {"seq": index(-1, 0, 0)},
        "side": {"seq": index(0, 1, 0)},
        "mate": {"seq": index(0, 0, 1)},
        "right": {"head": yh * 4 + lax.rem(x + 1, 4)},
        "left": {"head": yh * 4 + lax.rem(x + 3, 4)},
        "across": {"head": yh * 4 + lax.rem(x + 2, 4)},
        "partner": {"head": (1 - yh) * 4 + x},
    }
    barrier = pltpu.get_barrier_semaphore()
    for place in places.values():
        pl.semaphore_signal(barrier, inc=1, device_id=place, device_id_type=pl.DeviceIdType.MESH)

    loads = {
        "wo": pltpu.make_async_copy(wo_hbm, wo, local_sem.at[0]),
        "wi": pltpu.make_async_copy(wi_hbm, wi, local_sem.at[1]),
        "wf": pltpu.make_async_copy(wf_hbm, wf, local_sem.at[2]),
        "targets": pltpu.make_async_copy(targets_hbm, targets, local_sem.at[3]),
        "wcq": pltpu.make_async_copy(wcq_hbm, wcq, local_sem.at[4]),
        "wckv": pltpu.make_async_copy(wckv_hbm, wckv, local_sem.at[5]),
    }
    for load in loads.values():
        load.start()

    normed = normalised(tokens[...].astype(jnp.float32), gain_attn[...]).astype(jnp.bfloat16)
    keys[me] = dot32(normed, wqkv[1]).astype(jnp.bfloat16)
    values[me] = dot32(normed, wqkv[2]).T.astype(jnp.bfloat16)
    q_t = dot32(normed, wqkv[0]).T
    pl.semaphore_wait(barrier, len(places))

    numbers = iter(range(256))
    started = []

    def remote(source, target, number, arrival, place):
        return pltpu.make_async_remote_copy(
            src_ref=source,
            dst_ref=target,
            send_sem=send.at[number],
            recv_sem=arrival,
            device_id=places[place],
            device_id_type=pl.DeviceIdType.MESH,
        )

    def go(source, target, arrival, place, alike=None):
        number = next(numbers)
        remote(source, target, number, arrival, place).start()
        started.append((number, alike or (lambda: source)))

    def block_copy(kv, slot):
        buffer = (keys, values)[kv]
        return buffer.at[slot], buffer.at[slot], recv.at[kv, slot]

    def wait_block(kv, slot):
        source, target, arrival = block_copy(kv, slot)
        remote(source, target, 0, arrival, "mate").wait_recv()

    def push(kv, slot, place):
        go(*block_copy(kv, slot), place, lambda: (keys, values)[kv].at[0])

    def slot_of(line, d):
        return index(-d, 0 if line == "O" else 1, 0)

    arrivals, sends = link_plan()
    for name, (line, d, kv) in sends[0]:
        push(kv, me, name)
    for kv in range(2):
        push(kv, me, "mate")

    def piece(item, slot, which, c):
        own, gathered = ((wo, wo_all), (wi, wi_all), (wf, wf_all))[item]
        ref = own if slot is None else gathered.at[slot]
        if item == 0:
            first, size = ((0, 64), (0, 32), (32, 32))[which]
            return ref.at[pl.ds(pl.multiple_of(c * 64 + first, 32), size), :]
        if item == 1:
            first, size = ((0, D), (0, D // 2), (D // 2, D // 2))[which]
            return ref.at[c, pl.ds(first, size), :]
        first, size = ((0, 176), (0, 96), (96, 80))[which]
        return ref.at[pl.ds(pl.multiple_of(c * 176 + first, 16), size), :]

    def wait_piece(item, slot, which, k, c):
        ref = piece(item, slot, which, c)
        remote(ref, ref, 0, recv_w.at[item, k], "mate").wait_recv()

    def send_piece(item, slot, slot_there, which, k, to):
        source, target = piece(item, slot, which, core), piece(item, slot_there, which, core)
        go(source, target, recv_w.at[item, k], to, lambda: piece(item, 0, which, 0))

    def weights_start(item):
        loads[("wo", "wi", "wf")[item]].wait()
        for slot, to in ((0, "right"), (1, "left")):
            send_piece(item, None, slot, 0, slot, to)

    def weights_pass(item):
        for slot, half, onward in ((0, 1, "right"), (1, 2, "left")):
            wait_piece(item, slot, 0, slot, core)
            send_piece(item, slot, 2, half, 1 + half, onward)
            send_piece(item, slot, slot, 0, 4 + slot, "mate")

    def weights_end(item):
        for half in (1, 2):
            wait_piece(item, 2, half, 1 + half, core)
            send_piece(item, 2, 2, half, 5 + half, "mate")

    def weights_here(item):
        for slot in (0, 1):
            wait_piece(item, slot, 0, 4 + slot, 1 - core)
        for half in (1, 2):
            wait_piece(item, 2, half, 5 + half, 1 - core)

    for item in range(3):
        weights_start(item)

    spread[...] = spread_queries(q_t * (HD ** (-0.5) * math.log2(math.e)))
    acc[...] = jnp.zeros_like(acc)
    for name in ("targets", "wcq", "wckv"):
        loads[name].wait()
    cross_normed = normalised(targets[...].astype(jnp.float32), gain_cross[...]).astype(jnp.bfloat16)
    cross_spread[...] = spread_queries(
        dot32(cross_normed, wcq[...]).T * (HD ** (-0.5) * math.log2(math.e))
    )

    def step(s):
        for line, d, kv in arrivals[s]:
            slot = slot_of(line, d)
            wait_block(kv, slot)
            push(kv, slot, "mate")
        for name, (line, d, kv) in sends[s + 1]:
            push(kv, slot_of(line, d), name)

    def chip_slot(j, dc):
        dz, dy = jnp.int32(0), jnp.int32(0)
        for k, (line, d) in enumerate(CHIPS):
            dz = jnp.where(j == k, -d, dz)
            dy = jnp.where(j == k, 0 if line == "O" else 1, dy)
        z_at = lax.rem(z + dz + NZ, NZ)
        y_at = lax.rem(y + dy, 2)
        c_at = core if dc == 0 else 1 - core
        return z_at * 4 + y_at * 2 + c_at

    def score(block, length, queries, into):
        rows = jnp.concatenate([block, key_bias(length, TOK_DEV)], axis=1)
        s = dot32(rows, queries[...])
        into[...] = s
        return jnp.max(s, axis=0, keepdims=True)

    def own_score(slot, into):
        return score(keys[slot], lens[slot], spread, into)

    def rest(block, held, old, top):
        p = jnp.exp2(held[...] - top).astype(jnp.bfloat16)
        shrink = jnp.exp2(old - top)
        ones = jnp.ones((16, TOK_DEV), jnp.bfloat16)
        for h in range(2):
            cols = slice(h * TOK_DEV, (h + 1) * TOK_DEV)
            lhs = jnp.concatenate([block[pl.ds(h * HD, HD), :], ones], axis=0)
            acc[h] = acc[h] * shrink[:, cols] + dot32(lhs, p[:, cols])

    def arrived(slot):
        for kv in range(2):
            wait_block(kv, slot)

    start = jnp.full((1, 2 * TOK_DEV), masked_score, jnp.float32)
    mate = index(0, 0, 1)
    top = own_score(me, scores_0)
    arrived(mate)
    following = jnp.maximum(top, own_score(mate, scores_1))
    rest(values.at[me], scores_0, start, top)

    def body(j, carry):
        old, top = carry
        for at in sorted({*STEPS_BEFORE, *WEIGHT_STEPS_BEFORE}):

            @pl.when(j == at)
            def _():
                for s in STEPS_BEFORE.get(at, ()):
                    step(s)
                for what, item in WEIGHT_STEPS_BEFORE.get(at, ()):
                    (weights_pass if what == "pass" else weights_end)(item)

        here, there = chip_slot(j, 0), chip_slot(j, 1)
        later = jnp.maximum(top, own_score(here, scores_0))
        rest(values.at[chip_slot(j - 1, 1)], scores_1, old, top)
        old, top = top, later
        arrived(there)
        later = jnp.maximum(top, own_score(there, scores_1))
        rest(values.at[here], scores_0, old, top)
        return top, later

    old, top = lax.fori_loop(1, len(CHIPS), body, (top, following))
    rest(values.at[chip_slot(jnp.int32(len(CHIPS) - 1), 1)], scores_1, old, top)
    both = jnp.concatenate([acc[h, 0:HD, :] / acc[h, HD : HD + 1, :] for h in range(2)], axis=0)
    ctx[...] = both.T.astype(jnp.bfloat16)

    def ctx_rows(at):
        return ctx.at[pl.ds(pl.multiple_of(lax.rem(at, 4) * ROWS, ROWS), ROWS), :]

    for g, (to, at) in enumerate((("right", x + 1), ("left", x + 3), ("across", x + 2))):
        go(ctx_rows(at), ctx_in.at[g], recv_c.at[g], to)
    weights_here(0)
    weights_end(1)
    total = dot32(ctx_rows(x)[...], wo[...])
    for g in range(3):
        remote(ctx_in.at[g], ctx_in.at[g], 0, recv_c.at[g], "mate").wait_recv()
        total += dot32(ctx_in[g], wo_all[g])
    out_1[...] = total.astype(jnp.bfloat16)
    go(out_1, in_1, recv_y.at[0], "partner")
    total += tokens[pl.ds(pl.multiple_of(x * ROWS, ROWS), ROWS), :].astype(jnp.float32)
    weights_end(2)
    weights_here(1)
    weights_here(2)
    remote(out_1, in_1, 0, recv_y.at[0], "partner").wait_recv()
    total += in_1[...].astype(jnp.float32)
    hidden[...] = total
    ffn_normed = normalised(total, gain_ffn[...]).astype(jnp.bfloat16)
    ffn = jnp.zeros((ROWS, D), jnp.float32)
    for g in range(4):
        gate_w, up_w, down_w = (
            (wi[0], wi[1], wf[...]) if g == 3 else (wi_all[g, 0], wi_all[g, 1], wf_all[g])
        )
        gate = dot32(ffn_normed, gate_w)
        up = dot32(ffn_normed, up_w)
        activated = (jax.nn.gelu(gate, approximate=True) * up).astype(jnp.bfloat16)
        ffn += dot32(activated, down_w)
    part[...] = ffn
    share_rows = ROWS // 2
    mine = pl.ds(pl.multiple_of(yh * share_rows, share_rows), share_rows)
    other = pl.ds(pl.multiple_of((1 - yh) * share_rows, share_rows), share_rows)
    out_2[...] = part[other, :].astype(jnp.bfloat16)
    go(out_2, in_2, recv_y.at[1], "partner")
    final = hidden[mine, :] + part[mine, :]
    remote(out_2, in_2, 0, recv_y.at[1], "partner").wait_recv()
    final += in_2[...].astype(jnp.float32)

    def share(dx, dy):
        return lax.rem(x + dx + 4, 4) * 2 + (yh if dy == 0 else 1 - yh)

    enc[share(0, 0)] = normalised(final, gain_final[...]).astype(jnp.bfloat16)

    def rows_of(at, half):
        if half is None:
            return enc.at[at]
        return enc.at[at, pl.ds(half * 32, 32), :]

    def send_share(at, half, to):
        go(rows_of(at, half), rows_of(at, half), recv_e.at[at, half or 0], to)

    def wait_share(at, half):
        ref = rows_of(at, half)
        remote(ref, ref, 0, recv_e.at[at, half or 0], "mate").wait_recv()

    for to in ("partner", "right", "left"):
        send_share(share(0, 0), None, to)
    for dy in (0, 1):
        if dy:
            wait_share(share(0, 1), None)
            for to in ("right", "left"):
                send_share(share(0, 1), None, to)
        for dx, half, to in ((-1, 0, "right"), (1, 1, "left")):
            wait_share(share(dx, dy), None)
            send_share(share(dx, dy), half, to)
    for dy in (0, 1):
        for half in (0, 1):
            wait_share(share(2, dy), half)

    whole = enc[...].reshape(TOK_DEV, D)
    encoded[...] = whole
    cross_keys = dot32(whole, wckv[0]).astype(jnp.bfloat16)
    cross_values[...] = dot32(whole, wckv[1]).T.astype(jnp.bfloat16)
    acc[...] = jnp.zeros_like(acc)
    cross_top = score(cross_keys, lens[me], cross_spread, scores_0)
    rest(cross_values, scores_0, start, cross_top)
    mixed[...] = jnp.concatenate([acc[h, 0:HD, :] for h in range(2)], axis=0).T
    stats[...] = jnp.concatenate(
        [cross_top[:, :TOK_DEV], cross_top[:, TOK_DEV:], acc[0, HD : HD + 1, :], acc[1, HD : HD + 1, :]]
        + [jnp.zeros((4, TOK_DEV), jnp.float32)],
        axis=0,
    )
    for number, alike in started:
        remote(alike(), alike(), number, recv_y.at[0], "mate").wait_send()


def layer(lens, tokens, gains, wqkv, wo, wi, wf, targets, wcq, wckv):
    vmem = pl.BlockSpec(memory_space=pltpu.VMEM)
    hbm = pl.BlockSpec(memory_space=pl.ANY)
    b16, f32 = jnp.bfloat16, jnp.float32
    gain_attn, gain_ffn, gain_final, gain_cross = (g.reshape(1, D) for g in gains)
    scratch = [
        ((SLOTS, TOK_DEV, 2 * HD), b16),
        ((SLOTS, 2 * HD, TOK_DEV), b16),
        ((256, 2 * TOK_DEV), b16),
        ((2, HD + 16, TOK_DEV), f32),
        ((TOK_DEV, 2 * TOK_DEV), f32),
        ((TOK_DEV, 2 * TOK_DEV), f32),
        (wo.shape, b16),
        (wi.shape, b16),
        (wf.shape, b16),
        (targets.shape, b16),
        (wcq.shape, b16),
        (wckv.shape, b16),
        ((3, *wo.shape), b16),
        ((3, *wi.shape), b16),
        ((3, *wf.shape), b16),
        ((TOK_DEV, 2 * HD), b16),
        ((3, ROWS, 2 * HD), b16),
        ((ROWS, D), f32),
        ((ROWS, D), f32),
        ((ROWS, D), b16),
        ((ROWS, D), b16),
        ((ROWS // 2, D), b16),
        ((ROWS // 2, D), b16),
        ((8, ROWS // 2, D), b16),
        ((256, 2 * TOK_DEV), b16),
        ((2 * HD, TOK_DEV), b16),
    ]
    sems = [(8,), (160,), (2, SLOTS), (3, 8), (4,), (2,), (8, 2)]
    return pl.pallas_call(
        layer_kernel,
        out_shape=(
            jax.ShapeDtypeStruct((TOK_DEV, D), b16),
            jax.ShapeDtypeStruct((TOK_DEV, 2 * HD), f32),
            jax.ShapeDtypeStruct((8, TOK_DEV), f32),
        ),
        in_specs=[pl.BlockSpec(memory_space=pltpu.SMEM)] + [vmem] * 6 + [hbm] * 6,
        out_specs=(vmem, vmem, vmem),
        scratch_shapes=[pltpu.VMEM(*s) for s in scratch] + [pltpu.SemaphoreType.DMA(s) for s in sems],
        compiler_params=pltpu.CompilerParams(
            collective_id=0, has_side_effects=True, vmem_limit_bytes=60 << 20
        ),
        name="layer",
    )(lens, tokens, gain_attn, wqkv, gain_ffn, gain_final, gain_cross, wo, wi, wf, targets, wcq, wckv)


def sent_to_all(x, axis):
    copies = jnp.broadcast_to(x, (lax.axis_size(axis), *x.shape))
    return lax.all_to_all(copies, axis, split_axis=0, concat_axis=0, tiled=True)


def laid_out(blocks, dim):
    shape = list(blocks.shape[1:])
    shape[dim] *= blocks.shape[0]
    return jnp.moveaxis(blocks, 0, dim).reshape(shape)


def gather_directly(x, axis, dim):
    blocks = sent_to_all(x, axis)
    return laid_out(blocks, dim)


def over_copies_2(x, axis):
    everything = sent_to_all(x, axis)
    return jnp.sum(everything.astype(jnp.float32), axis=0)


def spread_heads(per_head):
    return jnp.repeat(per_head.T, HD, axis=1)


def live_within(positions, lengths, span):
    block_ids = jnp.arange(lengths.shape[0], dtype=jnp.int32)
    owners = positions // span
    lengths_here = jnp.sum(
        jnp.where(owners[:, None] == block_ids[None, :], lengths[None, :], 0), axis=1
    )
    return positions % span < lengths_here


def local(
    tokens,
    norm_attn,
    self_qkv,
    self_out,
    norm_ffn,
    ffn_in,
    ffn_out,
    norm_final,
    pad_lengths,
    targets,
    target_lengths,
    norm_cross,
    cross_query,
    cross_kv,
    cross_out,
):
    heads_here = self_qkv.shape[2] // HD
    target_rows = targets.shape[0]
    encoded, mixed, stats = layer(
        pad_lengths,
        tokens,
        (norm_attn, norm_ffn, norm_final, norm_cross),
        self_qkv,
        self_out,
        ffn_in,
        ffn_out,
        targets,
        cross_query,
        cross_kv,
    )
    shares = lax.axis_size("seq")
    share_rows = target_rows // shares
    tops_sums = stats[: 2 * heads_here].reshape(2 * heads_here, shares, share_rows).transpose(1, 0, 2)
    tops_sums = jnp.pad(tops_sums.reshape(shares, 1, -1), ((0, 0), (0, 0), (0, 128 - 2 * heads_here * share_rows)))
    parts = jnp.concatenate([mixed.reshape(shares, share_rows, heads_here * HD), tops_sums], axis=1)
    parts = lax.all_to_all(parts, "seq", split_axis=0, concat_axis=0, tiled=True)
    arrived = parts[:, share_rows, : 2 * heads_here * share_rows].reshape(shares, 2, heads_here, share_rows)
    tops, sums = arrived[:, 0], arrived[:, 1]
    factors = jnp.exp2(tops - jnp.max(tops, axis=0, keepdims=True))
    total = jnp.sum(sums * factors, axis=0)
    spread = jnp.repeat(factors.transpose(0, 2, 1), HD, axis=2)
    mixed_rows = jnp.sum(parts[:, :share_rows] * spread, axis=0)
    first_row = lax.axis_index("seq") * share_rows
    cross_context = (mixed_rows / spread_heads(total)).astype(jnp.bfloat16)
    cross_part = jnp.dot(cross_context, cross_out, preferred_element_type=jnp.float32)
    cross_total = over_copies_2(cross_part.astype(jnp.bfloat16), "head").astype(jnp.float32)
    slots = first_row + jnp.arange(share_rows, dtype=jnp.int32)
    target_live = live_within(slots, target_lengths, TGT_LEN)
    target_share = lax.dynamic_slice_in_dim(targets, first_row, share_rows, 0).astype(jnp.float32)
    decoded_share = (target_share + jnp.where(target_live[:, None], cross_total, 0.0)).astype(
        jnp.bfloat16
    )
    decoded = gather_directly(decoded_share, "seq", 0)
    return (encoded, decoded)


def solution(mesh):
    in_specs = (
        P("seq", None),
        P(),
        P(None, None, "head"),
        P("head", None),
        P(),
        P(None, None, "head"),
        P("head", None),
        P(),
        P(),
        P(),
        P(),
        P(),
        P(None, "head"),
        P(None, None, "head"),
        P("head", None),
    )
    out_specs = (P("seq", None), P())
    return jax.shard_map(local, mesh=mesh, in_specs=in_specs, out_specs=out_specs, check_vma=False)
```

time: 223 us -> 172 us (0.77)
  blocking collectives: 52.6 us -> 0 us
  Pallas kernels: 51.8 us -> 84.8 us
  waiting for transfers between devices: 72.2 us -> 49.3 us
  matrix products: 12.2 us -> 0.15 us
  local copies, waits for them, and re-layouts: 6.3 us -> 8.81 us
    all_to_all x2 -> x0, blocking collectives: 52.6 us -> none  [sent_to_all(): return lax.all_to_all(copies, axis, split_axis=0, concat_axis=0, tiled=True)]
    all_to_all x2 -> x0, waiting for transfers between devices: 34.7 us -> none  [sent_and_summed(): lax.all_to_all(blocks, axis, split_axis=0, concat_axis=0, tiled=True)]
    pallas_call x1, Pallas kernels: 51.8 us -> 84.8 us  [layer(): pl.pallas_call(layer_kernel, out_shape=(jax.ShapeDtypeStruct((TOK_DEV, D)...]
    dot_general x8 -> x0, matrix products: 12.1 us -> none  [the longest x1 3.62 us: feed_forward(): return jnp.dot(activated, ffn_out, preferred_element_type=jnp.float32)]
    all_to_all x2, waiting for transfers between devices: 23.9 us -> 35.5 us  [sent_to_all(): return lax.all_to_all(copies, axis, split_axis=0, concat_axis=0, tiled=True)]
    all_to_all x2 -> x0, starting transfers between devices: 10.5 us -> none  [sent_and_summed(): lax.all_to_all(blocks, axis, split_axis=0, concat_axis=0, tiled=True)]
    all_to_all x1, starting transfers between devices: 4.99 us -> 12.6 us  [local(): lax.all_to_all(parts, 'seq', split_axis=0, concat_axis=0, tiled=True)]
    all_to_all x2, starting transfers between devices: 6.97 us -> 12.1 us  [sent_to_all(): return lax.all_to_all(copies, axis, split_axis=0, concat_axis=0, tiled=True)]
  transfers between devices with their start and end apart: 5 -> 3, of which waited for: 5 -> 3; matrix products, arithmetic and copies ran while one was open for 0% -> 0% of each run, Pallas kernels for 0% -> 0%
where the time goes in v2:
time: 172 us; the launch traced here: 171 us
  Pallas kernels  84.8 us (49%)
  waiting for transfers between devices  49.3 us (29%)
  starting transfers between devices  24.7 us (14%)
  local copies, waits for them, and re-layouts  8.81 us (5%)
  other arithmetic  3.04 us (2%)
    pallas_call x1, Pallas kernels, layer(): pl.pallas_call(layer_kernel, out_shape=(jax.ShapeDtypeStruct((TOK_DEV, D)...  84.8 us
    all_to_all x2, waiting for transfers between devices, sent_to_all(): return lax.all_to_all(copies, axis, split_axis=0, concat_axis=0, tiled=True)  35.5 us
    all_to_all x1, waiting for transfers between devices, local(): lax.all_to_all(parts, 'seq', split_axis=0, concat_axis=0, tiled=True)  13.7 us
    all_to_all x1, starting transfers between devices, local(): lax.all_to_all(parts, 'seq', split_axis=0, concat_axis=0, tiled=True)  12.6 us
    all_to_all x2, starting transfers between devices, sent_to_all(): return lax.all_to_all(copies, axis, split_axis=0, concat_axis=0, tiled=True)  12.1 us
    unnamed x11, local copies, waits for them, and re-layouts  4.73 us
  transfers between devices with their start and end apart: 3, of which 3 were waited for; matrix products, arithmetic and copies ran while one was open for 0% of the time, Pallas kernels for 0%

profile of v2, /device:TPU:1, one launch (start us, length us, event | category | flops | bytes accessed | tf_op | source)
XLA Modules:
  0.0 171.5 jit_solution(9156669106777824674)
XLA Ops:
  0.6 2.6 %copy.32.wi_hbm = bf16[2,1024,352]{2,1,0:T(8,128)(2,1)} copy(bf16[2,1024,352]{1,2,0:T(8,128)(2,1)} %param.20) | data formatting | bytes 2883584 | tf_op args[5]
  3.3 84.8 %layer.1 = (bf16[512,1024]{1,0:T(8,128)(2,1)}, f32[512,128]{1,0:T(8,128)}, f32[8,512]{1,0:T(8,128)}) custom-call(s32[32]{0:T(128)} %lens.1, bf16[512,1024]{1,0:T(8,128)(2,1)} %tokens.1, f32[1,1024]{1,0:T(1,128)} %bitcast.35, bf16[3,1024,128]{2,1,0:T(8,128)(2,1)} %wqkv.1, f32[1,1024]{1,0:T(1,128)} %bitcast.36, f32[1,1024]{1,0:T(1,128)} %bitcast.37, ...), custom_call_target="tpu_custom_call" | custom-call | tf_op jit(solution)/shard_map/layer/pallas_call | solution.py:462
  88.0 0.7 slice.15
  88.8 0.1 reshape.76
  89.0 1.7 %select_maximum_fusion = f32[32,17,128]{2,1,0:T(8,128)} fusion(f32[32,1,64]{2,1,0:T(1,128)S(1)} %copy.39, f32[32,16,128]{2,1,0:T(8,128)} %bitcast.31), kind=kLoop, calls=%fused_computation.2 | loop fusion | flops 208896 | bytes 548864 | tf_op jit(solution)/shard_map/concatenate | solution.py:548
  90.7 12.6 %all-to-all-start = ((f32[32,17,128]{2,1,0:T(8,128)}), f32[32,17,128]{2,1,0:T(8,128)S(1)}, u32[]{:S(2)}, u32[]{:S(2)}) async-start(f32[32,17,128]{2,1,0:T(8,128)} %select_maximum_fusion), calls=%async_computation | async-start | bytes 786432 | tf_op jit(solution)/shard_map/all_to_all | solution.py:549
  103.4 13.7 %all-to-all-done = f32[32,17,128]{2,1,0:T(8,128)S(1)} async-done(((f32[32,17,128]{2,1,0:T(8,128)}), f32[32,17,128]{2,1,0:T(8,128)S(1)}, u32[]{:S(2)}, u32[]{:S(2)}) %all-to-all-start) | async-done | bytes 278560 | tf_op jit(solution)/shard_map/all_to_all | solution.py:549
  117.3 0.2 fusion.2
  117.5 0.1 copy.37
  117.6 0.1 reshape.79
  117.7 0.2 copy.36
  117.9 0.6 broadcast_in_dim.44
  118.5 0.3 reshape.78
  118.9 0.1 convolution_convert_fusion
  119.1 0.7 broadcast_in_dim.46
  119.8 5.4 %all-to-all-start.1 = ((bf16[8,16,1024]{2,1,0:T(8,128)(2,1)}), bf16[8,16,1024]{2,1,0:T(8,128)(2,1)S(1)}, u32[]{:S(2)}, u32[]{:S(2)}) async-start(bf16[8,16,1024]{2,1,0:T(8,128)(2,1)} %broadcast_in_dim.46), calls=%async_computation.1 | async-start | bytes 524288 | tf_op jit(solution)/shard_map/all_to_all | solution.py:481
  125.2 0.1 select_reduce_fusion
  125.3 7.5 %all-to-all-done.1 = bf16[8,16,1024]{2,1,0:T(8,128)(2,1)S(1)} async-done(((bf16[8,16,1024]{2,1,0:T(8,128)(2,1)}), bf16[8,16,1024]{2,1,0:T(8,128)(2,1)S(1)}, u32[]{:S(2)}, u32[]{:S(2)}) %all-to-all-start.1) | async-done | bytes 262176 | tf_op jit(solution)/shard_map/all_to_all | solution.py:481
  132.9 0.8 add_convert_fusion
  133.7 1.1 broadcast_in_dim.48
  134.8 6.7 %all-to-all-start.2 = ((bf16[32,16,1024]{2,1,0:T(8,128)(2,1)}), bf16[32,16,1024]{2,1,0:T(8,128)(2,1)S(1)}, u32[]{:S(2)}, u32[]{:S(2)}) async-start(bf16[32,16,1024]{2,1,0:T(8,128)(2,1)} %broadcast_in_dim.48), calls=%async_computation.2 | async-start | bytes 2097152 | tf_op jit(solution)/shard_map/all_to_all | solution.py:481
  141.5 28.0 %all-to-all-done.2 = bf16[32,16,1024]{2,1,0:T(8,128)(2,1)S(1)} async-done(((bf16[32,16,1024]{2,1,0:T(8,128)(2,1)}), bf16[32,16,1024]{2,1,0:T(8,128)(2,1)S(1)}, u32[]{:S(2)}, u32[]{:S(2)}) %all-to-all-start.2) | async-done | bytes 1048608 | tf_op jit(solution)/shard_map/all_to_all | solution.py:481
  169.5 1.0 copy.42
  170.5 1.0 copy.43
  (16 shorter events, 0.5 us)
Async XLA Ops:
  0.6 118.3 %copy-start = (bf16[128,1024]{1,0:T(8,128)(2,1)S(1)}, bf16[128,1024]{1,0:T(8,128)(2,1)}, u32[]{:S(2)}) copy-start(bf16[128,1024]{1,0:T(8,128)(2,1)} %param.29) | copy-start | bytes 786436
  90.7 26.4 %all-to-all-start = ((f32[32,17,128]{2,1,0:T(8,128)}), f32[32,17,128]{2,1,0:T(8,128)S(1)}, u32[]{:S(2)}, u32[]{:S(2)}) async-start(f32[32,17,128]{2,1,0:T(8,128)} %select_maximum_fusion), calls=%async_computation | async-start | bytes 786432 | tf_op jit(solution)/shard_map/all_to_all | solution.py:549
  117.9 7.3 %copy-start.2 = (s32[4]{0:T(128)S(1)}, s32[4]{0:T(128)}, u32[]{:S(2)}) copy-start(s32[4]{0:T(128)} %param.25) | copy-start | bytes 52
  119.8 13.0 %all-to-all-start.1 = ((bf16[8,16,1024]{2,1,0:T(8,128)(2,1)}), bf16[8,16,1024]{2,1,0:T(8,128)(2,1)S(1)}, u32[]{:S(2)}, u32[]{:S(2)}) async-start(bf16[8,16,1024]{2,1,0:T(8,128)(2,1)} %broadcast_in_dim.46), calls=%async_computation.1 | async-start | bytes 524288 | tf_op jit(solution)/shard_map/all_to_all | solution.py:481
  133.7 35.8 %copy-start.1 = (bf16[512,1024]{1,0:T(8,128)(2,1)S(1)}, bf16[512,1024]{1,0:T(8,128)(2,1)}, u32[]{:S(2)}) copy-start(bf16[512,1024]{1,0:T(8,128)(2,1)} %get-tuple-element.12) | copy-start | bytes 3145732
  134.8 34.7 %all-to-all-start.2 = ((bf16[32,16,1024]{2,1,0:T(8,128)(2,1)}), bf16[32,16,1024]{2,1,0:T(8,128)(2,1)S(1)}, u32[]{:S(2)}, u32[]{:S(2)}) async-start(bf16[32,16,1024]{2,1,0:T(8,128)(2,1)} %broadcast_in_dim.48), calls=%async_computation.2 | async-start | bytes 2097152 | tf_op jit(solution)/shard_map/all_to_all | solution.py:481

commit v3 on v2

--- a/solution.py
+++ b/solution.py
@@ -12,7 +12,6 @@
 D = 1024
 HD = 64
 TOK_DEV = 512
-TGT_LEN = 128
 
 
 epsilon = 1e-06
@@ -27,7 +26,7 @@
 CHIPS = (("O", 0), ("O", 1), ("O", -1), ("P", 0), ("O", 2), ("O", -2), ("O", 3), ("O", -3), ("P", 2), ("P", -2), ("O", 4), ("P", 1), ("P", 3), ("P", -1), ("P", -3), ("P", 4))
 STEPS_BEFORE = {1: (0, 1), 3: (2,), 4: (3,), 6: (4, 5), 8: (6,), 9: (7,), 11: (8,), 13: (9,)}
 STEPS = 10
-WEIGHT_STEPS_BEFORE = {3: (("pass", 0),), 9: (("pass", 1), ("end", 0)), 13: (("pass", 2),)}
+WEIGHT_STEPS_BEFORE = {3: (("pass", 0),), 9: (("pass", 1), ("end", 0)), 13: (("pass", 2),), 15: (("pass", 3),)}
 FF_DEV = 352
 ROWS = 128
 
@@ -91,9 +90,10 @@
     targets_hbm,
     wcq_hbm,
     wckv_hbm,
+    wco_hbm,
+    target_lens,
     encoded,
-    mixed,
-    stats,
+    decoded,
     keys,
     values,
     spread,
@@ -120,6 +120,23 @@
     enc,
     cross_spread,
     cross_values,
+    wco_all,
+    o_all,
+    s_all,
+    o_mate,
+    s_mate,
+    o_half,
+    s_half,
+    o_side,
+    s_side,
+    o_rows,
+    s_rows,
+    o_line,
+    s_line,
+    c_all,
+    sum_out,
+    sum_in,
+    dec,
     local_sem,
     send,
     recv,
@@ -127,6 +144,10 @@
     recv_c,
     recv_y,
     recv_e,
+    recv_m,
+    recv_l,
+    recv_h,
+    recv_d,
 ):
     me = lax.axis_index("seq")
     core = lax.rem(me, 2)
@@ -152,6 +173,9 @@
         "across": {"head": yh * 4 + lax.rem(x + 2, 4)},
         "partner": {"head": (1 - yh) * 4 + x},
     }
+    for dz in range(2, NZ - 1):
+        places[dz] = {"seq": index(dz, 0, 0)}
+    line_place = {1: "up", NZ - 1: "down", **{dz: dz for dz in range(2, NZ - 1)}}
     barrier = pltpu.get_barrier_semaphore()
     for place in places.values():
         pl.semaphore_signal(barrier, inc=1, device_id=place, device_id_type=pl.DeviceIdType.MESH)
@@ -163,6 +187,7 @@
         "targets": pltpu.make_async_copy(targets_hbm, targets, local_sem.at[3]),
         "wcq": pltpu.make_async_copy(wcq_hbm, wcq, local_sem.at[4]),
         "wckv": pltpu.make_async_copy(wckv_hbm, wckv, local_sem.at[5]),
+        "wco": pltpu.make_async_copy(wco_hbm, wco_all.at[3], local_sem.at[6]),
     }
     for load in loads.values():
         load.start()
@@ -212,13 +237,13 @@
         push(kv, me, "mate")
 
     def piece(item, slot, which, c):
-        own, gathered = ((wo, wo_all), (wi, wi_all), (wf, wf_all))[item]
+        own, gathered = ((wo, wo_all), (wi, wi_all), (wf, wf_all), (wco_all.at[3], wco_all))[item]
         ref = own if slot is None else gathered.at[slot]
-        if item == 0:
+        if item in (0, 3):
             first, size = ((0, 64), (0, 32), (32, 32))[which]
             return ref.at[pl.ds(pl.multiple_of(c * 64 + first, 32), size), :]
         if item == 1:
-            first, size = ((0, D), (0, D // 2), (D // 2, D // 2))[which]
+            first, size = ((0, 352), (0, 176), (176, 176))[which]
             return ref.at[c, pl.ds(first, size), :]
         first, size = ((0, 176), (0, 96), (96, 80))[which]
         return ref.at[pl.ds(pl.multiple_of(c * 176 + first, 16), size), :]
@@ -232,7 +257,7 @@
         go(source, target, recv_w.at[item, k], to, lambda: piece(item, 0, which, 0))
 
     def weights_start(item):
-        loads[("wo", "wi", "wf")[item]].wait()
+        loads[("wo", "wi", "wf", "wco")[item]].wait()
         for slot, to in ((0, "right"), (1, "left")):
             send_piece(item, None, slot, 0, slot, to)
 
@@ -253,7 +278,7 @@
         for half in (1, 2):
             wait_piece(item, 2, half, 5 + half, 1 - core)
 
-    for item in range(3):
+    for item in range(4):
         weights_start(item)
 
     spread[...] = spread_queries(q_t * (HD ** (-0.5) * math.log2(math.e)))
@@ -357,15 +382,15 @@
     remote(out_1, in_1, 0, recv_y.at[0], "partner").wait_recv()
     total += in_1[...].astype(jnp.float32)
     hidden[...] = total
-    ffn_normed = normalised(total, gain_ffn[...]).astype(jnp.bfloat16)
+    ffn_normed = normalised(total, gain_ffn[...]).T.astype(jnp.bfloat16)
     ffn = jnp.zeros((ROWS, D), jnp.float32)
     for g in range(4):
         gate_w, up_w, down_w = (
             (wi[0], wi[1], wf[...]) if g == 3 else (wi_all[g, 0], wi_all[g, 1], wf_all[g])
         )
-        gate = dot32(ffn_normed, gate_w)
-        up = dot32(ffn_normed, up_w)
-        activated = (jax.nn.gelu(gate, approximate=True) * up).astype(jnp.bfloat16)
+        gate = dot32(gate_w, ffn_normed)
+        up = dot32(up_w, ffn_normed)
+        activated = (jax.nn.gelu(gate, approximate=True) * up).T.astype(jnp.bfloat16)
         ffn += dot32(activated, down_w)
     part[...] = ffn
     share_rows = ROWS // 2
@@ -373,6 +398,7 @@
     other = pl.ds(pl.multiple_of((1 - yh) * share_rows, share_rows), share_rows)
     out_2[...] = part[other, :].astype(jnp.bfloat16)
     go(out_2, in_2, recv_y.at[1], "partner")
+    weights_end(3)
     final = hidden[mine, :] + part[mine, :]
     remote(out_2, in_2, 0, recv_y.at[1], "partner").wait_recv()
     final += in_2[...].astype(jnp.float32)
@@ -415,19 +441,131 @@
     acc[...] = jnp.zeros_like(acc)
     cross_top = score(cross_keys, lens[me], cross_spread, scores_0)
     rest(cross_values, scores_0, start, cross_top)
-    mixed[...] = jnp.concatenate([acc[h, 0:HD, :] for h in range(2)], axis=0).T
-    stats[...] = jnp.concatenate(
-        [cross_top[:, :TOK_DEV], cross_top[:, TOK_DEV:], acc[0, HD : HD + 1, :], acc[1, HD : HD + 1, :]]
-        + [jnp.zeros((4, TOK_DEV), jnp.float32)],
+    o_all[...] = jnp.concatenate([acc[h, 0:HD, :] / acc[h, HD : HD + 1, :] for h in range(2)], axis=0)
+    s_all[...] = jnp.concatenate(
+        [
+            cross_top[:, h * TOK_DEV : (h + 1) * TOK_DEV] + jnp.log2(acc[h, HD : HD + 1, :])
+            for h in range(2)
+        ]
+        + [jnp.zeros((6, TOK_DEV), jnp.float32)],
         axis=0,
     )
+
+    def joined(first, first_lse, second, second_lse):
+        outs, lses = [], []
+        for h in range(2):
+            one, two = first_lse[h : h + 1], second_lse[h : h + 1]
+            top = jnp.maximum(one, two)
+            one, two = jnp.exp2(one - top), jnp.exp2(two - top)
+            both = one + two
+            dims = slice(h * HD, (h + 1) * HD)
+            outs.append(first[dims] * (one / both) + second[dims] * (two / both))
+            lses.append(top + jnp.log2(both))
+        return jnp.concatenate(outs, axis=0), lses
+
+    def lanes(at, size):
+        return pl.ds(pl.multiple_of(at * size, size), size)
+
+    def wait_for(ref, arrival):
+        remote(ref, ref, 0, arrival, "mate").wait_recv()
+
+    half, quarter = TOK_DEV // 2, TOK_DEV // 4
+    go(o_all.at[:, lanes(1 - core, half)], o_mate, recv_m.at[0], "mate", lambda: o_mate)
+    go(s_all.at[:, lanes(1 - core, half)], s_mate, recv_m.at[1], "mate", lambda: s_mate)
+    wait_for(o_mate, recv_m.at[0])
+    wait_for(s_mate, recv_m.at[1])
+    o, lse = joined(
+        o_all[:, lanes(core, half)], s_all[:, lanes(core, half)], o_mate[...], s_mate[...]
+    )
+    o_half[...] = o.astype(jnp.bfloat16)
+    s_half[...] = jnp.concatenate(lse + [jnp.zeros((6, half), jnp.float32)], axis=0)
+    go(o_half.at[:, lanes(1 - y, quarter)], o_side, recv_m.at[2], "side", lambda: o_side)
+    go(s_half.at[:, lanes(1 - y, quarter)], s_side, recv_m.at[3], "side", lambda: s_side)
+    wait_for(o_side, recv_m.at[2])
+    wait_for(s_side, recv_m.at[3])
+    o, lse = joined(
+        o_half[:, lanes(y, quarter)].astype(jnp.float32),
+        s_half[:, lanes(y, quarter)],
+        o_side[...].astype(jnp.float32),
+        s_side[...],
+    )
+    o_rows[...] = o.T.astype(jnp.bfloat16)
+    s_rows[...] = jnp.concatenate([jnp.broadcast_to(part, (HD, quarter)) for part in lse], axis=0).T
+    few = quarter // NZ
+
+    def few_rows(ref, at):
+        return ref.at[pl.ds(pl.multiple_of(at * few, few), few), :]
+
+    for dz in (4, 3, 5, 2, 6, 1, 7):
+        at = lax.rem(z + dz, NZ)
+        go(few_rows(o_rows, at), o_line.at[z], recv_l.at[0, z], line_place[dz], lambda: o_line.at[0])
+        go(few_rows(s_rows, at), s_line.at[z], recv_l.at[1, z], line_place[dz], lambda: s_line.at[0])
+    o_line[z] = few_rows(o_rows, z)[...]
+    s_line[z] = few_rows(s_rows, z)[...]
+    for dz in range(1, NZ):
+        at = lax.rem(z + dz, NZ)
+        wait_for(o_line.at[at], recv_l.at[0, at])
+        wait_for(s_line.at[at], recv_l.at[1, at])
+    lines = s_line[...]
+    factors = jnp.exp2(lines - jnp.max(lines, axis=0, keepdims=True))
+    c_all[3] = (
+        jnp.sum(o_line[...].astype(jnp.float32) * factors, axis=0) / jnp.sum(factors, axis=0)
+    ).astype(jnp.bfloat16)
+    for g, to in enumerate(("right", "left", "across")):
+        go(c_all.at[3], c_all.at[g], recv_h.at[g], to)
+    weights_here(3)
+    for g in range(3):
+        wait_for(c_all.at[g], recv_h.at[g])
+    total = jnp.zeros((few, D), jnp.float32)
+    for k in range(4):
+        away = lax.rem(k - x + 4, 4)
+        g = jnp.where(away == 0, 3, jnp.where(away == 3, 0, away))
+        total += dot32(c_all[g], wco_all[g])
+    sum_out[...] = total.astype(jnp.bfloat16)
+    go(sum_out, sum_in, recv_h.at[3], "partner")
+
+    def place_of(z_at, dy, dc):
+        y_at = y if dy == 0 else 1 - y
+        c_at = core if dc == 0 else 1 - core
+        return c_at * 16 + y_at * NZ + z_at
+
+    mine = place_of(z, 0, 0)
+    target_rows = targets[pl.ds(pl.multiple_of(mine * few, few), few), :].astype(jnp.float32)
+    slots = z * few + lax.broadcasted_iota(jnp.int32, (few, D), 0)
+    wait_for(sum_in, recv_h.at[3])
+    total = sum_out[...].astype(jnp.float32) + sum_in[...].astype(jnp.float32)
+    live = slots < target_lens[core * 2 + y]
+    dec[mine] = (target_rows + jnp.where(live, total, 0.0)).astype(jnp.bfloat16)
+
+    def hand(at, to):
+        go(dec.at[at], dec.at[at], recv_d.at[at], to, lambda: dec.at[0])
+
+    for dz in (4, 3, 5, 2, 6, 1, 7):
+        hand(mine, line_place[dz])
+    hand(mine, "side")
+    hand(mine, "mate")
+    for dz in (1, 7, 2, 6, 3, 5, 4):
+        at = place_of(lax.rem(z + dz, NZ), 0, 0)
+        wait_for(dec.at[at], recv_d.at[at])
+        hand(at, "side")
+        hand(at, "mate")
+    for dz in (0, 1, 7, 2, 6, 3, 5, 4):
+        at = place_of(lax.rem(z + dz, NZ), 1, 0)
+        wait_for(dec.at[at], recv_d.at[at])
+        hand(at, "mate")
+    for dz in range(NZ):
+        for dy in (0, 1):
+            at = place_of(lax.rem(z + dz, NZ), dy, 1)
+            wait_for(dec.at[at], recv_d.at[at])
+    decoded[...] = dec[...].reshape(TOK_DEV, D)
     for number, alike in started:
         remote(alike(), alike(), number, recv_y.at[0], "mate").wait_send()
 
 
-def layer(lens, tokens, gains, wqkv, wo, wi, wf, targets, wcq, wckv):
+def layer(lens, tokens, gains, wqkv, wo, wi, wf, targets, wcq, wckv, wco, target_lens):
     vmem = pl.BlockSpec(memory_space=pltpu.VMEM)
     hbm = pl.BlockSpec(memory_space=pl.ANY)
+    smem = pl.BlockSpec(memory_space=pltpu.SMEM)
     b16, f32 = jnp.bfloat16, jnp.float32
     gain_attn, gain_ffn, gain_final, gain_cross = (g.reshape(1, D) for g in gains)
     scratch = [
@@ -457,57 +595,39 @@
         ((8, ROWS // 2, D), b16),
         ((256, 2 * TOK_DEV), b16),
         ((2 * HD, TOK_DEV), b16),
+        ((4, *wco.shape), b16),
+        ((2 * HD, TOK_DEV), f32),
+        ((8, TOK_DEV), f32),
+        ((2 * HD, TOK_DEV // 2), f32),
+        ((8, TOK_DEV // 2), f32),
+        ((2 * HD, TOK_DEV // 2), b16),
+        ((8, TOK_DEV // 2), f32),
+        ((2 * HD, TOK_DEV // 4), b16),
+        ((8, TOK_DEV // 4), f32),
+        ((TOK_DEV // 4, 2 * HD), b16),
+        ((TOK_DEV // 4, 2 * HD), f32),
+        ((NZ, 16, 2 * HD), b16),
+        ((NZ, 16, 2 * HD), f32),
+        ((4, 16, 2 * HD), b16),
+        ((16, D), b16),
+        ((16, D), b16),
+        ((SLOTS, 16, D), b16),
     ]
-    sems = [(8,), (160,), (2, SLOTS), (3, 8), (4,), (2,), (8, 2)]
+    sems = [(8,), (200,), (2, SLOTS), (4, 8), (4,), (2,), (8, 2), (4,), (2, NZ), (4,), (SLOTS,)]
     return pl.pallas_call(
         layer_kernel,
         out_shape=(
             jax.ShapeDtypeStruct((TOK_DEV, D), b16),
-            jax.ShapeDtypeStruct((TOK_DEV, 2 * HD), f32),
-            jax.ShapeDtypeStruct((8, TOK_DEV), f32),
+            jax.ShapeDtypeStruct(targets.shape, b16),
         ),
-        in_specs=[pl.BlockSpec(memory_space=pltpu.SMEM)] + [vmem] * 6 + [hbm] * 6,
-        out_specs=(vmem, vmem, vmem),
+        in_specs=[smem] + [vmem] * 6 + [hbm] * 7 + [smem],
+        out_specs=(vmem, vmem),
         scratch_shapes=[pltpu.VMEM(*s) for s in scratch] + [pltpu.SemaphoreType.DMA(s) for s in sems],
         compiler_params=pltpu.CompilerParams(
             collective_id=0, has_side_effects=True, vmem_limit_bytes=60 << 20
         ),
         name="layer",
-    )(lens, tokens, gain_attn, wqkv, gain_ffn, gain_final, gain_cross, wo, wi, wf, targets, wcq, wckv)
-
-
-def sent_to_all(x, axis):
-    copies = jnp.broadcast_to(x, (lax.axis_size(axis), *x.shape))
-    return lax.all_to_all(copies, axis, split_axis=0, concat_axis=0, tiled=True)
-
-
-def laid_out(blocks, dim):
-    shape = list(blocks.shape[1:])
-    shape[dim] *= blocks.shape[0]
-    return jnp.moveaxis(blocks, 0, dim).reshape(shape)
-
-
-def gather_directly(x, axis, dim):
-    blocks = sent_to_all(x, axis)
-    return laid_out(blocks, dim)
-
-
-def over_copies_2(x, axis):
-    everything = sent_to_all(x, axis)
-    return jnp.sum(everything.astype(jnp.float32), axis=0)
-
-
-def spread_heads(per_head):
-    return jnp.repeat(per_head.T, HD, axis=1)
-
-
-def live_within(positions, lengths, span):
-    block_ids = jnp.arange(lengths.shape[0], dtype=jnp.int32)
-    owners = positions // span
-    lengths_here = jnp.sum(
-        jnp.where(owners[:, None] == block_ids[None, :], lengths[None, :], 0), axis=1
-    )
-    return positions % span < lengths_here
+    )(lens, tokens, gain_attn, wqkv, gain_ffn, gain_final, gain_cross, wo, wi, wf, targets, wcq, wckv, wco, target_lens)
 
 
 def local(
@@ -527,44 +647,20 @@
     cross_kv,
     cross_out,
 ):
-    heads_here = self_qkv.shape[2] // HD
-    target_rows = targets.shape[0]
-    encoded, mixed, stats = layer(
+    return layer(
         pad_lengths,
         tokens,
         (norm_attn, norm_ffn, norm_final, norm_cross),
         self_qkv,
         self_out,
-        ffn_in,
+        jnp.swapaxes(ffn_in, 1, 2),
         ffn_out,
         targets,
         cross_query,
         cross_kv,
+        cross_out,
+        target_lengths,
     )
-    shares = lax.axis_size("seq")
-    share_rows = target_rows // shares
-    tops_sums = stats[: 2 * heads_here].reshape(2 * heads_here, shares, share_rows).transpose(1, 0, 2)
-    tops_sums = jnp.pad(tops_sums.reshape(shares, 1, -1), ((0, 0), (0, 0), (0, 128 - 2 * heads_here * share_rows)))
-    parts = jnp.concatenate([mixed.reshape(shares, share_rows, heads_here * HD), tops_sums], axis=1)
-    parts = lax.all_to_all(parts, "seq", split_axis=0, concat_axis=0, tiled=True)
-    arrived = parts[:, share_rows, : 2 * heads_here * share_rows].reshape(shares, 2, heads_here, share_rows)
-    tops, sums = arrived[:, 0], arrived[:, 1]
-    factors = jnp.exp2(tops - jnp.max(tops, axis=0, keepdims=True))
-    total = jnp.sum(sums * factors, axis=0)
-    spread = jnp.repeat(factors.transpose(0, 2, 1), HD, axis=2)
-    mixed_rows = jnp.sum(parts[:, :share_rows] * spread, axis=0)
-    first_row = lax.axis_index("seq") * share_rows
-    cross_context = (mixed_rows / spread_heads(total)).astype(jnp.bfloat16)
-    cross_part = jnp.dot(cross_context, cross_out, preferred_element_type=jnp.float32)
-    cross_total = over_copies_2(cross_part.astype(jnp.bfloat16), "head").astype(jnp.float32)
-    slots = first_row + jnp.arange(share_rows, dtype=jnp.int32)
-    target_live = live_within(slots, target_lengths, TGT_LEN)
-    target_share = lax.dynamic_slice_in_dim(targets, first_row, share_rows, 0).astype(jnp.float32)
-    decoded_share = (target_share + jnp.where(target_live[:, None], cross_total, 0.0)).astype(
-        jnp.bfloat16
-    )
-    decoded = gather_directly(decoded_share, "seq", 0)
-    return (encoded, decoded)
 
 
 def solution(mesh):

time: 172 us -> 132 us (0.77)
  waiting for transfers between devices: 49.3 us -> 0 us
  Pallas kernels: 84.8 us -> 127 us
  starting transfers between devices: 24.7 us -> 0 us
  local copies, waits for them, and re-layouts: 8.81 us -> 3.32 us
  other arithmetic: 3.04 us -> 0 us
    all_to_all x3 -> x0, waiting for transfers between devices: 49.3 us -> none  [the longest x2 35.5 us: sent_to_all(): return lax.all_to_all(copies, axis, split_axis=0, concat_axis=0, tiled=True)]
    pallas_call x1, Pallas kernels: 84.8 us -> 127 us  [layer(): pl.pallas_call(layer_kernel, out_shape=(jax.ShapeDtypeStruct((TOK_DEV, D)...]
    all_to_all x3 -> x0, starting transfers between devices: 24.7 us -> none  [the longest x1 12.6 us: local(): lax.all_to_all(parts, 'seq', split_axis=0, concat_axis=0, tiled=True)]
    broadcast_in_dim x4 -> x0, local copies, waits for them, and re-layouts: 2.51 us -> none  [the longest x2 1.83 us: sent_to_all(): copies = jnp.broadcast_to(x, (lax.axis_size(axis), *x.shape))]
    concatenate x1 -> x0, other arithmetic: 1.74 us -> none  [local(): jnp.concatenate([mixed.reshape(shares, share_rows, heads_here * HD), tops...]
    unnamed x11 -> x4, local copies, waits for them, and re-layouts: 4.73 us -> 3.32 us
  transfers between devices with their start and end apart: 3 -> 0, of which waited for: 3 -> 0; matrix products, arithmetic and copies ran while one was open for 0% -> 0% of each run, Pallas kernels for 0% -> 0%
where the time goes in v3:
time: 132 us; the launch traced here: 131 us
  Pallas kernels  127 us (96%)
  local copies, waits for them, and re-layouts  3.32 us (3%)
    pallas_call x1, Pallas kernels, layer(): pl.pallas_call(layer_kernel, out_shape=(jax.ShapeDtypeStruct((TOK_DEV, D)...  127 us
    unnamed x4, local copies, waits for them, and re-layouts  3.32 us

profile of v3, /device:TPU:1, one launch (start us, length us, event | category | flops | bytes accessed | tf_op | source)
XLA Modules:
  0.0 131.4 jit_solution(5680002986743614714)
XLA Ops:
  0.6 127.5 %layer.1 = (bf16[512,1024]{1,0:T(8,128)(2,1)}, bf16[512,1024]{1,0:T(8,128)(2,1)}) custom-call(s32[32]{0:T(128)} %lens.1, bf16[512,1024]{1,0:T(8,128)(2,1)} %tokens.1, f32[1,1024]{1,0:T(1,128)} %bitcast.6, bf16[3,1024,128]{2,1,0:T(8,128)(2,1)} %wqkv.1, f32[1,1024]{1,0:T(1,128)} %bitcast.7, f32[1,1024]{1,0:T(1,128)} %bitcast.8, f32[1,1024]{1,0:T(1,128)} %bitcast.9, ...), custom_call_target="tpu_custom_call" | custom-call | tf_op jit(solution)/shard_map/layer/pallas_call | solution.py:617
  128.1 0.0 copy-start
  128.1 2.4 %copy.19 = bf16[512,1024]{1,0:T(8,128)(2,1)} copy(bf16[512,1024]{1,0:T(8,128)(2,1)} %get-tuple-element.4) | data formatting | bytes 2097152
  130.5 0.0 copy-done
  130.5 1.0 copy.20
Async XLA Ops:
  128.1 2.4 %copy-start = (bf16[512,1024]{1,0:T(8,128)(2,1)S(1)}, bf16[512,1024]{1,0:T(8,128)(2,1)}, u32[]{:S(2)}) copy-start(bf16[512,1024]{1,0:T(8,128)(2,1)} %get-tuple-element.5) | copy-start | bytes 3145732

commit v4 on v3

--- a/solution.py
+++ b/solution.py
@@ -23,12 +23,10 @@
 UP = (("O", 0, 0), ("O", 0, 1), ("O", 1, 0), ("O", 1, 1), ("O", 2, 0), ("O", 2, 1), ("P", 2, 0), ("O", 3, 0), ("P", 2, 1), ("P", 3, 0))
 DOWN = (("O", 0, 1), ("O", 0, 0), ("O", -1, 1), ("O", -1, 0), ("O", -2, 1), ("O", -2, 0), ("P", -2, 1), ("O", -3, 1), ("P", -3, 1), ("P", -2, 0))
 SIDE = (("O", 0, 0), ("O", 0, 1), ("O", 1, 0), ("O", -1, 1), ("O", 2, 0), ("O", -2, 1), ("O", 2, 1), ("O", -2, 0), ("O", 1, 1), ("O", -1, 0))
-CHIPS = (("O", 0), ("O", 1), ("O", -1), ("P", 0), ("O", 2), ("O", -2), ("O", 3), ("O", -3), ("P", 2), ("P", -2), ("O", 4), ("P", 1), ("P", 3), ("P", -1), ("P", -3), ("P", 4))
-STEPS_BEFORE = {1: (0, 1), 3: (2,), 4: (3,), 6: (4, 5), 8: (6,), 9: (7,), 11: (8,), 13: (9,)}
 STEPS = 10
-WEIGHT_STEPS_BEFORE = {3: (("pass", 0),), 9: (("pass", 1), ("end", 0)), 13: (("pass", 2),), 15: (("pass", 3),)}
 FF_DEV = 352
 ROWS = 128
+UNIT = 256
 
 
 def link_plan():
@@ -52,8 +50,19 @@
     return arrivals, sends
 
 
-def key_bias(length, rows):
-    row = lax.broadcasted_iota(jnp.int32, (rows, 128), 0)
+ARRIVALS, SENDS = link_plan()
+UNITS = (("O", 0, 0), ("O", 0, 1), *(item for step in ARRIVALS for item in step))
+STEP_AT = {2: (0,), **{3 * s: (s,) for s in range(1, STEPS)}}
+WEIGHT_STEP_AT = {9: (("pass", 0),), 21: (("pass", 2),), 28: (("pass", 1), ("end", 0))}
+UNIT_CODES = tuple((4 - d) * 4 + (line == "P") * 2 + half for line, d, half in UNITS)
+CODE_WORDS = tuple(
+    sum(code << (8 * k) for k, code in enumerate(UNIT_CODES[first : first + 3]))
+    for first in range(0, len(UNITS), 3)
+)
+
+
+def key_bias(length, first, rows):
+    row = first + lax.broadcasted_iota(jnp.int32, (rows, 128), 0)
     lane = lax.broadcasted_iota(jnp.int32, (rows, 128), 1)
     return jnp.where((lane == 0) & (row >= length), masked_score, 0.0).astype(jnp.bfloat16)
 
@@ -78,12 +87,12 @@
 
 def layer_kernel(
     lens,
-    tokens,
-    gain_attn,
-    wqkv,
-    gain_ffn,
-    gain_final,
-    gain_cross,
+    tokens_hbm,
+    gain_attn_hbm,
+    wqkv_hbm,
+    gain_ffn_hbm,
+    gain_final_hbm,
+    gain_cross_hbm,
     wo_hbm,
     wi_hbm,
     wf_hbm,
@@ -92,10 +101,15 @@
     wckv_hbm,
     wco_hbm,
     target_lens,
-    encoded,
-    decoded,
-    keys,
-    values,
+    enc,
+    dec,
+    tokens,
+    gain_attn,
+    wqkv,
+    gain_ffn,
+    gain_final,
+    gain_cross,
+    kv,
     spread,
     acc,
     scores_0,
@@ -117,7 +131,6 @@
     in_1,
     out_2,
     in_2,
-    enc,
     cross_spread,
     cross_values,
     wco_all,
@@ -136,7 +149,6 @@
     c_all,
     sum_out,
     sum_in,
-    dec,
     local_sem,
     send,
     recv,
@@ -180,26 +192,40 @@
     for place in places.values():
         pl.semaphore_signal(barrier, inc=1, device_id=place, device_id_type=pl.DeviceIdType.MESH)
 
+    pairs = {
+        "tokens": (tokens_hbm, tokens),
+        "wqkv": (wqkv_hbm, wqkv),
+        "gain_attn": (gain_attn_hbm, gain_attn),
+        "wo": (wo_hbm, wo),
+        "wi": (wi_hbm, wi),
+        "wf": (wf_hbm, wf),
+        "wco": (wco_hbm, wco_all.at[3]),
+        "targets": (targets_hbm, targets),
+        "wcq": (wcq_hbm, wcq),
+        "gain_cross": (gain_cross_hbm, gain_cross),
+        "gain_ffn": (gain_ffn_hbm, gain_ffn),
+        "gain_final": (gain_final_hbm, gain_final),
+        "wckv": (wckv_hbm, wckv),
+    }
     loads = {
-        "wo": pltpu.make_async_copy(wo_hbm, wo, local_sem.at[0]),
-        "wi": pltpu.make_async_copy(wi_hbm, wi, local_sem.at[1]),
-        "wf": pltpu.make_async_copy(wf_hbm, wf, local_sem.at[2]),
-        "targets": pltpu.make_async_copy(targets_hbm, targets, local_sem.at[3]),
-        "wcq": pltpu.make_async_copy(wcq_hbm, wcq, local_sem.at[4]),
-        "wckv": pltpu.make_async_copy(wckv_hbm, wckv, local_sem.at[5]),
-        "wco": pltpu.make_async_copy(wco_hbm, wco_all.at[3], local_sem.at[6]),
+        name: pltpu.make_async_copy(source, target, local_sem.at[k])
+        for k, (name, (source, target)) in enumerate(pairs.items())
     }
     for load in loads.values():
         load.start()
 
+    for name in ("tokens", "gain_attn", "wqkv"):
+        loads[name].wait()
     normed = normalised(tokens[...].astype(jnp.float32), gain_attn[...]).astype(jnp.bfloat16)
-    keys[me] = dot32(normed, wqkv[1]).astype(jnp.bfloat16)
-    values[me] = dot32(normed, wqkv[2]).T.astype(jnp.bfloat16)
+    own_keys = dot32(normed, wqkv[1]).astype(jnp.bfloat16)
+    own_values = dot32(normed, wqkv[2]).T.astype(jnp.bfloat16)
+    for half in range(2):
+        kv[me, half, 0:UNIT, :] = own_keys[half * UNIT : (half + 1) * UNIT, :]
+        for k in range(2):
+            first = half * UNIT + k * 128
+            kv[me, half, pl.ds(UNIT + k * 128, 128), :] = own_values[:, first : first + 128]
     q_t = dot32(normed, wqkv[0]).T
     pl.semaphore_wait(barrier, len(places))
-
-    numbers = iter(range(256))
-    started = []
 
     def remote(source, target, number, arrival, place):
         return pltpu.make_async_remote_copy(
@@ -211,30 +237,24 @@
             device_id_type=pl.DeviceIdType.MESH,
         )
 
-    def go(source, target, arrival, place, alike=None):
-        number = next(numbers)
-        remote(source, target, number, arrival, place).start()
-        started.append((number, alike or (lambda: source)))
-
-    def block_copy(kv, slot):
-        buffer = (keys, values)[kv]
-        return buffer.at[slot], buffer.at[slot], recv.at[kv, slot]
-
-    def wait_block(kv, slot):
-        source, target, arrival = block_copy(kv, slot)
-        remote(source, target, 0, arrival, "mate").wait_recv()
-
-    def push(kv, slot, place):
-        go(*block_copy(kv, slot), place, lambda: (keys, values)[kv].at[0])
+    def go(source, target, arrival, place, group):
+        remote(source, target, group, arrival, place).start()
+
+    def wait_block(half, slot):
+        ref = kv.at[slot, half]
+        remote(ref, ref, 0, recv.at[half, slot], "mate").wait_recv()
+
+    def push(half, slot, place):
+        ref = kv.at[slot, half]
+        go(ref, ref, recv.at[half, slot], place, 4)
 
     def slot_of(line, d):
         return index(-d, 0 if line == "O" else 1, 0)
 
-    arrivals, sends = link_plan()
-    for name, (line, d, kv) in sends[0]:
-        push(kv, me, name)
-    for kv in range(2):
-        push(kv, me, "mate")
+    for name, (line, d, half) in SENDS[0]:
+        push(half, me, name)
+    for half in range(2):
+        push(half, me, "mate")
 
     def piece(item, slot, which, c):
         own, gathered = ((wo, wo_all), (wi, wi_all), (wf, wf_all), (wco_all.at[3], wco_all))[item]
@@ -254,7 +274,7 @@
 
     def send_piece(item, slot, slot_there, which, k, to):
         source, target = piece(item, slot, which, core), piece(item, slot_there, which, core)
-        go(source, target, recv_w.at[item, k], to, lambda: piece(item, 0, which, 0))
+        go(source, target, recv_w.at[item, k], to, item)
 
     def weights_start(item):
         loads[("wo", "wi", "wf", "wco")[item]].wait()
@@ -278,12 +298,12 @@
         for half in (1, 2):
             wait_piece(item, 2, half, 5 + half, 1 - core)
 
-    for item in range(4):
+    for item in range(3):
         weights_start(item)
 
     spread[...] = spread_queries(q_t * (HD ** (-0.5) * math.log2(math.e)))
     acc[...] = jnp.zeros_like(acc)
-    for name in ("targets", "wcq", "wckv"):
+    for name in ("targets", "wcq", "gain_cross", "gain_ffn", "gain_final", "wckv"):
         loads[name].wait()
     cross_normed = normalised(targets[...].astype(jnp.float32), gain_cross[...]).astype(jnp.bfloat16)
     cross_spread[...] = spread_queries(
@@ -291,74 +311,95 @@
     )
 
     def step(s):
-        for line, d, kv in arrivals[s]:
+        for line, d, half in ARRIVALS[s]:
             slot = slot_of(line, d)
-            wait_block(kv, slot)
-            push(kv, slot, "mate")
-        for name, (line, d, kv) in sends[s + 1]:
-            push(kv, slot_of(line, d), name)
-
-    def chip_slot(j, dc):
-        dz, dy = jnp.int32(0), jnp.int32(0)
-        for k, (line, d) in enumerate(CHIPS):
-            dz = jnp.where(j == k, -d, dz)
-            dy = jnp.where(j == k, 0 if line == "O" else 1, dy)
-        z_at = lax.rem(z + dz + NZ, NZ)
-        y_at = lax.rem(y + dy, 2)
-        c_at = core if dc == 0 else 1 - core
-        return z_at * 4 + y_at * 2 + c_at
-
-    def score(block, length, queries, into):
-        rows = jnp.concatenate([block, key_bias(length, TOK_DEV)], axis=1)
-        s = dot32(rows, queries[...])
+            wait_block(half, slot)
+            push(half, slot, "mate")
+        for name, (line, d, half) in SENDS[s + 1]:
+            push(half, slot_of(line, d), name)
+
+    def unit_of(u):
+        third = u // 3
+        word = jnp.int32(CODE_WORDS[0])
+        for k in range(1, len(CODE_WORDS)):
+            word = jnp.where(third == k, CODE_WORDS[k], word)
+        code = lax.rem(lax.shift_right_logical(word, 8 * (u - 3 * third)), 256)
+        half = lax.rem(code, 2)
+        chip = lax.rem(z + code // 4 + 4, NZ) * 4 + lax.rem(y + code // 2, 2) * 2
+        return chip + core, chip + 1 - core, half
+
+    def score(block, bias, queries, into):
+        s = dot32(jnp.concatenate([block, bias], axis=1), queries[...])
         into[...] = s
         return jnp.max(s, axis=0, keepdims=True)
 
-    def own_score(slot, into):
-        return score(keys[slot], lens[slot], spread, into)
-
-    def rest(block, held, old, top):
+    def unit_score(unit, into):
+        here, there, half = unit
+        wait_block(half, there)
+        block = jnp.concatenate([kv[here, half, 0:UNIT, :], kv[there, half, 0:UNIT, :]], axis=0)
+        bias = jnp.concatenate(
+            [key_bias(lens[slot], half * UNIT, UNIT) for slot in (here, there)], axis=0
+        )
+        return score(block, bias, spread, into)
+
+    def rest(rows_of_head, held, old, top):
         p = jnp.exp2(held[...] - top).astype(jnp.bfloat16)
         shrink = jnp.exp2(old - top)
         ones = jnp.ones((16, TOK_DEV), jnp.bfloat16)
         for h in range(2):
             cols = slice(h * TOK_DEV, (h + 1) * TOK_DEV)
-            lhs = jnp.concatenate([block[pl.ds(h * HD, HD), :], ones], axis=0)
+            lhs = jnp.concatenate([rows_of_head(h), ones], axis=0)
             acc[h] = acc[h] * shrink[:, cols] + dot32(lhs, p[:, cols])
 
-    def arrived(slot):
-        for kv in range(2):
-            wait_block(kv, slot)
+    def unit_rest(unit, held, old, top):
+        here, there, half = unit
+
+        def rows_of_head(h):
+            return jnp.concatenate(
+                [
+                    kv[slot, half, pl.ds(UNIT + k * 128 + h * HD, HD), :]
+                    for slot in (here, there)
+                    for k in range(2)
+                ],
+                axis=1,
+            )
+
+        rest(rows_of_head, held, old, top)
+
+    def handle(u, odd):
+        for at in sorted({*STEP_AT, *WEIGHT_STEP_AT}):
+            if at % 2 != odd:
+                continue
+
+            @pl.when(u == at)
+            def _():
+                for s in STEP_AT.get(at, ()):
+                    step(s)
+                for what, item in WEIGHT_STEP_AT.get(at, ()):
+                    (weights_pass if what == "pass" else weights_end)(item)
 
     start = jnp.full((1, 2 * TOK_DEV), masked_score, jnp.float32)
-    mate = index(0, 0, 1)
-    top = own_score(me, scores_0)
-    arrived(mate)
-    following = jnp.maximum(top, own_score(mate, scores_1))
-    rest(values.at[me], scores_0, start, top)
+    zero = jnp.int32(0)
+    first, second = unit_of(zero), unit_of(zero + 1)
+    top = unit_score(first, scores_0)
+    following = jnp.maximum(top, unit_score(second, scores_1))
+    unit_rest(first, scores_0, start, top)
 
     def body(j, carry):
-        old, top = carry
-        for at in sorted({*STEPS_BEFORE, *WEIGHT_STEPS_BEFORE}):
-
-            @pl.when(j == at)
-            def _():
-                for s in STEPS_BEFORE.get(at, ()):
-                    step(s)
-                for what, item in WEIGHT_STEPS_BEFORE.get(at, ()):
-                    (weights_pass if what == "pass" else weights_end)(item)
-
-        here, there = chip_slot(j, 0), chip_slot(j, 1)
-        later = jnp.maximum(top, own_score(here, scores_0))
-        rest(values.at[chip_slot(j - 1, 1)], scores_1, old, top)
+        old, top, before = carry
+        u = 2 * j
+        here, after = unit_of(u), unit_of(u + 1)
+        handle(u, 0)
+        later = jnp.maximum(top, unit_score(here, scores_0))
+        unit_rest(before, scores_1, old, top)
         old, top = top, later
-        arrived(there)
-        later = jnp.maximum(top, own_score(there, scores_1))
-        rest(values.at[here], scores_0, old, top)
-        return top, later
-
-    old, top = lax.fori_loop(1, len(CHIPS), body, (top, following))
-    rest(values.at[chip_slot(jnp.int32(len(CHIPS) - 1), 1)], scores_1, old, top)
+        handle(u + 1, 1)
+        later = jnp.maximum(top, unit_score(after, scores_1))
+        unit_rest(here, scores_0, old, top)
+        return top, later, after
+
+    old, top, last = lax.fori_loop(1, len(UNITS) // 2, body, (top, following, second))
+    unit_rest(last, scores_1, old, top)
     both = jnp.concatenate([acc[h, 0:HD, :] / acc[h, HD : HD + 1, :] for h in range(2)], axis=0)
     ctx[...] = both.T.astype(jnp.bfloat16)
 
@@ -366,7 +407,8 @@
         return ctx.at[pl.ds(pl.multiple_of(lax.rem(at, 4) * ROWS, ROWS), ROWS), :]
 
     for g, (to, at) in enumerate((("right", x + 1), ("left", x + 3), ("across", x + 2))):
-        go(ctx_rows(at), ctx_in.at[g], recv_c.at[g], to)
+        go(ctx_rows(at), ctx_in.at[g], recv_c.at[g], to, 5)
+    weights_start(3)
     weights_here(0)
     weights_end(1)
     total = dot32(ctx_rows(x)[...], wo[...])
@@ -374,7 +416,7 @@
         remote(ctx_in.at[g], ctx_in.at[g], 0, recv_c.at[g], "mate").wait_recv()
         total += dot32(ctx_in[g], wo_all[g])
     out_1[...] = total.astype(jnp.bfloat16)
-    go(out_1, in_1, recv_y.at[0], "partner")
+    go(out_1, in_1, recv_y.at[0], "partner", 6)
     total += tokens[pl.ds(pl.multiple_of(x * ROWS, ROWS), ROWS), :].astype(jnp.float32)
     weights_end(2)
     weights_here(1)
@@ -397,8 +439,8 @@
     mine = pl.ds(pl.multiple_of(yh * share_rows, share_rows), share_rows)
     other = pl.ds(pl.multiple_of((1 - yh) * share_rows, share_rows), share_rows)
     out_2[...] = part[other, :].astype(jnp.bfloat16)
-    go(out_2, in_2, recv_y.at[1], "partner")
-    weights_end(3)
+    go(out_2, in_2, recv_y.at[1], "partner", 7)
+    weights_pass(3)
     final = hidden[mine, :] + part[mine, :]
     remote(out_2, in_2, 0, recv_y.at[1], "partner").wait_recv()
     final += in_2[...].astype(jnp.float32)
@@ -414,7 +456,7 @@
         return enc.at[at, pl.ds(half * 32, 32), :]
 
     def send_share(at, half, to):
-        go(rows_of(at, half), rows_of(at, half), recv_e.at[at, half or 0], to)
+        go(rows_of(at, half), rows_of(at, half), recv_e.at[at, half or 0], to, 8)
 
     def wait_share(at, half):
         ref = rows_of(at, half)
@@ -435,12 +477,11 @@
             wait_share(share(2, dy), half)
 
     whole = enc[...].reshape(TOK_DEV, D)
-    encoded[...] = whole
     cross_keys = dot32(whole, wckv[0]).astype(jnp.bfloat16)
     cross_values[...] = dot32(whole, wckv[1]).T.astype(jnp.bfloat16)
     acc[...] = jnp.zeros_like(acc)
-    cross_top = score(cross_keys, lens[me], cross_spread, scores_0)
-    rest(cross_values, scores_0, start, cross_top)
+    cross_top = score(cross_keys, key_bias(lens[me], 0, TOK_DEV), cross_spread, scores_0)
+    rest(lambda h: cross_values[pl.ds(h * HD, HD), :], scores_0, start, cross_top)
     o_all[...] = jnp.concatenate([acc[h, 0:HD, :] / acc[h, HD : HD + 1, :] for h in range(2)], axis=0)
     s_all[...] = jnp.concatenate(
         [
@@ -470,8 +511,9 @@
         remote(ref, ref, 0, arrival, "mate").wait_recv()
 
     half, quarter = TOK_DEV // 2, TOK_DEV // 4
-    go(o_all.at[:, lanes(1 - core, half)], o_mate, recv_m.at[0], "mate", lambda: o_mate)
-    go(s_all.at[:, lanes(1 - core, half)], s_mate, recv_m.at[1], "mate", lambda: s_mate)
+    go(o_all.at[:, lanes(1 - core, half)], o_mate, recv_m.at[0], "mate", 9)
+    go(s_all.at[:, lanes(1 - core, half)], s_mate, recv_m.at[1], "mate", 10)
+    weights_end(3)
     wait_for(o_mate, recv_m.at[0])
     wait_for(s_mate, recv_m.at[1])
     o, lse = joined(
@@ -479,8 +521,8 @@
     )
     o_half[...] = o.astype(jnp.bfloat16)
     s_half[...] = jnp.concatenate(lse + [jnp.zeros((6, half), jnp.float32)], axis=0)
-    go(o_half.at[:, lanes(1 - y, quarter)], o_side, recv_m.at[2], "side", lambda: o_side)
-    go(s_half.at[:, lanes(1 - y, quarter)], s_side, recv_m.at[3], "side", lambda: s_side)
+    go(o_half.at[:, lanes(1 - y, quarter)], o_side, recv_m.at[2], "side", 11)
+    go(s_half.at[:, lanes(1 - y, quarter)], s_side, recv_m.at[3], "side", 12)
     wait_for(o_side, recv_m.at[2])
     wait_for(s_side, recv_m.at[3])
     o, lse = joined(
@@ -498,8 +540,8 @@
 
     for dz in (4, 3, 5, 2, 6, 1, 7):
         at = lax.rem(z + dz, NZ)
-        go(few_rows(o_rows, at), o_line.at[z], recv_l.at[0, z], line_place[dz], lambda: o_line.at[0])
-        go(few_rows(s_rows, at), s_line.at[z], recv_l.at[1, z], line_place[dz], lambda: s_line.at[0])
+        go(few_rows(o_rows, at), o_line.at[z], recv_l.at[0, z], line_place[dz], 13)
+        go(few_rows(s_rows, at), s_line.at[z], recv_l.at[1, z], line_place[dz], 14)
     o_line[z] = few_rows(o_rows, z)[...]
     s_line[z] = few_rows(s_rows, z)[...]
     for dz in range(1, NZ):
@@ -512,7 +554,7 @@
         jnp.sum(o_line[...].astype(jnp.float32) * factors, axis=0) / jnp.sum(factors, axis=0)
     ).astype(jnp.bfloat16)
     for g, to in enumerate(("right", "left", "across")):
-        go(c_all.at[3], c_all.at[g], recv_h.at[g], to)
+        go(c_all.at[3], c_all.at[g], recv_h.at[g], to, 15)
     weights_here(3)
     for g in range(3):
         wait_for(c_all.at[g], recv_h.at[g])
@@ -522,7 +564,7 @@
         g = jnp.where(away == 0, 3, jnp.where(away == 3, 0, away))
         total += dot32(c_all[g], wco_all[g])
     sum_out[...] = total.astype(jnp.bfloat16)
-    go(sum_out, sum_in, recv_h.at[3], "partner")
+    go(sum_out, sum_in, recv_h.at[3], "partner", 16)
 
     def place_of(z_at, dy, dc):
         y_at = y if dy == 0 else 1 - y
@@ -538,7 +580,7 @@
     dec[mine] = (target_rows + jnp.where(live, total, 0.0)).astype(jnp.bfloat16)
 
     def hand(at, to):
-        go(dec.at[at], dec.at[at], recv_d.at[at], to, lambda: dec.at[0])
+        go(dec.at[at], dec.at[at], recv_d.at[at], to, 17)
 
     for dz in (4, 3, 5, 2, 6, 1, 7):
         hand(mine, line_place[dz])
@@ -557,20 +599,44 @@
         for dy in (0, 1):
             at = place_of(lax.rem(z + dz, NZ), dy, 1)
             wait_for(dec.at[at], recv_d.at[at])
-    decoded[...] = dec[...].reshape(TOK_DEV, D)
-    for number, alike in started:
-        remote(alike(), alike(), number, recv_y.at[0], "mate").wait_send()
+    sent = (
+        wo_all,
+        wi_all,
+        wf_all,
+        wco_all.at[pl.ds(0, 3)],
+        kv.at[pl.ds(0, SLOTS - 1)],
+        ctx_in,
+        out_1,
+        out_2,
+        enc.at[pl.ds(0, 7)],
+        o_mate,
+        s_mate,
+        o_side,
+        s_side,
+        o_line.at[pl.ds(0, NZ - 1)],
+        s_line.at[pl.ds(0, NZ - 1)],
+        c_all.at[pl.ds(0, 3)],
+        sum_out,
+        dec.at[pl.ds(0, SLOTS - 1)],
+    )
+    for group, ref in enumerate(sent):
+        remote(ref, ref, group, recv_y.at[0], "mate").wait_send()
 
 
 def layer(lens, tokens, gains, wqkv, wo, wi, wf, targets, wcq, wckv, wco, target_lens):
+    hbm = pl.BlockSpec(memory_space=pl.ANY)
     vmem = pl.BlockSpec(memory_space=pltpu.VMEM)
-    hbm = pl.BlockSpec(memory_space=pl.ANY)
     smem = pl.BlockSpec(memory_space=pltpu.SMEM)
     b16, f32 = jnp.bfloat16, jnp.float32
     gain_attn, gain_ffn, gain_final, gain_cross = (g.reshape(1, D) for g in gains)
     scratch = [
-        ((SLOTS, TOK_DEV, 2 * HD), b16),
-        ((SLOTS, 2 * HD, TOK_DEV), b16),
+        (tokens.shape, b16),
+        ((1, D), f32),
+        (wqkv.shape, b16),
+        ((1, D), f32),
+        ((1, D), f32),
+        ((1, D), f32),
+        ((SLOTS, 2, 2 * UNIT, 2 * HD), b16),
         ((256, 2 * TOK_DEV), b16),
         ((2, HD + 16, TOK_DEV), f32),
         ((TOK_DEV, 2 * TOK_DEV), f32),
@@ -592,7 +658,6 @@
         ((ROWS, D), b16),
         ((ROWS // 2, D), b16),
         ((ROWS // 2, D), b16),
-        ((8, ROWS // 2, D), b16),
         ((256, 2 * TOK_DEV), b16),
         ((2 * HD, TOK_DEV), b16),
         ((4, *wco.shape), b16),
@@ -611,23 +676,23 @@
         ((4, 16, 2 * HD), b16),
         ((16, D), b16),
         ((16, D), b16),
-        ((SLOTS, 16, D), b16),
     ]
-    sems = [(8,), (200,), (2, SLOTS), (4, 8), (4,), (2,), (8, 2), (4,), (2, NZ), (4,), (SLOTS,)]
-    return pl.pallas_call(
+    sems = [(16,), (18,), (2, SLOTS), (4, 8), (4,), (2,), (8, 2), (4,), (2, NZ), (4,), (SLOTS,)]
+    encoded, decoded = pl.pallas_call(
         layer_kernel,
         out_shape=(
-            jax.ShapeDtypeStruct((TOK_DEV, D), b16),
-            jax.ShapeDtypeStruct(targets.shape, b16),
+            pltpu.VMEM((8, ROWS // 2, D), b16),
+            pltpu.VMEM((SLOTS, 16, D), b16),
         ),
-        in_specs=[smem] + [vmem] * 6 + [hbm] * 7 + [smem],
+        in_specs=[smem] + [hbm] * 13 + [smem],
         out_specs=(vmem, vmem),
         scratch_shapes=[pltpu.VMEM(*s) for s in scratch] + [pltpu.SemaphoreType.DMA(s) for s in sems],
         compiler_params=pltpu.CompilerParams(
-            collective_id=0, has_side_effects=True, vmem_limit_bytes=60 << 20
+            collective_id=0, has_side_effects=True, vmem_limit_bytes=54 << 20
         ),
         name="layer",
     )(lens, tokens, gain_attn, wqkv, gain_ffn, gain_final, gain_cross, wo, wi, wf, targets, wcq, wckv, wco, target_lens)
+    return encoded.reshape(TOK_DEV, D), decoded.reshape(targets.shape)
 
 
 def local(

time: 132 us -> 120 us (0.909)
  Pallas kernels: 127 us -> 117 us
  local copies, waits for them, and re-layouts: 3.32 us -> 1.94 us
    pallas_call x1, Pallas kernels: 127 us -> 117 us  [layer(): pl.pallas_call(layer_kernel, out_shape=(pltpu.VMEM((8, ROWS // 2, D), b16...]
    unnamed x4 -> x2, local copies, waits for them, and re-layouts: 3.32 us -> 1.94 us
where the time goes in v4:
time: 120 us
  Pallas kernels  117 us (98%)
  local copies, waits for them, and re-layouts  1.94 us (2%)
    pallas_call x1, Pallas kernels, layer(): pl.pallas_call(layer_kernel, out_shape=(pltpu.VMEM((8, ROWS // 2, D), b16...  117 us

profile of v4, /device:TPU:1, one launch (start us, length us, event | category | flops | bytes accessed | tf_op | source)
XLA Modules:
  0.0 119.9 jit_solution(13992475633263303089)
XLA Ops:
  0.6 117.3 %layer.1 = (bf16[8,64,1024]{2,1,0:T(8,128)(2,1)S(1)}, bf16[32,16,1024]{2,1,0:T(8,128)(2,1)S(1)}) custom-call(s32[32]{0:T(128)} %lens.1, bf16[512,1024]{1,0:T(8,128)(2,1)} %tokens_hbm.1, f32[1,1024]{1,0:T(1,128)} %bitcast.10, bf16[3,1024,128]{2,1,0:T(8,128)(2,1)} %wqkv_hbm.1, f32[1,1024]{1,0:T(1,128)} %bitcast.11, f32[1,1024]{1,0:T(1,128)} %bitcast.12, ...), custom_call_target="tpu_custom_call" | custom-call | tf_op jit(solution)/shard_map/layer/pallas_call | solution.py:681
  118.0 1.0 copy.19
  118.9 1.0 copy.20

commit v5 on v4

--- a/solution.py
+++ b/solution.py
@@ -52,8 +52,8 @@
 
 ARRIVALS, SENDS = link_plan()
 UNITS = (("O", 0, 0), ("O", 0, 1), *(item for step in ARRIVALS for item in step))
-STEP_AT = {2: (0,), **{3 * s: (s,) for s in range(1, STEPS)}}
-WEIGHT_STEP_AT = {9: (("pass", 0),), 21: (("pass", 2),), 28: (("pass", 1), ("end", 0))}
+STEP_AT = {2: 0, 4: 1, 6: 2, 8: 3, 12: 4, 14: 5, 18: 6, 20: 7, 24: 8, 26: 9}
+WEIGHT_STEP_AT = {8: (("pass", 0),), 14: (("start", 2),), 18: (("pass", 1), ("end", 0))}
 UNIT_CODES = tuple((4 - d) * 4 + (line == "P") * 2 + half for line, d, half in UNITS)
 CODE_WORDS = tuple(
     sum(code << (8 * k) for k, code in enumerate(UNIT_CODES[first : first + 3]))
@@ -211,11 +211,14 @@
         name: pltpu.make_async_copy(source, target, local_sem.at[k])
         for k, (name, (source, target)) in enumerate(pairs.items())
     }
-    for load in loads.values():
-        load.start()
-
-    for name in ("tokens", "gain_attn", "wqkv"):
+    first_loads = ("tokens", "gain_attn", "wqkv")
+    for name in first_loads:
+        loads[name].start()
+    for name in first_loads:
         loads[name].wait()
+    for name, load in loads.items():
+        if name not in first_loads:
+            load.start()
     normed = normalised(tokens[...].astype(jnp.float32), gain_attn[...]).astype(jnp.bfloat16)
     own_keys = dot32(normed, wqkv[1]).astype(jnp.bfloat16)
     own_values = dot32(normed, wqkv[2]).T.astype(jnp.bfloat16)
@@ -224,7 +227,6 @@
         for k in range(2):
             first = half * UNIT + k * 128
             kv[me, half, pl.ds(UNIT + k * 128, 128), :] = own_values[:, first : first + 128]
-    q_t = dot32(normed, wqkv[0]).T
     pl.semaphore_wait(barrier, len(places))
 
     def remote(source, target, number, arrival, place):
@@ -285,21 +287,26 @@
         for slot, half, onward in ((0, 1, "right"), (1, 2, "left")):
             wait_piece(item, slot, 0, slot, core)
             send_piece(item, slot, 2, half, 1 + half, onward)
-            send_piece(item, slot, slot, 0, 4 + slot, "mate")
+            send_piece(item, slot, slot, 0, 4, "mate")
 
     def weights_end(item):
         for half in (1, 2):
             wait_piece(item, 2, half, 1 + half, core)
-            send_piece(item, 2, 2, half, 5 + half, "mate")
+            send_piece(item, 2, 2, half, 4, "mate")
 
     def weights_here(item):
-        for slot in (0, 1):
-            wait_piece(item, slot, 0, 4 + slot, 1 - core)
-        for half in (1, 2):
-            wait_piece(item, 2, half, 5 + half, 1 - core)
-
-    for item in range(3):
+        c = 1 - core
+        ref = (
+            lambda: wo_all.at[:, pl.ds(pl.multiple_of(c * 64, 64), 64), :],
+            lambda: wi_all.at[:, c],
+            lambda: wf_all.at[:, pl.ds(pl.multiple_of(c * 176, 16), 176), :],
+            lambda: wco_all.at[pl.ds(0, 3), pl.ds(pl.multiple_of(c * 64, 64), 64), :],
+        )[item]()
+        remote(ref, ref, 0, recv_w.at[item, 4], "mate").wait_recv()
+
+    for item in range(2):
         weights_start(item)
+    q_t = dot32(normed, wqkv[0]).T
 
     spread[...] = spread_queries(q_t * (HD ** (-0.5) * math.log2(math.e)))
     acc[...] = jnp.zeros_like(acc)
@@ -335,7 +342,6 @@
 
     def unit_score(unit, into):
         here, there, half = unit
-        wait_block(half, there)
         block = jnp.concatenate([kv[here, half, 0:UNIT, :], kv[there, half, 0:UNIT, :]], axis=0)
         bias = jnp.concatenate(
             [key_bias(lens[slot], half * UNIT, UNIT) for slot in (here, there)], axis=0
@@ -366,21 +372,27 @@
 
         rest(rows_of_head, held, old, top)
 
-    def handle(u, odd):
+    acts = {"start": weights_start, "pass": weights_pass, "end": weights_end}
+
+    def handle(u):
         for at in sorted({*STEP_AT, *WEIGHT_STEP_AT}):
-            if at % 2 != odd:
-                continue
 
             @pl.when(u == at)
             def _():
-                for s in STEP_AT.get(at, ()):
-                    step(s)
+                if at in STEP_AT:
+                    step(STEP_AT[at])
                 for what, item in WEIGHT_STEP_AT.get(at, ()):
-                    (weights_pass if what == "pass" else weights_end)(item)
+                    acts[what](item)
+
+    def wait_mate(unit):
+        here, there, half = unit
+        wait_block(half, there)
 
     start = jnp.full((1, 2 * TOK_DEV), masked_score, jnp.float32)
     zero = jnp.int32(0)
     first, second = unit_of(zero), unit_of(zero + 1)
+    wait_mate(first)
+    wait_mate(second)
     top = unit_score(first, scores_0)
     following = jnp.maximum(top, unit_score(second, scores_1))
     unit_rest(first, scores_0, start, top)
@@ -389,11 +401,12 @@
         old, top, before = carry
         u = 2 * j
         here, after = unit_of(u), unit_of(u + 1)
-        handle(u, 0)
+        handle(u)
+        wait_mate(here)
+        wait_mate(after)
         later = jnp.maximum(top, unit_score(here, scores_0))
         unit_rest(before, scores_1, old, top)
         old, top = top, later
-        handle(u + 1, 1)
         later = jnp.maximum(top, unit_score(after, scores_1))
         unit_rest(here, scores_0, old, top)
         return top, later, after
@@ -408,6 +421,7 @@
 
     for g, (to, at) in enumerate((("right", x + 1), ("left", x + 3), ("across", x + 2))):
         go(ctx_rows(at), ctx_in.at[g], recv_c.at[g], to, 5)
+    weights_pass(2)
     weights_start(3)
     weights_here(0)
     weights_end(1)
@@ -540,14 +554,12 @@
 
     for dz in (4, 3, 5, 2, 6, 1, 7):
         at = lax.rem(z + dz, NZ)
-        go(few_rows(o_rows, at), o_line.at[z], recv_l.at[0, z], line_place[dz], 13)
-        go(few_rows(s_rows, at), s_line.at[z], recv_l.at[1, z], line_place[dz], 14)
+        go(few_rows(o_rows, at), o_line.at[z], recv_l.at[0], line_place[dz], 13)
+        go(few_rows(s_rows, at), s_line.at[z], recv_l.at[1], line_place[dz], 14)
     o_line[z] = few_rows(o_rows, z)[...]
     s_line[z] = few_rows(s_rows, z)[...]
-    for dz in range(1, NZ):
-        at = lax.rem(z + dz, NZ)
-        wait_for(o_line.at[at], recv_l.at[0, at])
-        wait_for(s_line.at[at], recv_l.at[1, at])
+    wait_for(o_line.at[pl.ds(0, NZ - 1)], recv_l.at[0])
+    wait_for(s_line.at[pl.ds(0, NZ - 1)], recv_l.at[1])
     lines = s_line[...]
     factors = jnp.exp2(lines - jnp.max(lines, axis=0, keepdims=True))
     c_all[3] = (
@@ -580,7 +592,7 @@
     dec[mine] = (target_rows + jnp.where(live, total, 0.0)).astype(jnp.bfloat16)
 
     def hand(at, to):
-        go(dec.at[at], dec.at[at], recv_d.at[at], to, 17)
+        go(dec.at[at], dec.at[at], recv_d.at[16 if to == "mate" else at - core * 16], to, 17)
 
     for dz in (4, 3, 5, 2, 6, 1, 7):
         hand(mine, line_place[dz])
@@ -588,17 +600,14 @@
     hand(mine, "mate")
     for dz in (1, 7, 2, 6, 3, 5, 4):
         at = place_of(lax.rem(z + dz, NZ), 0, 0)
-        wait_for(dec.at[at], recv_d.at[at])
+        wait_for(dec.at[at], recv_d.at[at - core * 16])
         hand(at, "side")
         hand(at, "mate")
     for dz in (0, 1, 7, 2, 6, 3, 5, 4):
         at = place_of(lax.rem(z + dz, NZ), 1, 0)
-        wait_for(dec.at[at], recv_d.at[at])
+        wait_for(dec.at[at], recv_d.at[at - core * 16])
         hand(at, "mate")
-    for dz in range(NZ):
-        for dy in (0, 1):
-            at = place_of(lax.rem(z + dz, NZ), dy, 1)
-            wait_for(dec.at[at], recv_d.at[at])
+    wait_for(dec.at[pl.ds(pl.multiple_of((1 - core) * 16, 16), 16)], recv_d.at[16])
     sent = (
         wo_all,
         wi_all,
@@ -677,7 +686,7 @@
         ((16, D), b16),
         ((16, D), b16),
     ]
-    sems = [(16,), (18,), (2, SLOTS), (4, 8), (4,), (2,), (8, 2), (4,), (2, NZ), (4,), (SLOTS,)]
+    sems = [(16,), (18,), (2, SLOTS), (4, 5), (4,), (2,), (8, 2), (4,), (2,), (4,), (17,)]
     encoded, decoded = pl.pallas_call(
         layer_kernel,
         out_shape=(

time: 120 us -> 115 us (0.958)
  Pallas kernels: 117 us -> 113 us
    pallas_call x1, Pallas kernels: 117 us -> 113 us  [layer(): pl.pallas_call(layer_kernel, out_shape=(pltpu.VMEM((8, ROWS // 2, D), b16...]
where the time goes in v5:
time: 115 us
  Pallas kernels  113 us (98%)
  local copies, waits for them, and re-layouts  1.94 us (2%)
    pallas_call x1, Pallas kernels, layer(): pl.pallas_call(layer_kernel, out_shape=(pltpu.VMEM((8, ROWS // 2, D), b16...  113 us

profile of v5, /device:TPU:1, one launch (start us, length us, event | category | flops | bytes accessed | tf_op | source)
XLA Modules:
  0.0 115.2 jit_solution(519189790215463305)
XLA Ops:
  0.6 112.6 %layer.1 = (bf16[8,64,1024]{2,1,0:T(8,128)(2,1)S(1)}, bf16[32,16,1024]{2,1,0:T(8,128)(2,1)S(1)}) custom-call(s32[32]{0:T(128)} %lens.1, bf16[512,1024]{1,0:T(8,128)(2,1)} %tokens_hbm.1, f32[1,1024]{1,0:T(1,128)} %bitcast.10, bf16[3,1024,128]{2,1,0:T(8,128)(2,1)} %wqkv_hbm.1, f32[1,1024]{1,0:T(1,128)} %bitcast.11, f32[1,1024]{1,0:T(1,128)} %bitcast.12, ...), custom_call_target="tpu_custom_call" | custom-call | tf_op jit(solution)/shard_map/layer/pallas_call | solution.py:690
  113.2 1.0 copy.19
  114.2 1.0 copy.20

commit v6 on v5

--- a/solution.py
+++ b/solution.py
@@ -119,18 +119,19 @@
     wf,
     targets,
     wcq,
-    wckv,
+    wckv_all,
     wo_all,
     wi_all,
     wf_all,
     ctx,
     ctx_in,
     hidden,
-    part,
     out_1,
     in_1,
     out_2,
     in_2,
+    kvc_out,
+    kvc_in,
     cross_spread,
     cross_values,
     wco_all,
@@ -160,6 +161,7 @@
     recv_l,
     recv_h,
     recv_d,
+    recv_k,
 ):
     me = lax.axis_index("seq")
     core = lax.rem(me, 2)
@@ -205,7 +207,7 @@
         "gain_cross": (gain_cross_hbm, gain_cross),
         "gain_ffn": (gain_ffn_hbm, gain_ffn),
         "gain_final": (gain_final_hbm, gain_final),
-        "wckv": (wckv_hbm, wckv),
+        "wckv": (wckv_hbm, wckv_all.at[3]),
     }
     loads = {
         name: pltpu.make_async_copy(source, target, local_sem.at[k])
@@ -259,13 +261,14 @@
         push(half, me, "mate")
 
     def piece(item, slot, which, c):
-        own, gathered = ((wo, wo_all), (wi, wi_all), (wf, wf_all), (wco_all.at[3], wco_all))[item]
+        own, gathered = ((wo, wo_all), (wi, wi_all), (wf, wf_all), (wco_all.at[3], wco_all), (wckv_all.at[3], wckv_all))[item]
         ref = own if slot is None else gathered.at[slot]
         if item in (0, 3):
             first, size = ((0, 64), (0, 32), (32, 32))[which]
             return ref.at[pl.ds(pl.multiple_of(c * 64 + first, 32), size), :]
-        if item == 1:
-            first, size = ((0, 352), (0, 176), (176, 176))[which]
+        if item in (1, 4):
+            rows = ref.shape[1] // 2
+            first, size = ((0, 2 * rows), (0, rows), (rows, rows))[which]
             return ref.at[c, pl.ds(first, size), :]
         first, size = ((0, 176), (0, 96), (96, 80))[which]
         return ref.at[pl.ds(pl.multiple_of(c * 176 + first, 16), size), :]
@@ -276,10 +279,10 @@
 
     def send_piece(item, slot, slot_there, which, k, to):
         source, target = piece(item, slot, which, core), piece(item, slot_there, which, core)
-        go(source, target, recv_w.at[item, k], to, item)
+        go(source, target, recv_w.at[item, k], to, 18 if item == 4 else item)
 
     def weights_start(item):
-        loads[("wo", "wi", "wf", "wco")[item]].wait()
+        loads[("wo", "wi", "wf", "wco", "wckv")[item]].wait()
         for slot, to in ((0, "right"), (1, "left")):
             send_piece(item, None, slot, 0, slot, to)
 
@@ -301,6 +304,7 @@
             lambda: wi_all.at[:, c],
             lambda: wf_all.at[:, pl.ds(pl.multiple_of(c * 176, 16), 176), :],
             lambda: wco_all.at[pl.ds(0, 3), pl.ds(pl.multiple_of(c * 64, 64), 64), :],
+            lambda: wckv_all.at[pl.ds(0, 3), c],
         )[item]()
         remote(ref, ref, 0, recv_w.at[item, 4], "mate").wait_recv()
 
@@ -310,7 +314,7 @@
 
     spread[...] = spread_queries(q_t * (HD ** (-0.5) * math.log2(math.e)))
     acc[...] = jnp.zeros_like(acc)
-    for name in ("targets", "wcq", "gain_cross", "gain_ffn", "gain_final", "wckv"):
+    for name in ("targets", "wcq", "gain_cross", "gain_ffn", "gain_final"):
         loads[name].wait()
     cross_normed = normalised(targets[...].astype(jnp.float32), gain_cross[...]).astype(jnp.bfloat16)
     cross_spread[...] = spread_queries(
@@ -422,7 +426,6 @@
     for g, (to, at) in enumerate((("right", x + 1), ("left", x + 3), ("across", x + 2))):
         go(ctx_rows(at), ctx_in.at[g], recv_c.at[g], to, 5)
     weights_pass(2)
-    weights_start(3)
     weights_here(0)
     weights_end(1)
     total = dot32(ctx_rows(x)[...], wo[...])
@@ -431,12 +434,13 @@
         total += dot32(ctx_in[g], wo_all[g])
     out_1[...] = total.astype(jnp.bfloat16)
     go(out_1, in_1, recv_y.at[0], "partner", 6)
-    total += tokens[pl.ds(pl.multiple_of(x * ROWS, ROWS), ROWS), :].astype(jnp.float32)
+    weights_start(4)
     weights_end(2)
     weights_here(1)
     weights_here(2)
     remote(out_1, in_1, 0, recv_y.at[0], "partner").wait_recv()
-    total += in_1[...].astype(jnp.float32)
+    total = out_1[...].astype(jnp.float32) + in_1[...].astype(jnp.float32)
+    total += tokens[pl.ds(pl.multiple_of(x * ROWS, ROWS), ROWS), :].astype(jnp.float32)
     hidden[...] = total
     ffn_normed = normalised(total, gain_ffn[...]).T.astype(jnp.bfloat16)
     ffn = jnp.zeros((ROWS, D), jnp.float32)
@@ -448,26 +452,43 @@
         up = dot32(up_w, ffn_normed)
         activated = (jax.nn.gelu(gate, approximate=True) * up).T.astype(jnp.bfloat16)
         ffn += dot32(activated, down_w)
-    part[...] = ffn
-    share_rows = ROWS // 2
-    mine = pl.ds(pl.multiple_of(yh * share_rows, share_rows), share_rows)
-    other = pl.ds(pl.multiple_of((1 - yh) * share_rows, share_rows), share_rows)
-    out_2[...] = part[other, :].astype(jnp.bfloat16)
+        if g == 1:
+            weights_pass(4)
+    out_2[...] = ffn.astype(jnp.bfloat16)
     go(out_2, in_2, recv_y.at[1], "partner", 7)
-    weights_pass(3)
-    final = hidden[mine, :] + part[mine, :]
+    weights_end(4)
+    weights_start(3)
+    weights_here(4)
     remote(out_2, in_2, 0, recv_y.at[1], "partner").wait_recv()
-    final += in_2[...].astype(jnp.float32)
-
-    def share(dx, dy):
-        return lax.rem(x + dx + 4, 4) * 2 + (yh if dy == 0 else 1 - yh)
-
-    enc[share(0, 0)] = normalised(final, gain_final[...]).astype(jnp.bfloat16)
+    final = out_2[...].astype(jnp.float32) + in_2[...].astype(jnp.float32)
+    final += hidden[...]
+    rows_here = normalised(final, gain_final[...]).astype(jnp.bfloat16)
+    enc[x] = rows_here
+
+    def cross_pair(slot):
+        weights = jnp.concatenate([wckv_all[slot, 0], wckv_all[slot, 1]], axis=1)
+        return dot32(rows_here, weights).astype(jnp.bfloat16)
+
+    for slot, to in ((2, "across"), (0, "left"), (1, "right")):
+        both = cross_pair(slot)
+        kvc_out[slot, 0] = both[:, : 2 * HD]
+        kvc_out[slot, 1] = both[:, 2 * HD :]
+        go(kvc_out.at[slot], kvc_in.at[x], recv_k.at[x], to, 19)
+    both = cross_pair(3)
+    kvc_in[x, 0] = both[:, : 2 * HD]
+    kvc_in[x, 1] = both[:, 2 * HD :]
+
+    def beside(dx):
+        return lax.rem(x + dx + 4, 4)
+
+    for dx in (-1, 1, 2):
+        ref = kvc_in.at[beside(dx)]
+        remote(ref, ref, 0, recv_k.at[beside(dx)], "mate").wait_recv()
 
     def rows_of(at, half):
         if half is None:
             return enc.at[at]
-        return enc.at[at, pl.ds(half * 32, 32), :]
+        return enc.at[at, pl.ds(half * 64, 64), :]
 
     def send_share(at, half, to):
         go(rows_of(at, half), rows_of(at, half), recv_e.at[at, half or 0], to, 8)
@@ -476,23 +497,10 @@
         ref = rows_of(at, half)
         remote(ref, ref, 0, recv_e.at[at, half or 0], "mate").wait_recv()
 
-    for to in ("partner", "right", "left"):
-        send_share(share(0, 0), None, to)
-    for dy in (0, 1):
-        if dy:
-            wait_share(share(0, 1), None)
-            for to in ("right", "left"):
-                send_share(share(0, 1), None, to)
-        for dx, half, to in ((-1, 0, "right"), (1, 1, "left")):
-            wait_share(share(dx, dy), None)
-            send_share(share(dx, dy), half, to)
-    for dy in (0, 1):
-        for half in (0, 1):
-            wait_share(share(2, dy), half)
-
-    whole = enc[...].reshape(TOK_DEV, D)
-    cross_keys = dot32(whole, wckv[0]).astype(jnp.bfloat16)
-    cross_values[...] = dot32(whole, wckv[1]).T.astype(jnp.bfloat16)
+    weights_pass(3)
+    cross_keys = jnp.concatenate([kvc_in[k, 0] for k in range(4)], axis=0)
+    cross_rows = jnp.concatenate([kvc_in[k, 1] for k in range(4)], axis=0)
+    cross_values[...] = cross_rows.astype(jnp.float32).T.astype(jnp.bfloat16)
     acc[...] = jnp.zeros_like(acc)
     cross_top = score(cross_keys, key_bias(lens[me], 0, TOK_DEV), cross_spread, scores_0)
     rest(lambda h: cross_values[pl.ds(h * HD, HD), :], scores_0, start, cross_top)
@@ -527,7 +535,8 @@
     half, quarter = TOK_DEV // 2, TOK_DEV // 4
     go(o_all.at[:, lanes(1 - core, half)], o_mate, recv_m.at[0], "mate", 9)
     go(s_all.at[:, lanes(1 - core, half)], s_mate, recv_m.at[1], "mate", 10)
-    weights_end(3)
+    for to in ("right", "left"):
+        send_share(x, None, to)
     wait_for(o_mate, recv_m.at[0])
     wait_for(s_mate, recv_m.at[1])
     o, lse = joined(
@@ -556,6 +565,10 @@
         at = lax.rem(z + dz, NZ)
         go(few_rows(o_rows, at), o_line.at[z], recv_l.at[0], line_place[dz], 13)
         go(few_rows(s_rows, at), s_line.at[z], recv_l.at[1], line_place[dz], 14)
+    for dx, half, to in ((-1, 0, "right"), (1, 1, "left")):
+        wait_share(beside(dx), None)
+        send_share(beside(dx), half, to)
+    weights_end(3)
     o_line[z] = few_rows(o_rows, z)[...]
     s_line[z] = few_rows(s_rows, z)[...]
     wait_for(o_line.at[pl.ds(0, NZ - 1)], recv_l.at[0])
@@ -608,6 +621,8 @@
         wait_for(dec.at[at], recv_d.at[at - core * 16])
         hand(at, "mate")
     wait_for(dec.at[pl.ds(pl.multiple_of((1 - core) * 16, 16), 16)], recv_d.at[16])
+    for half in (0, 1):
+        wait_share(beside(2), half)
     sent = (
         wo_all,
         wi_all,
@@ -617,7 +632,7 @@
         ctx_in,
         out_1,
         out_2,
-        enc.at[pl.ds(0, 7)],
+        enc.at[pl.ds(0, 3)],
         o_mate,
         s_mate,
         o_side,
@@ -627,6 +642,8 @@
         c_all.at[pl.ds(0, 3)],
         sum_out,
         dec.at[pl.ds(0, SLOTS - 1)],
+        wckv_all.at[pl.ds(0, 3)],
+        kvc_out,
     )
     for group, ref in enumerate(sent):
         remote(ref, ref, group, recv_y.at[0], "mate").wait_send()
@@ -655,18 +672,19 @@
         (wf.shape, b16),
         (targets.shape, b16),
         (wcq.shape, b16),
-        (wckv.shape, b16),
+        ((4, *wckv.shape), b16),
         ((3, *wo.shape), b16),
         ((3, *wi.shape), b16),
         ((3, *wf.shape), b16),
         ((TOK_DEV, 2 * HD), b16),
         ((3, ROWS, 2 * HD), b16),
         ((ROWS, D), f32),
-        ((ROWS, D), f32),
         ((ROWS, D), b16),
         ((ROWS, D), b16),
-        ((ROWS // 2, D), b16),
-        ((ROWS // 2, D), b16),
+        ((ROWS, D), b16),
+        ((ROWS, D), b16),
+        ((3, 2, ROWS, 2 * HD), b16),
+        ((4, 2, ROWS, 2 * HD), b16),
         ((256, 2 * TOK_DEV), b16),
         ((2 * HD, TOK_DEV), b16),
         ((4, *wco.shape), b16),
@@ -686,11 +704,11 @@
         ((16, D), b16),
         ((16, D), b16),
     ]
-    sems = [(16,), (18,), (2, SLOTS), (4, 5), (4,), (2,), (8, 2), (4,), (2,), (4,), (17,)]
+    sems = [(16,), (20,), (2, SLOTS), (5, 5), (3,), (2,), (4, 2), (4,), (2,), (4,), (17,), (4,)]
     encoded, decoded = pl.pallas_call(
         layer_kernel,
         out_shape=(
-            pltpu.VMEM((8, ROWS // 2, D), b16),
+            pltpu.VMEM((4, ROWS, D), b16),
             pltpu.VMEM((SLOTS, 16, D), b16),
         ),
         in_specs=[smem] + [hbm] * 13 + [smem],

time: 115 us -> 108 us (0.939)
  Pallas kernels: 113 us -> 105 us
    pallas_call x1, Pallas kernels: 113 us -> 105 us  [layer(): pl.pallas_call(layer_kernel, out_shape=(pltpu.VMEM((4, ROWS, D), b16), pl...]
where the time goes in v6:
time: 108 us
  Pallas kernels  105 us (97%)
  local copies, waits for them, and re-layouts  1.94 us (2%)
    pallas_call x1, Pallas kernels, layer(): pl.pallas_call(layer_kernel, out_shape=(pltpu.VMEM((4, ROWS, D), b16), pl...  105 us

profile of v6, /device:TPU:1, one launch (start us, length us, event | category | flops | bytes accessed | tf_op | source)
XLA Modules:
  0.0 108.1 jit_solution(14405462101032837603)
XLA Ops:
  0.6 105.5 %layer.1 = (bf16[4,128,1024]{2,1,0:T(8,128)(2,1)S(1)}, bf16[32,16,1024]{2,1,0:T(8,128)(2,1)S(1)}) custom-call(s32[32]{0:T(128)} %lens.1, bf16[512,1024]{1,0:T(8,128)(2,1)} %tokens_hbm.1, f32[1,1024]{1,0:T(1,128)} %bitcast.10, bf16[3,1024,128]{2,1,0:T(8,128)(2,1)} %wqkv_hbm.1, f32[1,1024]{1,0:T(1,128)} %bitcast.11, f32[1,1024]{1,0:T(1,128)} %bitcast.12, ...), custom_call_target="tpu_custom_call" | custom-call | tf_op jit(solution)/shard_map/layer/pallas_call | solution.py:708
  106.1 1.0 copy.19
  107.1 1.0 copy.20

commit v7 on v6

--- a/solution.py
+++ b/solution.py
@@ -52,6 +52,7 @@
 
 ARRIVALS, SENDS = link_plan()
 UNITS = (("O", 0, 0), ("O", 0, 1), *(item for step in ARRIVALS for item in step))
+MATE_AT = {(2 + 3 * s) // 2 * 2: s for s in range(STEPS)}
 STEP_AT = {2: 0, 4: 1, 6: 2, 8: 3, 12: 4, 14: 5, 18: 6, 20: 7, 24: 8, 26: 9}
 WEIGHT_STEP_AT = {8: (("pass", 0),), 14: (("start", 2),), 18: (("pass", 1), ("end", 0))}
 UNIT_CODES = tuple((4 - d) * 4 + (line == "P") * 2 + half for line, d, half in UNITS)
@@ -244,21 +245,22 @@
     def go(source, target, arrival, place, group):
         remote(source, target, group, arrival, place).start()
 
-    def wait_block(half, slot):
+    def wait_step(mate_side, s):
+        ref = kv.at[pl.ds(0, 3), 0]
+        remote(ref, ref, 0, recv.at[mate_side, s], "mate").wait_recv()
+
+    def push(half, slot, place, s):
         ref = kv.at[slot, half]
-        remote(ref, ref, 0, recv.at[half, slot], "mate").wait_recv()
-
-    def push(half, slot, place):
-        ref = kv.at[slot, half]
-        go(ref, ref, recv.at[half, slot], place, 4)
+        go(ref, ref, recv.at[int(place == "mate"), s], place, 4)
 
     def slot_of(line, d):
         return index(-d, 0 if line == "O" else 1, 0)
 
-    for name, (line, d, half) in SENDS[0]:
-        push(half, me, name)
+    link_items = {"up": UP, "down": DOWN, "side": SIDE}
+    for name, item in SENDS[0]:
+        push(item[2], me, name, link_items[name].index(item))
     for half in range(2):
-        push(half, me, "mate")
+        push(half, me, "mate", STEPS)
 
     def piece(item, slot, which, c):
         own, gathered = ((wo, wo_all), (wi, wi_all), (wf, wf_all), (wco_all.at[3], wco_all), (wckv_all.at[3], wckv_all))[item]
@@ -322,12 +324,12 @@
     )
 
     def step(s):
+        wait_step(0, s)
         for line, d, half in ARRIVALS[s]:
-            slot = slot_of(line, d)
-            wait_block(half, slot)
-            push(half, slot, "mate")
-        for name, (line, d, half) in SENDS[s + 1]:
-            push(half, slot_of(line, d), name)
+            push(half, slot_of(line, d), "mate", s)
+        for name, item in SENDS[s + 1]:
+            line, d, half = item
+            push(half, slot_of(line, d), name, link_items[name].index(item))
 
     def unit_of(u):
         third = u // 3
@@ -379,7 +381,7 @@
     acts = {"start": weights_start, "pass": weights_pass, "end": weights_end}
 
     def handle(u):
-        for at in sorted({*STEP_AT, *WEIGHT_STEP_AT}):
+        for at in sorted({*STEP_AT, *MATE_AT, *WEIGHT_STEP_AT}):
 
             @pl.when(u == at)
             def _():
@@ -387,16 +389,14 @@
                     step(STEP_AT[at])
                 for what, item in WEIGHT_STEP_AT.get(at, ()):
                     acts[what](item)
-
-    def wait_mate(unit):
-        here, there, half = unit
-        wait_block(half, there)
+                if at in MATE_AT:
+                    wait_step(1, MATE_AT[at])
 
     start = jnp.full((1, 2 * TOK_DEV), masked_score, jnp.float32)
     zero = jnp.int32(0)
     first, second = unit_of(zero), unit_of(zero + 1)
-    wait_mate(first)
-    wait_mate(second)
+    both_halves = kv.at[me]
+    remote(both_halves, both_halves, 0, recv.at[1, STEPS], "mate").wait_recv()
     top = unit_score(first, scores_0)
     following = jnp.maximum(top, unit_score(second, scores_1))
     unit_rest(first, scores_0, start, top)
@@ -406,8 +406,6 @@
         u = 2 * j
         here, after = unit_of(u), unit_of(u + 1)
         handle(u)
-        wait_mate(here)
-        wait_mate(after)
         later = jnp.maximum(top, unit_score(here, scores_0))
         unit_rest(before, scores_1, old, top)
         old, top = top, later
@@ -443,24 +441,32 @@
     total += tokens[pl.ds(pl.multiple_of(x * ROWS, ROWS), ROWS), :].astype(jnp.float32)
     hidden[...] = total
     ffn_normed = normalised(total, gain_ffn[...]).T.astype(jnp.bfloat16)
-    ffn = jnp.zeros((ROWS, D), jnp.float32)
+    acts_here = []
     for g in range(4):
         gate_w, up_w, down_w = (
-            (wi[0], wi[1], wf[...]) if g == 3 else (wi_all[g, 0], wi_all[g, 1], wf_all[g])
+            (wi[0], wi[1], wf) if g == 3 else (wi_all[g, 0], wi_all[g, 1], wf_all.at[g])
         )
         gate = dot32(gate_w, ffn_normed)
         up = dot32(up_w, ffn_normed)
         activated = (jax.nn.gelu(gate, approximate=True) * up).T.astype(jnp.bfloat16)
-        ffn += dot32(activated, down_w)
+        acts_here.append((activated, down_w))
         if g == 1:
             weights_pass(4)
-    out_2[...] = ffn.astype(jnp.bfloat16)
-    go(out_2, in_2, recv_y.at[1], "partner", 7)
+    wide = D // 2
+    for k in range(2):
+        ffn = jnp.zeros((ROWS, wide), jnp.float32)
+        for activated, down_w in acts_here:
+            ffn += dot32(activated, down_w[:, k * wide : (k + 1) * wide])
+        out_2[k] = ffn.astype(jnp.bfloat16)
+        go(out_2.at[k], in_2.at[k], recv_y.at[1 + k], "partner", 7 if k == 0 else 20)
     weights_end(4)
     weights_start(3)
     weights_here(4)
-    remote(out_2, in_2, 0, recv_y.at[1], "partner").wait_recv()
-    final = out_2[...].astype(jnp.float32) + in_2[...].astype(jnp.float32)
+    for k in range(2):
+        remote(out_2.at[k], in_2.at[k], 0, recv_y.at[1 + k], "partner").wait_recv()
+    final = jnp.concatenate(
+        [out_2[k].astype(jnp.float32) + in_2[k].astype(jnp.float32) for k in range(2)], axis=1
+    )
     final += hidden[...]
     rows_here = normalised(final, gain_final[...]).astype(jnp.bfloat16)
     enc[x] = rows_here
@@ -607,10 +613,10 @@
     def hand(at, to):
         go(dec.at[at], dec.at[at], recv_d.at[16 if to == "mate" else at - core * 16], to, 17)
 
-    for dz in (4, 3, 5, 2, 6, 1, 7):
-        hand(mine, line_place[dz])
     hand(mine, "side")
     hand(mine, "mate")
+    for dz in (1, 7, 2, 6, 3, 5, 4):
+        hand(mine, line_place[dz])
     for dz in (1, 7, 2, 6, 3, 5, 4):
         at = place_of(lax.rem(z + dz, NZ), 0, 0)
         wait_for(dec.at[at], recv_d.at[at - core * 16])
@@ -631,7 +637,7 @@
         kv.at[pl.ds(0, SLOTS - 1)],
         ctx_in,
         out_1,
-        out_2,
+        out_2.at[0],
         enc.at[pl.ds(0, 3)],
         o_mate,
         s_mate,
@@ -644,9 +650,21 @@
         dec.at[pl.ds(0, SLOTS - 1)],
         wckv_all.at[pl.ds(0, 3)],
         kvc_out,
+        out_2.at[1],
     )
     for group, ref in enumerate(sent):
         remote(ref, ref, group, recv_y.at[0], "mate").wait_send()
+
+
+def leave_kernel(encoded, decoded, encoded_out, decoded_out, sems):
+    moves = (
+        pltpu.make_async_copy(encoded, encoded_out, sems.at[0]),
+        pltpu.make_async_copy(decoded, decoded_out, sems.at[1]),
+    )
+    for move in moves:
+        move.start()
+    for move in moves:
+        move.wait()
 
 
 def layer(lens, tokens, gains, wqkv, wo, wi, wf, targets, wcq, wckv, wco, target_lens):
@@ -681,8 +699,8 @@
         ((ROWS, D), f32),
         ((ROWS, D), b16),
         ((ROWS, D), b16),
-        ((ROWS, D), b16),
-        ((ROWS, D), b16),
+        ((2, ROWS, D // 2), b16),
+        ((2, ROWS, D // 2), b16),
         ((3, 2, ROWS, 2 * HD), b16),
         ((4, 2, ROWS, 2 * HD), b16),
         ((256, 2 * TOK_DEV), b16),
@@ -704,7 +722,7 @@
         ((16, D), b16),
         ((16, D), b16),
     ]
-    sems = [(16,), (20,), (2, SLOTS), (5, 5), (3,), (2,), (4, 2), (4,), (2,), (4,), (17,), (4,)]
+    sems = [(16,), (21,), (2, STEPS + 1), (5, 5), (3,), (3,), (4, 2), (4,), (2,), (4,), (17,), (4,)]
     encoded, decoded = pl.pallas_call(
         layer_kernel,
         out_shape=(
@@ -719,6 +737,20 @@
         ),
         name="layer",
     )(lens, tokens, gain_attn, wqkv, gain_ffn, gain_final, gain_cross, wo, wi, wf, targets, wcq, wckv, wco, target_lens)
+    encoded, decoded = pl.pallas_call(
+        leave_kernel,
+        out_shape=(
+            jax.ShapeDtypeStruct(encoded.shape, b16),
+            jax.ShapeDtypeStruct(decoded.shape, b16),
+        ),
+        in_specs=[vmem, vmem],
+        out_specs=(hbm, hbm),
+        scratch_shapes=[pltpu.SemaphoreType.DMA((2,))],
+        name="leave",
+    )(
+        pltpu.with_memory_space_constraint(encoded, pltpu.VMEM),
+        pltpu.with_memory_space_constraint(decoded, pltpu.VMEM),
+    )
     return encoded.reshape(TOK_DEV, D), decoded.reshape(targets.shape)
 
 

time: 108 us -> 107 us (level)
  local copies, waits for them, and re-layouts: 1.94 us -> 0 us
    unnamed x2 -> x0, local copies, waits for them, and re-layouts: 1.94 us -> none
    pallas_call x0 -> x1, Pallas kernels: none -> 1.33 us  [layer(): pl.pallas_call(leave_kernel, out_shape=(jax.ShapeDtypeStruct(encoded.shap...]
where the time goes in v7:
time: 107 us
  Pallas kernels  106 us (99%)
    pallas_call x1, Pallas kernels, layer(): pl.pallas_call(layer_kernel, out_shape=(pltpu.VMEM((4, ROWS, D), b16), pl...  105 us

profile of v7, /device:TPU:1, one launch (start us, length us, event | category | flops | bytes accessed | tf_op | source)
XLA Modules:
  0.0 106.9 jit_solution(17564559304534866980)
XLA Ops:
  0.6 104.9 %layer.1 = (bf16[4,128,1024]{2,1,0:T(8,128)(2,1)S(1)}, bf16[32,16,1024]{2,1,0:T(8,128)(2,1)S(1)}) custom-call(s32[32]{0:T(128)} %lens.1, bf16[512,1024]{1,0:T(8,128)(2,1)} %tokens_hbm.1, f32[1,1024]{1,0:T(1,128)} %bitcast.8, bf16[3,1024,128]{2,1,0:T(8,128)(2,1)} %wqkv_hbm.1, f32[1,1024]{1,0:T(1,128)} %bitcast.9, f32[1,1024]{1,0:T(1,128)} %bitcast.10, ...), custom_call_target="tpu_custom_call" | custom-call | tf_op jit(solution)/shard_map/layer/pallas_call | solution.py:726
  105.6 1.3 %leave.1 = (bf16[4,128,1024]{2,1,0:T(8,128)(2,1)}, bf16[32,16,1024]{2,1,0:T(8,128)(2,1)}) custom-call(bf16[4,128,1024]{2,1,0:T(8,128)(2,1)S(1)} %get-tuple-element.6.encoded, bf16[32,16,1024]{2,1,0:T(8,128)(2,1)S(1)} %get-tuple-element.7.decoded), custom_call_target="tpu_custom_call" | custom-call | tf_op jit(solution)/shard_map/leave/pallas_call | solution.py:740

commit v8 on v7

--- a/solution.py
+++ b/solution.py
@@ -183,6 +183,7 @@
         "down": {"seq": index(-1, 0, 0)},
         "side": {"seq": index(0, 1, 0)},
         "mate": {"seq": index(0, 0, 1)},
+        "diagonal": {"seq": index(0, 1, 1)},
         "right": {"head": yh * 4 + lax.rem(x + 1, 4)},
         "left": {"head": yh * 4 + lax.rem(x + 3, 4)},
         "across": {"head": yh * 4 + lax.rem(x + 2, 4)},
@@ -610,9 +611,12 @@
     live = slots < target_lens[core * 2 + y]
     dec[mine] = (target_rows + jnp.where(live, total, 0.0)).astype(jnp.bfloat16)
 
+    same_core = ("side", *line_place.values())
+
     def hand(at, to):
-        go(dec.at[at], dec.at[at], recv_d.at[16 if to == "mate" else at - core * 16], to, 17)
-
+        go(dec.at[at], dec.at[at], recv_d.at[at - core * 16 if to in same_core else 16], to, 17)
+
+    far = (3, 4, 5)
     hand(mine, "side")
     hand(mine, "mate")
     for dz in (1, 7, 2, 6, 3, 5, 4):
@@ -622,10 +626,13 @@
         wait_for(dec.at[at], recv_d.at[at - core * 16])
         hand(at, "side")
         hand(at, "mate")
+        if dz in far:
+            hand(at, "diagonal")
     for dz in (0, 1, 7, 2, 6, 3, 5, 4):
         at = place_of(lax.rem(z + dz, NZ), 1, 0)
         wait_for(dec.at[at], recv_d.at[at - core * 16])
-        hand(at, "mate")
+        if dz not in far:
+            hand(at, "mate")
     wait_for(dec.at[pl.ds(pl.multiple_of((1 - core) * 16, 16), 16)], recv_d.at[16])
     for half in (0, 1):
         wait_share(beside(2), half)

time: 107 us -> 107 us (level)
  no operation moved by 1% of the time
where the time goes in v8:
time: 107 us; the launch traced here: 106 us
  Pallas kernels  106 us (99%)
    pallas_call x1, Pallas kernels, layer(): pl.pallas_call(layer_kernel, out_shape=(pltpu.VMEM((4, ROWS, D), b16), pl...  104 us

profile of v8, /device:TPU:1, one launch (start us, length us, event | category | flops | bytes accessed | tf_op | source)
XLA Modules:
  0.0 106.3 jit_solution(16069222138315487706)
XLA Ops:
  0.6 104.4 %layer.1 = (bf16[4,128,1024]{2,1,0:T(8,128)(2,1)S(1)}, bf16[32,16,1024]{2,1,0:T(8,128)(2,1)S(1)}) custom-call(s32[32]{0:T(128)} %lens.1, bf16[512,1024]{1,0:T(8,128)(2,1)} %tokens_hbm.1, f32[1,1024]{1,0:T(1,128)} %bitcast.8, bf16[3,1024,128]{2,1,0:T(8,128)(2,1)} %wqkv_hbm.1, f32[1,1024]{1,0:T(1,128)} %bitcast.9, f32[1,1024]{1,0:T(1,128)} %bitcast.10, ...), custom_call_target="tpu_custom_call" | custom-call | tf_op jit(solution)/shard_map/layer/pallas_call | solution.py:733
  105.0 1.3 %leave.1 = (bf16[4,128,1024]{2,1,0:T(8,128)(2,1)}, bf16[32,16,1024]{2,1,0:T(8,128)(2,1)}) custom-call(bf16[4,128,1024]{2,1,0:T(8,128)(2,1)S(1)} %get-tuple-element.6.encoded, bf16[32,16,1024]{2,1,0:T(8,128)(2,1)S(1)} %get-tuple-element.7.decoded), custom_call_target="tpu_custom_call" | custom-call | tf_op jit(solution)/shard_map/leave/pallas_call | solution.py:747

commit v9 on v8

--- a/solution.py
+++ b/solution.py
@@ -430,15 +430,23 @@
     total = dot32(ctx_rows(x)[...], wo[...])
     for g in range(3):
         remote(ctx_in.at[g], ctx_in.at[g], 0, recv_c.at[g], "mate").wait_recv()
-        total += dot32(ctx_in[g], wo_all[g])
-    out_1[...] = total.astype(jnp.bfloat16)
-    go(out_1, in_1, recv_y.at[0], "partner", 6)
+    wide = D // 2
+    for k in range(2):
+        cols = slice(k * wide, (k + 1) * wide)
+        summed = total[:, cols]
+        for g in range(3):
+            summed += dot32(ctx_in[g], wo_all[g, :, cols])
+        out_1[k] = summed.astype(jnp.bfloat16)
+        go(out_1.at[k], in_1.at[k], recv_y.at[3 * k], "partner", 6 if k == 0 else 21)
     weights_start(4)
     weights_end(2)
     weights_here(1)
     weights_here(2)
-    remote(out_1, in_1, 0, recv_y.at[0], "partner").wait_recv()
-    total = out_1[...].astype(jnp.float32) + in_1[...].astype(jnp.float32)
+    for k in range(2):
+        remote(out_1.at[k], in_1.at[k], 0, recv_y.at[3 * k], "partner").wait_recv()
+    total = jnp.concatenate(
+        [out_1[k].astype(jnp.float32) + in_1[k].astype(jnp.float32) for k in range(2)], axis=1
+    )
     total += tokens[pl.ds(pl.multiple_of(x * ROWS, ROWS), ROWS), :].astype(jnp.float32)
     hidden[...] = total
     ffn_normed = normalised(total, gain_ffn[...]).T.astype(jnp.bfloat16)
@@ -453,7 +461,6 @@
         acts_here.append((activated, down_w))
         if g == 1:
             weights_pass(4)
-    wide = D // 2
     for k in range(2):
         ffn = jnp.zeros((ROWS, wide), jnp.float32)
         for activated, down_w in acts_here:
@@ -643,7 +650,7 @@
         wco_all.at[pl.ds(0, 3)],
         kv.at[pl.ds(0, SLOTS - 1)],
         ctx_in,
-        out_1,
+        out_1.at[0],
         out_2.at[0],
         enc.at[pl.ds(0, 3)],
         o_mate,
@@ -658,6 +665,7 @@
         wckv_all.at[pl.ds(0, 3)],
         kvc_out,
         out_2.at[1],
+        out_1.at[1],
     )
     for group, ref in enumerate(sent):
         remote(ref, ref, group, recv_y.at[0], "mate").wait_send()
@@ -704,8 +712,8 @@
         ((TOK_DEV, 2 * HD), b16),
         ((3, ROWS, 2 * HD), b16),
         ((ROWS, D), f32),
-        ((ROWS, D), b16),
-        ((ROWS, D), b16),
+        ((2, ROWS, D // 2), b16),
+        ((2, ROWS, D // 2), b16),
         ((2, ROWS, D // 2), b16),
         ((2, ROWS, D // 2), b16),
         ((3, 2, ROWS, 2 * HD), b16),
@@ -729,7 +737,7 @@
         ((16, D), b16),
         ((16, D), b16),
     ]
-    sems = [(16,), (21,), (2, STEPS + 1), (5, 5), (3,), (3,), (4, 2), (4,), (2,), (4,), (17,), (4,)]
+    sems = [(16,), (22,), (2, STEPS + 1), (5, 5), (3,), (4,), (4, 2), (4,), (2,), (4,), (17,), (4,)]
     encoded, decoded = pl.pallas_call(
         layer_kernel,
         out_shape=(

time: 107 us -> 106 us (level)
  no operation moved by 1% of the time
where the time goes in v9:
time: 106 us
  Pallas kernels  106 us (100%)
    pallas_call x1, Pallas kernels, layer(): pl.pallas_call(layer_kernel, out_shape=(pltpu.VMEM((4, ROWS, D), b16), pl...  104 us

profile of v9, /device:TPU:1, one launch (start us, length us, event | category | flops | bytes accessed | tf_op | source)
XLA Modules:
  0.0 106.3 jit_solution(13158602748731949624)
XLA Ops:
  0.6 104.3 %layer.1 = (bf16[4,128,1024]{2,1,0:T(8,128)(2,1)S(1)}, bf16[32,16,1024]{2,1,0:T(8,128)(2,1)S(1)}) custom-call(s32[32]{0:T(128)} %lens.1, bf16[512,1024]{1,0:T(8,128)(2,1)} %tokens_hbm.1, f32[1,1024]{1,0:T(1,128)} %bitcast.8, bf16[3,1024,128]{2,1,0:T(8,128)(2,1)} %wqkv_hbm.1, f32[1,1024]{1,0:T(1,128)} %bitcast.9, f32[1,1024]{1,0:T(1,128)} %bitcast.10, ...), custom_call_target="tpu_custom_call" | custom-call | tf_op jit(solution)/shard_map/layer/pallas_call | solution.py:741
  105.0 1.3 %leave.1 = (bf16[4,128,1024]{2,1,0:T(8,128)(2,1)}, bf16[32,16,1024]{2,1,0:T(8,128)(2,1)}) custom-call(bf16[4,128,1024]{2,1,0:T(8,128)(2,1)S(1)} %get-tuple-element.6.encoded, bf16[32,16,1024]{2,1,0:T(8,128)(2,1)S(1)} %get-tuple-element.7.decoded), custom_call_target="tpu_custom_call" | custom-call | tf_op jit(solution)/shard_map/leave/pallas_call | solution.py:755
